TPU v7x, 32 devices: a whole 2x2x4 slice. The times are simulated.
32 devices in a mesh: dp: 4 (over z), expert: 8 (over y, x, core).
Axes of the slice: x: 2, y: 2, z: 4, core: 2. Of those that a mesh axis runs over, the one named last changes fastest.
Arguments:
- grad_output: bfloat16 [8, 8, 3840], P('expert', None, 'dp'), may hold values from -6 to 6
- router_logits: float32 [8, 8, 32], P('expert'), may hold values from -8 to 8
- expert_ids: int32 [8, 8, 8], P('expert'), may hold values from 0 to 31, all different within a row; in each aligned block of 8 rows (0 to 7, 8 to 15, ..., all dimensions but the last counted through in order) at most 3 rows name the same one
- router_input: bfloat16 [8, 8, 3840], P('expert', 'dp'), may hold values from -6 to 6
- router_weight: bfloat16 [32, 3840], P(None, 'dp'), may hold values from -0.09375 to 0.09375
- gate_weight: bfloat16 [32, 3840, 1024], P('expert', 'dp'), may hold values from -0.09375 to 0.09375
- up_weight: bfloat16 [32, 3840, 1024], P('expert', 'dp'), may hold values from -0.09375 to 0.09375
- down_weight: bfloat16 [32, 1024, 3840], P('expert', None, 'dp'), may hold values from -0.1875 to 0.1875
- gate_saved: bfloat16 [32, 24, 1024], P('expert'), may hold values from -6 to 6
- up_saved: bfloat16 [32, 24, 1024], P('expert'), may hold values from -6 to 6
Outputs:
- grad_input: bfloat16 [8, 8, 3840], P('expert', None, 'dp')
- grad_router: float32 [32, 3840], P('expert', 'dp')
Inputs may be any that keep to these rules, and one draw needn't show every extreme that they name: `expert_ids`: within one token group (the 8 tokens of one index of expert, in order), no expert is named more than 3 times, a bound that some block reaches; every row names 8 different experts.
All inputs are finite; a program needn't handle non-finite values.
Results may differ from a plain program's by a relative error of at most 0.008.
Values may be sent and summed in bfloat16 or wider, within the bound.
No kernel may reach another device: no remote copies, remote signals or barrier semaphores. Data moves between devices by JAX's collectives and lax.ppermute only.
A program may use at most 64 MiB of HBM per device.

v0:
```python
import jax
import jax.numpy as jnp
from jax import lax
from jax.sharding import PartitionSpec as P

route_scale = 2.5


def split_pair(values):
    upper = values.astype(jnp.bfloat16)
    lower = (values - upper.astype(jnp.float32)).astype(jnp.bfloat16)
    return jnp.stack([upper, lower], axis=-1)


def join_pair(paired):
    return paired[..., 0].astype(jnp.float32) + paired[..., 1].astype(jnp.float32)


def activation_backward(hidden_grad, saved_gate, saved_up):
    gate_value = saved_gate.astype(jnp.float32)
    up_value = saved_up.astype(jnp.float32)
    gate_sigmoid = jax.nn.sigmoid(gate_value)
    activated = gate_value * gate_sigmoid
    hidden = lax.optimization_barrier((activated * up_value).astype(jnp.bfloat16)).astype(
        jnp.float32
    )
    gate_share = jnp.sum(hidden * hidden_grad, axis=1)
    gate_part = (
        hidden_grad * up_value * gate_sigmoid * (1.0 + gate_value * (1.0 - gate_sigmoid))
    ).astype(jnp.bfloat16)
    up_part = (hidden_grad * activated).astype(jnp.bfloat16)
    return (gate_part, up_part, gate_share)


def local(
    grad_output,
    router_logits,
    expert_ids,
    router_input,
    router_weight,
    gate_weight,
    up_weight,
    down_weight,
    gate_saved,
    up_saved,
):
    expert_count = lax.axis_size("expert")
    out_rows = grad_output[0]
    group_size, feature_share = out_rows.shape
    expert_total = router_logits.shape[2]
    top_count = expert_ids.shape[2]
    local_experts, slot_count, hidden_size = gate_saved.shape
    slot_depth = slot_count // expert_count
    assign_count = group_size * top_count
    flat_ids = expert_ids[0].reshape(assign_count)
    expert_hot = (flat_ids[:, None] == jnp.arange(expert_total, dtype=jnp.int32)[None, :]).astype(
        jnp.int32
    )
    earlier = jnp.cumsum(expert_hot, axis=0) - expert_hot
    ranking = jnp.sum(expert_hot * earlier, axis=1)
    target = flat_ids * slot_depth + ranking
    slot_place = (
        jnp.arange(expert_total * slot_depth, dtype=jnp.int32)[:, None] == target[None, :]
    ).astype(jnp.bfloat16)
    owner_hot = (
        (jnp.arange(assign_count, dtype=jnp.int32) // top_count)[:, None]
        == jnp.arange(group_size, dtype=jnp.int32)[None, :]
    ).astype(jnp.bfloat16)
    slot_token = jnp.dot(slot_place, owner_hot, preferred_element_type=jnp.float32).astype(
        jnp.bfloat16
    )
    outgoing = jnp.dot(slot_token, out_rows, preferred_element_type=jnp.float32).astype(
        jnp.bfloat16
    )
    incoming = lax.all_to_all(
        outgoing.reshape(expert_total, slot_depth, feature_share),
        "expert",
        split_axis=0,
        concat_axis=1,
        tiled=True,
    )
    partial_hidden = jnp.einsum(
        "esd,efd->esf", incoming, down_weight, preferred_element_type=jnp.float32
    )
    row_total = local_experts * slot_count
    hidden_grad = lax.psum(partial_hidden.reshape(row_total, hidden_size), "dp")
    grad_gate, grad_up, gate_grad = activation_backward(
        hidden_grad,
        gate_saved.reshape(row_total, hidden_size),
        up_saved.reshape(row_total, hidden_size),
    )
    grad_gate = grad_gate.reshape(local_experts, slot_count, hidden_size)
    grad_up = grad_up.reshape(local_experts, slot_count, hidden_size)
    gate_grad = gate_grad.reshape(local_experts, slot_count)
    expert_input = jnp.einsum(
        "esf,edf->esd", grad_gate, gate_weight, preferred_element_type=jnp.float32
    )
    expert_input = expert_input + jnp.einsum(
        "esf,edf->esd", grad_up, up_weight, preferred_element_type=jnp.float32
    )
    expert_input = expert_input.astype(jnp.bfloat16)
    rows_back, gate_paired_back = (
        lax.all_to_all(expert_input, "expert", split_axis=1, concat_axis=0, tiled=True),
        lax.all_to_all(split_pair(gate_grad), "expert", split_axis=1, concat_axis=0, tiled=True),
    )
    gate_back = join_pair(gate_paired_back)
    pick_map = slot_place.T.astype(jnp.float32)
    picked_gate = jnp.dot(
        pick_map, gate_back.reshape(expert_total * slot_depth), precision=lax.Precision.HIGHEST
    ).reshape(group_size, top_count)
    scores = jax.nn.sigmoid(router_logits[0])
    hot_float = expert_hot.reshape(group_size, top_count, expert_total).astype(jnp.float32)
    chosen = jnp.sum(hot_float * scores[:, None, :], axis=2)
    chosen_total = jnp.sum(chosen, axis=1, keepdims=True)
    gates = route_scale * chosen / chosen_total
    mixture = jnp.sum(picked_gate * gates, axis=1, keepdims=True)
    d_chosen = (route_scale * picked_gate - mixture) / chosen_total
    d_scores = jnp.sum(hot_float * d_chosen[:, :, None], axis=1)
    logit_grad = (d_scores * scores * (1.0 - scores)).astype(jnp.bfloat16)
    grouped_input = lax.all_to_all(router_input[0], "dp", split_axis=1, concat_axis=0, tiled=True)
    router_term = jnp.einsum(
        "ge,gc->ec", logit_grad, grouped_input, preferred_element_type=jnp.float32
    )
    grad_router = lax.psum_scatter(router_term, "expert", scatter_dimension=0, tiled=True)
    picked_rows = jnp.dot(
        slot_place.T,
        rows_back.reshape(expert_total * slot_depth, feature_share),
        preferred_element_type=jnp.float32,
    )
    mixed = jnp.sum(
        gates[:, :, None] * picked_rows.reshape(group_size, top_count, feature_share), axis=1
    )
    router_part = jnp.dot(logit_grad, router_weight, preferred_element_type=jnp.float32)
    grad_input = (mixed + router_part).astype(jnp.bfloat16)[None]
    return (grad_input, grad_router)


def solution(mesh):
    placed = (
        P("expert", None, "dp"),
        P("expert", None, None),
        P("expert", None, None),
        P("expert", "dp", None),
        P(None, "dp"),
        P("expert", "dp", None),
        P("expert", "dp", None),
        P("expert", None, "dp"),
        P("expert", None, None),
        P("expert", None, None),
    )
    return jax.shard_map(
        local,
        mesh=mesh,
        in_specs=placed,
        out_specs=(P("expert", None, "dp"), P("expert", "dp")),
        check_vma=False,
    )
```

profile of v0, /device:TPU:0, one launch (start us, length us, event | category | flops | bytes accessed | tf_op | source)
XLA Modules:
  0.0 147.4 jit_solution(7802566168627807311)
XLA Ops:
  7.2 0.8 reshape_squeeze.3
  8.4 1.2 convolution_convert_fusion
  9.7 0.8 reshape.186
  10.5 5.2 %all-to-all-start = ((bf16[32,3,960]{2,1,0:T(4,128)(2,1)}), bf16[32,3,960]{2,1,0:T(4,128)(2,1)S(1)}, u32[]{:S(2)}, u32[]{:S(2)}) async-start(bf16[32,3,960]{2,1,0:T(4,128)(2,1)} %reshape.186), calls=%async_computation | async-start | bytes 524288 | tf_op jit(solution)/shard_map/all_to_all | solution.py:75
  15.7 0.8 all_to_all.62
  16.5 0.6 copy.46
  17.1 5.5 %all-to-all-done = bf16[32,3,960]{2,1,0:T(4,128)(2,1)S(1)} async-done(((bf16[32,3,960]{2,1,0:T(4,128)(2,1)}), bf16[32,3,960]{2,1,0:T(4,128)(2,1)S(1)}, u32[]{:S(2)}, u32[]{:S(2)}) %all-to-all-start) | async-done | bytes 184352 | tf_op jit(solution)/shard_map/all_to_all | solution.py:75
  22.6 4.9 %all-to-all-start.3 = ((bf16[2,4,960]{2,0,1:T(2,128)(2,1)}), bf16[2,4,960]{2,0,1:T(2,128)(2,1)S(1)}, u32[]{:S(2)}, u32[]{:S(2)}) async-start(bf16[2,4,960]{2,0,1:T(2,128)(2,1)} %copy.46), calls=%async_computation.3 | async-start | bytes 32768 | tf_op jit(solution)/shard_map/all_to_all | solution.py:120
  27.6 5.1 %fusion.12 = f32[4,24,1024]{2,1,0:T(8,128)} fusion(bf16[4,1024,960]{1,2,0:T(8,128)(2,1)} %param.17, bf16[4,24,960]{2,0,1:T(4,128)(2,1)S(1)} %bitcast.79), kind=kOutput, calls=%fused_computation.24 | convolution fusion | flops 188743680 | bytes 8441856 | tf_op jit(solution)/shard_map/esd,efd->esf/dot_general | solution.py:82
  33.1 36.3 %all-reduce.4.cloned.1.call-done = f32[96,1024]{1,0:T(8,128)} async-done(((f32[96,1024]{1,0:T(8,128)}), f32[96,1024]{1,0:T(8,128)}) %all-reduce.4.cloned.1.call-update) | async-done | bytes 393232 | tf_op jit(solution)/shard_map/psum | solution.py:86
  69.4 1.2 multiply_convert_fusion
  70.7 1.1 multiply_reduce_fusion
  71.9 0.7 copy.42
  72.6 3.6 %all-to-all-start.2 = ((bf16[4,24,2]{0,2,1:T(2,128)(2,1)}), bf16[4,24,2]{0,2,1:T(2,128)(2,1)S(1)}, u32[]{:S(2)}, u32[]{:S(2)}) async-start(bf16[4,24,2]{0,2,1:T(2,128)(2,1)} %copy.42), calls=%async_computation.2 | async-start | bytes 24576 | tf_op jit(solution)/shard_map/all_to_all | solution.py:104
  76.3 5.4 %fusion.41 = f32[4,24,960]{2,1,0:T(8,128)S(1)} fusion(bf16[4,24,1024]{2,1,0:T(8,128)(2,1)S(1)} %bitcast.81, bf16[4,960,1024]{2,1,0:T(8,128)(2,1)} %param.15), kind=kOutput, calls=%fused_computation.74 | convolution fusion | flops 188743680 | bytes 8429568 | tf_op jit(solution)/shard_map/esf,edf->esd/dot_general | solution.py:95
  82.0 0.4 fusion.20
  82.8 0.9 fusion.32
  83.7 5.4 %fusion = bf16[4,24,960]{2,1,0:T(8,128)(2,1)S(1)} fusion(f32[4,24,960]{2,1,0:T(8,128)S(1)} %fusion.41, bf16[4,24,1024]{2,1,0:T(8,128)(2,1)S(1)} %bitcast.80, bf16[4,960,1024]{2,1,0:T(8,128)(2,1)} %param.16), kind=kOutput, calls=%fused_computation.1 | convolution fusion | flops 188928000 | bytes 8613888 | tf_op jit(solution)/shard_map/esf,edf->esd/dot_general | solution.py:98
  89.0 0.8 copy.40
  89.9 4.2 %all-to-all-start.1 = ((bf16[4,24,960]{2,0,1:T(4,128)(2,1)}), bf16[4,24,960]{2,0,1:T(4,128)(2,1)S(1)}, u32[]{:S(2)}, u32[]{:S(2)}) async-start(bf16[4,24,960]{2,0,1:T(4,128)(2,1)} %copy.40), calls=%async_computation.1 | async-start | bytes 393216 | tf_op jit(solution)/shard_map/all_to_all | solution.py:103
  94.0 0.6 dynamic-slice
  95.3 42.5 %all-reduce.6.cloned.1.call-done = f32[32,960]{1,0:T(8,128)} async-done(((f32[32,960]{1,0:T(8,128)}), f32[32,960]{1,0:T(8,128)}) %all-reduce.6.cloned.1.call-update) | async-done | bytes 122896
  137.8 1.4 constant_dynamic-slice_fusion
  139.8 0.7 fusion.3
  (43 shorter events, 2.3 us)
Async XLA Ops:
  7.2 132.6 %copy-start = (bf16[32,960]{1,0:T(8,128)(2,1)S(1)}, bf16[32,960]{1,0:T(8,128)(2,1)}, u32[]{:S(2)}) copy-start(bf16[32,960]{1,0:T(8,128)(2,1)} %param.14) | copy-start | bytes 184324
  7.2 25.7 %copy-start.3 = (s32[1,8,8]{2,1,0:T(8,128)S(1)}, s32[1,8,8]{2,1,0:T(8,128)}, u32[]{:S(2)}) copy-start(s32[1,8,8]{2,1,0:T(8,128)} %param.12) | copy-start | bytes 772
  7.2 25.6 %copy-start.4 = (f32[1,8,32]{2,1,0:T(8,128)S(1)}, f32[1,8,32]{2,1,0:T(8,128)}, u32[]{:S(2)}) copy-start(f32[1,8,32]{2,1,0:T(8,128)} %param.11) | copy-start | bytes 3076
  7.2 62.2 %copy-start.1 = (bf16[4,24,1024]{2,1,0:T(8,128)(2,1)S(1)}, bf16[4,24,1024]{2,1,0:T(8,128)(2,1)}, u32[]{:S(2)}) copy-start(bf16[4,24,1024]{2,1,0:T(8,128)(2,1)} %param.18) | copy-start | bytes 589828
  7.2 62.2 %copy-start.2 = (bf16[4,24,1024]{2,1,0:T(8,128)(2,1)S(1)}, bf16[4,24,1024]{2,1,0:T(8,128)(2,1)}, u32[]{:S(2)}) copy-start(bf16[4,24,1024]{2,1,0:T(8,128)(2,1)} %param.19) | copy-start | bytes 589828
  10.5 12.1 %all-to-all-start = ((bf16[32,3,960]{2,1,0:T(4,128)(2,1)}), bf16[32,3,960]{2,1,0:T(4,128)(2,1)S(1)}, u32[]{:S(2)}, u32[]{:S(2)}) async-start(bf16[32,3,960]{2,1,0:T(4,128)(2,1)} %reshape.186), calls=%async_computation | async-start | bytes 524288 | tf_op jit(solution)/shard_map/all_to_all | solution.py:75
  22.6 10.5 %all-to-all-start.3 = ((bf16[2,4,960]{2,0,1:T(2,128)(2,1)}), bf16[2,4,960]{2,0,1:T(2,128)(2,1)S(1)}, u32[]{:S(2)}, u32[]{:S(2)}) async-start(bf16[2,4,960]{2,0,1:T(2,128)(2,1)} %copy.46), calls=%async_computation.3 | async-start | bytes 32768 | tf_op jit(solution)/shard_map/all_to_all | solution.py:120
  27.5 42.0 %all-reduce.4.cloned.1.call-start = ((), (), s32[]{:S(2)}) async-start(), calls=%async_computation.4 | async-start | bytes 786432 | tf_op jit(solution)/shard_map/psum | solution.py:86
  72.6 9.0 %all-to-all-start.2 = ((bf16[4,24,2]{0,2,1:T(2,128)(2,1)}), bf16[4,24,2]{0,2,1:T(2,128)(2,1)S(1)}, u32[]{:S(2)}, u32[]{:S(2)}) async-start(bf16[4,24,2]{0,2,1:T(2,128)(2,1)} %copy.42), calls=%async_computation.2 | async-start | bytes 24576 | tf_op jit(solution)/shard_map/all_to_all | solution.py:104
  76.2 61.6 %all-reduce.6.cloned.1.call-start = ((), (), s32[]{:S(2)}) async-start(), calls=%async_computation.5 | async-start | bytes 262144
  76.2 17.8 %copy-start.5 = (u32[32]{0:T(128)S(1)}, u32[32]{0:T(128)}, u32[]{:S(2)}) copy-start(u32[32]{0:T(128)} %constant.42) | copy-start | bytes 388
  89.9 49.3 %all-to-all-start.1 = ((bf16[4,24,960]{2,0,1:T(4,128)(2,1)}), bf16[4,24,960]{2,0,1:T(4,128)(2,1)S(1)}, u32[]{:S(2)}, u32[]{:S(2)}) async-start(bf16[4,24,960]{2,0,1:T(4,128)(2,1)} %copy.40), calls=%async_computation.1 | async-start | bytes 393216 | tf_op jit(solution)/shard_map/all_to_all | solution.py:103
Sparse Core Ops, SparseCore 0:
  32.9 36.5 all-reduce.3
  83.8 53.9 all-reduce.5
where the time goes:
time: 148 us; the launch traced here: 147 us
  waiting for transfers between devices  84.4 us (57%)
  matrix products  19.4 us (13%)
  starting transfers between devices  17.8 us (12%)
  between operations  14.9 us (10%)
  local copies, waits for them, and re-layouts  7.53 us (5%)
  other arithmetic  3.35 us (2%)
    unnamed x3, waiting for transfers between devices  42.6 us
    psum x1, waiting for transfers between devices, local(): hidden_grad = lax.psum(partial_hidden.reshape(row_total, hidden_size), 'dp')  36.3 us
    all_to_all x1, waiting for transfers between devices, local(): lax.all_to_all(outgoing.reshape(expert_total, slot_depth, feature_share),...  5.47 us
    dot_general x1, matrix products, local(): jnp.einsum('esf,edf->esd', grad_up, up_weight, preferred_element_type=jnp...  5.39 us
    dot_general x1, matrix products, local(): jnp.einsum('esf,edf->esd', grad_gate, gate_weight, preferred_element_type...  5.39 us
    all_to_all x1, starting transfers between devices, local(): lax.all_to_all(outgoing.reshape(expert_total, slot_depth, feature_share),...  5.2 us
    dot_general x1, matrix products, local(): jnp.einsum('esd,efd->esf', incoming, down_weight, preferred_element_type=...  5.13 us
    all_to_all x1, starting transfers between devices, local(): lax.all_to_all(router_input[0], 'dp', split_axis=1, concat_axis=0, tiled=...  4.87 us
  transfers between devices with their start and end apart: 6, of which 3 were waited for; matrix products, arithmetic and copies ran while one was open for 13% of the time, Pallas kernels for 0%

commit v1 on v0

v1 whole, which is shorter than its diff:
```python
import functools

import jax
import jax.numpy as jnp
from jax import lax
from jax.experimental import pallas as pl
from jax.experimental.pallas import tpu as pltpu
from jax.sharding import PartitionSpec as P

route_scale = 2.5
LANES = 128
HIGH = lax.Precision.HIGHEST
VMEM = pltpu.VMEM


def spec(space):
    return pl.BlockSpec(memory_space=space)


def iota(shape, dim):
    return lax.broadcasted_iota(jnp.int32, shape, dim)


def pairwise(count):
    return count <= 8 and count & (count - 1) == 0


def place_of(block, me, count):
    return lax.bitwise_xor(block, me) if pairwise(count) else block


def pack_kernel(expert_total, logits_ref, ids_ref, rows_ref, out_ref):
    copies, group, width = out_ref.shape
    top = ids_ref.shape[2]
    share = rows_ref.shape[2]
    aux = width - share
    logits = logits_ref[0]
    first = logits.astype(jnp.bfloat16).astype(jnp.float32)
    rest = logits - first
    second = rest.astype(jnp.bfloat16).astype(jnp.float32)
    third = rest - second
    pieces = [first, second, third, ids_ref[0].astype(jnp.float32)]
    spare = aux - 3 * expert_total - top
    if spare:
        pieces.append(jnp.zeros((group, spare), jnp.float32))
    head = jnp.concatenate(pieces, axis=1).astype(jnp.bfloat16)
    rows = rows_ref[0]
    for copy in range(copies):
        out_ref[copy, :, :aux] = head
        out_ref[copy, :, aux:] = rows


def down_kernel(
    sizes, tokens_ref, weight_ref, send_ref, high_ref, low_ref, gates_ref, slope_ref, slot_ref, held, sems
):
    group, expert_total, top, aux, depth, local_experts, slots, dp_count = sizes
    tokens, width = tokens_ref.shape
    rows = local_experts * slots
    piece = rows // dp_count
    per_expert = slots // piece
    copies = [
        pltpu.make_async_copy(weight_ref.at[e], held.at[e], sems.at[e]) for e in range(local_experts)
    ]
    for copy in copies:
        copy.start()
    dp_me = lax.axis_index("dp")
    base = lax.axis_index("expert") * local_experts
    head = tokens_ref[:, :aux].astype(jnp.float32)
    logits = (
        head[:, :expert_total]
        + head[:, expert_total : 2 * expert_total]
        + head[:, 2 * expert_total : 3 * expert_total]
    )
    lane = iota((tokens, expert_total), 1)
    named = jnp.zeros((tokens, expert_total), jnp.float32)
    for k in range(top):
        at = 3 * expert_total + k
        named = named + (head[:, at : at + 1].astype(jnp.int32) == lane).astype(jnp.float32)
    row_at, col_at = iota((tokens, tokens), 0), iota((tokens, tokens), 1)
    earlier = (lax.div(row_at, group) == lax.div(col_at, group)) & (col_at < row_at)
    rank = jnp.dot(
        earlier.astype(jnp.bfloat16), named.astype(jnp.bfloat16), preferred_element_type=jnp.float32
    )
    first_slot = (lax.div(iota((tokens, expert_total), 0), group) * depth).astype(jnp.float32)
    slot = jnp.where(named > 0.5, first_slot + rank, -1.0)
    scores = jax.nn.sigmoid(logits)
    total = jnp.sum(named * scores, axis=1, keepdims=True)
    gates = route_scale * (named * scores) / total
    gates_ref[...] = gates
    slope_ref[...] = named * scores * (1.0 - scores) / total
    slot_ref[...] = slot
    pick = (iota((8, expert_total), 1) == base + iota((8, expert_total), 0)).astype(jnp.float32)
    contract = (((1,), (1,)), ((), ()))
    slot_rows = lax.dot_general(
        pick, slot, contract, precision=HIGH, preferred_element_type=jnp.float32
    )
    spread = (
        iota((expert_total, rows), 0) == base + lax.div(iota((expert_total, rows), 1), slots)
    ).astype(jnp.float32)
    slot_wide = jnp.dot(slot, spread, precision=HIGH, preferred_element_type=jnp.float32)
    gates_wide = jnp.dot(gates, spread, precision=HIGH, preferred_element_type=jnp.float32)
    wanted = lax.rem(iota((tokens, rows), 1), slots).astype(jnp.float32)
    combine = jnp.where(slot_wide == wanted, gates_wide, 0.0)
    upper = combine.astype(jnp.bfloat16)
    high_ref[...] = upper
    low_ref[...] = (combine - upper.astype(jnp.float32)).astype(jnp.bfloat16)
    features = tokens_ref[:, aux:]
    slot_at = iota((slots, tokens), 0).astype(jnp.float32)
    for e in range(local_experts):
        chosen = (slot_at == slot_rows[e : e + 1, :]).astype(jnp.bfloat16)
        sent = jnp.dot(chosen, features, preferred_element_type=jnp.float32).astype(jnp.bfloat16)
        copies[e].wait()
        partial = jnp.dot(sent, held[e], preferred_element_type=jnp.float32)
        for b in range(per_expert):
            send_ref[place_of(e * per_expert + b, dp_me, dp_count)] = partial[
                b * piece : (b + 1) * piece
            ].astype(jnp.bfloat16)


def gathered_blocks(refs):
    if len(refs) == 1 and len(refs[0].shape) == 3:
        return [(refs[0], k) for k in range(refs[0].shape[0])]
    return [(ref, None) for ref in refs]


def read_block(item):
    ref, at = item
    return ref[...] if at is None else ref[at]


def hidden_kernel(block_count, gate_ref, up_ref, *refs):
    parts = gathered_blocks(refs[:block_count])
    hidden_ref, share_ref, gate_held, up_held, sems = refs[block_count:]
    me = lax.axis_index("dp")
    fetches = [
        pltpu.make_async_copy(gate_ref.at[me], gate_held, sems.at[0]),
        pltpu.make_async_copy(up_ref.at[me], up_held, sems.at[1]),
    ]
    for fetch in fetches:
        fetch.start()
    total = read_block(parts[0]).astype(jnp.float32)
    for part in parts[1:]:
        total = total + read_block(part).astype(jnp.float32)
    hidden_ref[...] = total.astype(jnp.bfloat16)
    for fetch in fetches:
        fetch.wait()
    gate_value = gate_held[...].astype(jnp.float32)
    up_value = up_held[...].astype(jnp.float32)
    hidden = (gate_value * jax.nn.sigmoid(gate_value) * up_value).astype(jnp.bfloat16)
    share = jnp.sum(hidden.astype(jnp.float32) * total, axis=1, keepdims=True)
    piece = total.shape[0]
    across = iota((piece, LANES), 0) == iota((piece, LANES), 1)
    line = jnp.sum(jnp.where(across, share, 0.0), axis=0, keepdims=True)
    share_ref[...] = jnp.broadcast_to(line[None], share_ref.shape)


def input_kernel(block_count, slots, gate_w_ref, up_w_ref, high_ref, low_ref, gate_ref, up_ref, *refs):
    parts = gathered_blocks(refs[:block_count])
    out_ref, gate_held, up_held, hidden_held, rows_held, sems = refs[block_count:]
    local_experts = gate_w_ref.shape[0]
    dp_count, piece, _ = hidden_held.shape
    per_expert = slots // piece
    copies = []
    for e in range(local_experts):
        copies.append(pltpu.make_async_copy(gate_w_ref.at[e], gate_held.at[e], sems.at[2 * e]))
        copies.append(pltpu.make_async_copy(up_w_ref.at[e], up_held.at[e], sems.at[2 * e + 1]))
    for copy in copies:
        copy.start()
    me = lax.axis_index("dp")
    for k, part in enumerate(parts):
        hidden_held[place_of(k, me, dp_count)] = read_block(part)
    contract = (((1,), (1,)), ((), ()))
    for e in range(local_experts):
        grads = [
            hidden_held[e * per_expert + b].astype(jnp.float32) for b in range(per_expert)
        ]
        hidden_grad = grads[0] if per_expert == 1 else jnp.concatenate(grads, axis=0)
        gate_value = gate_ref[e].astype(jnp.float32)
        up_value = up_ref[e].astype(jnp.float32)
        sig = jax.nn.sigmoid(gate_value)
        gate_part = (hidden_grad * up_value * sig * (1.0 + gate_value * (1.0 - sig))).astype(jnp.bfloat16)
        up_part = (hidden_grad * (gate_value * sig)).astype(jnp.bfloat16)
        copies[2 * e].wait()
        value = lax.dot_general(gate_part, gate_held[e], contract, preferred_element_type=jnp.float32)
        copies[2 * e + 1].wait()
        value = value + lax.dot_general(
            up_part, up_held[e], contract, preferred_element_type=jnp.float32
        )
        rows_held[e * slots : (e + 1) * slots] = value
    rows = rows_held[...].astype(jnp.bfloat16)
    mixed = jnp.dot(high_ref[...], rows, preferred_element_type=jnp.float32)
    mixed = mixed + jnp.dot(low_ref[...], rows, preferred_element_type=jnp.float32)
    copies_out, group, _ = out_ref.shape
    for q in range(copies_out):
        out_ref[q] = mixed[q * group : (q + 1) * group].astype(jnp.bfloat16)


def router_kernel(
    sizes, shares_ref, gates_ref, slope_ref, slot_ref, inputs_ref, weight_ref, router_ref, part_ref
):
    group, depth, slots, dp_count, expert_count = sizes
    tokens, expert_total = gates_ref.shape
    local_experts = router_ref.shape[0]
    piece = local_experts * slots // dp_count
    per_expert = slots // piece
    devices = dp_count * expert_count
    me = lax.axis_index("expert")
    shares = shares_ref[...].reshape(devices, LANES)
    source = iota((devices, expert_total), 0)
    expert = iota((devices, expert_total), 1)
    dp_of, expert_of = lax.div(source, expert_count), lax.rem(source, expert_count)
    tables = []
    for b in range(per_expert):
        owner = (expert_of == lax.div(expert, local_experts)) & (
            dp_of == lax.rem(expert, local_experts) * per_expert + b
        )
        table = lax.dot_general(
            shares,
            owner.astype(jnp.float32),
            (((0,), (0,)), ((), ())),
            precision=HIGH,
            preferred_element_type=jnp.float32,
        )
        tables.append(table[:piece])
    table = tables[0] if per_expert == 1 else jnp.concatenate(tables, axis=0)
    slot = slot_ref[...]
    first = lax.div(iota((tokens, slots), 0), group) * depth
    column = iota((tokens, slots), 1)
    first_slot = (lax.div(iota((tokens, expert_total), 0), group) * depth).astype(jnp.float32)
    given = jnp.zeros((tokens, expert_total), jnp.float32)
    for r in range(depth):
        line = (column == first + r).astype(jnp.float32)
        found = jnp.dot(line, table, precision=HIGH, preferred_element_type=jnp.float32)
        given = given + jnp.where(slot == first_slot + float(r), found, 0.0)
    mixture = jnp.sum(given * gates_ref[...], axis=1, keepdims=True)
    logit_grad = (slope_ref[...] * (route_scale * given - mixture)).astype(jnp.bfloat16)
    own = (iota((group, tokens), 1) == me * group + iota((group, tokens), 0)).astype(jnp.bfloat16)
    own_grad = jnp.dot(own, logit_grad, preferred_element_type=jnp.float32).astype(jnp.bfloat16)
    part_ref[...] = jnp.dot(own_grad, weight_ref[...], preferred_element_type=jnp.float32)
    pick = (
        iota((8, expert_total), 1) == me * local_experts + iota((8, expert_total), 0)
    ).astype(jnp.bfloat16)
    mine = lax.dot_general(
        pick, logit_grad, (((1,), (1,)), ((), ())), preferred_element_type=jnp.float32
    ).astype(jnp.bfloat16)
    grads = jnp.dot(mine, inputs_ref[...], preferred_element_type=jnp.float32)
    router_ref[...] = grads[:local_experts]


def reduce_blocks(send, count):
    if pairwise(count):
        return [send[0]] + [
            lax.ppermute(send[k], "dp", [(j, j ^ k) for j in range(count)]) for k in range(1, count)
        ]
    return [lax.all_to_all(send, "dp", 0, 0, tiled=True)]


def spread_blocks(block, count):
    if pairwise(count):
        return [block] + [
            lax.ppermute(block, "dp", [(j, j ^ k) for j in range(count)]) for k in range(1, count)
        ]
    return [lax.all_gather(block, "dp", axis=0, tiled=False)]


def local(
    grad_output,
    router_logits,
    expert_ids,
    router_input,
    router_weight,
    gate_weight,
    up_weight,
    down_weight,
    gate_saved,
    up_saved,
):
    expert_count, dp_count = lax.axis_size("expert"), lax.axis_size("dp")
    devices = expert_count * dp_count
    _, group, share = grad_output.shape
    expert_total = router_logits.shape[2]
    top = expert_ids.shape[2]
    local_experts, slots, hidden_size = gate_saved.shape
    depth = slots // expert_count
    rows = local_experts * slots
    piece = rows // dp_count
    tokens = expert_count * group
    aux = -(-(3 * expert_total + top) // LANES) * LANES
    bf16, f32 = jnp.bfloat16, jnp.float32
    shaped = jax.ShapeDtypeStruct

    _, own_tokens, feature_total = router_input.shape
    routed = router_input.reshape(own_tokens, dp_count, share).transpose(1, 0, 2)
    routed = jnp.broadcast_to(routed[:, None], (dp_count, expert_count, own_tokens, share))
    routed = lax.all_to_all(
        routed.reshape(devices, own_tokens, share), ("dp", "expert"), 0, 0, tiled=True
    )
    routed = routed.reshape(dp_count, expert_count, own_tokens, share).transpose(1, 0, 2, 3)
    routed = routed.reshape(tokens, share)

    packed = pl.pallas_call(
        functools.partial(pack_kernel, expert_total),
        out_shape=shaped((expert_count, group, aux + share), bf16),
        in_specs=[spec(VMEM)] * 3,
        out_specs=spec(VMEM),
    )(router_logits, expert_ids, grad_output)
    gathered = lax.all_to_all(packed, "expert", 0, 0, tiled=True).reshape(tokens, aux + share)

    sizes = (group, expert_total, top, aux, depth, local_experts, slots, dp_count)
    table = shaped((tokens, expert_total), f32)
    send, high, low, gates, slope, slot = pl.pallas_call(
        functools.partial(down_kernel, sizes),
        out_shape=(
            shaped((dp_count, piece, hidden_size), bf16),
            shaped((tokens, rows), bf16),
            shaped((tokens, rows), bf16),
            table,
            table,
            table,
        ),
        in_specs=[spec(VMEM), spec(pl.ANY)],
        out_specs=(spec(VMEM),) * 6,
        scratch_shapes=[
            VMEM((local_experts, share, hidden_size), bf16),
            pltpu.SemaphoreType.DMA((local_experts,)),
        ],
    )(gathered, down_weight.swapaxes(1, 2))

    parts = reduce_blocks(send, dp_count)
    hidden, shares = pl.pallas_call(
        functools.partial(hidden_kernel, len(parts)),
        out_shape=(shaped((piece, hidden_size), bf16), shaped((devices, 1, LANES), f32)),
        in_specs=[spec(pl.ANY)] * 2 + [spec(VMEM)] * len(parts),
        out_specs=(spec(VMEM),) * 2,
        scratch_shapes=[
            VMEM((piece, hidden_size), bf16),
            VMEM((piece, hidden_size), bf16),
            pltpu.SemaphoreType.DMA((2,)),
        ],
    )(
        gate_saved.reshape(dp_count, piece, hidden_size),
        up_saved.reshape(dp_count, piece, hidden_size),
        *parts,
    )
    blocks = spread_blocks(hidden, dp_count)
    shares = lax.all_to_all(shares, ("dp", "expert"), 0, 0, tiled=True)

    mixed = pl.pallas_call(
        functools.partial(input_kernel, len(blocks), slots),
        out_shape=shaped((expert_count, group, share), bf16),
        in_specs=[spec(pl.ANY)] * 2 + [spec(VMEM)] * (4 + len(blocks)),
        out_specs=spec(VMEM),
        scratch_shapes=[
            VMEM((local_experts, share, hidden_size), bf16),
            VMEM((local_experts, share, hidden_size), bf16),
            VMEM((dp_count, piece, hidden_size), bf16),
            VMEM((rows, share), f32),
            pltpu.SemaphoreType.DMA((2 * local_experts,)),
        ],
    )(gate_weight, up_weight, high, low, gate_saved, up_saved, *blocks)
    mixed = lax.all_to_all(mixed, "expert", 0, 0, tiled=True)

    grad_router, router_part = pl.pallas_call(
        functools.partial(router_kernel, (group, depth, slots, dp_count, expert_count)),
        out_shape=(shaped((local_experts, share), f32), shaped((group, share), f32)),
        in_specs=[spec(VMEM)] * 6,
        out_specs=(spec(VMEM),) * 2,
    )(shares, gates, slope, slot, routed, router_weight)
    grad_input = jnp.sum(mixed.astype(f32), axis=0) + router_part
    return grad_input.astype(bf16)[None], grad_router


def solution(mesh):
    placed = (
        P("expert", None, "dp"),
        P("expert", None, None),
        P("expert", None, None),
        P("expert", "dp", None),
        P(None, "dp"),
        P("expert", "dp", None),
        P("expert", "dp", None),
        P("expert", None, "dp"),
        P("expert", None, None),
        P("expert", None, None),
    )
    return jax.shard_map(
        local,
        mesh=mesh,
        in_specs=placed,
        out_specs=(P("expert", None, "dp"), P("expert", "dp")),
        check_vma=False,
    )
```

time: 148 us -> 78.6 us (0.53)
  waiting for transfers between devices: 84.4 us -> 20.7 us
  Pallas kernels: 0 us -> 21.9 us
  matrix products: 19.4 us -> 0 us
  between operations: 14.9 us -> 0.74 us
  blocking collectives: 0 us -> 11 us
  local copies, waits for them, and re-layouts: 7.53 us -> 4.46 us
  other arithmetic: 3.35 us -> 1.39 us
    unnamed x3 -> x0, waiting for transfers between devices: 42.6 us -> none
    psum x1 -> x0, waiting for transfers between devices: 36.3 us -> none  [local(): hidden_grad = lax.psum(partial_hidden.reshape(row_total, hidden_size), 'dp')]
    pallas_call x0 -> x5, Pallas kernels: none -> 21.9 us  [the longest x1 9.87 us: local(): pl.pallas_call(functools.partial(input_kernel, len(blocks), slots), out_s...]
    dot_general x8 -> x0, matrix products: 19.4 us -> none  [the longest x1 5.39 us: local(): jnp.einsum('esf,edf->esd', grad_up, up_weight, preferred_element_type=jnp...]
    ppermute x0 -> x6, waiting for transfers between devices: none -> 11.7 us  [the longest x3 5.89 us: spread_blocks(): lax.ppermute(block, 'dp', [(j, j ^ k) for j in range(count)])]
    all_to_all x0 -> x1, blocking collectives: none -> 11 us  [local(): lax.all_to_all(packed, 'expert', 0, 0, tiled=True)]
    all_to_all x4 -> x3, starting transfers between devices: 17.8 us -> 8.84 us  [the longest x1 3.71 us: local(): mixed = lax.all_to_all(mixed, 'expert', 0, 0, tiled=True)]
    ppermute x0 -> x6, starting transfers between devices: none -> 8.84 us  [the longest x3 4.45 us: spread_blocks(): lax.ppermute(block, 'dp', [(j, j ^ k) for j in range(count)])]
  transfers between devices with their start and end apart: 6 -> 9, of which waited for: 3 -> 7; matrix products, arithmetic and copies ran while one was open for 13% -> 1% of each run, Pallas kernels for 0% -> 16%
where the time goes in v1:
time: 78.6 us; the launch traced here: 77.8 us
  Pallas kernels  21.9 us (28%)
  waiting for transfers between devices  20.7 us (26%)
  starting transfers between devices  17.7 us (23%)
  blocking collectives  11 us (14%)
  local copies, waits for them, and re-layouts  4.46 us (6%)
  other arithmetic  1.39 us (2%)
    all_to_all x1, blocking collectives, local(): lax.all_to_all(packed, 'expert', 0, 0, tiled=True)  11 us
    pallas_call x1, Pallas kernels, local(): pl.pallas_call(functools.partial(input_kernel, len(blocks), slots), out_s...  9.87 us
    all_to_all x1, waiting for transfers between devices, local(): shares = lax.all_to_all(shares, ('dp', 'expert'), 0, 0, tiled=True)  7.04 us
    ppermute x3, waiting for transfers between devices, spread_blocks(): lax.ppermute(block, 'dp', [(j, j ^ k) for j in range(count)])  5.89 us
    ppermute x3, waiting for transfers between devices, reduce_blocks(): lax.ppermute(send[k], 'dp', [(j, j ^ k) for j in range(count)])  5.83 us
    pallas_call x1, Pallas kernels, local(): pl.pallas_call(functools.partial(down_kernel, sizes), out_shape=(shaped((...  5.42 us
    ppermute x3, starting transfers between devices, spread_blocks(): lax.ppermute(block, 'dp', [(j, j ^ k) for j in range(count)])  4.45 us
    ppermute x3, starting transfers between devices, reduce_blocks(): lax.ppermute(send[k], 'dp', [(j, j ^ k) for j in range(count)])  4.39 us
  transfers between devices with their start and end apart: 9, of which 7 were waited for; matrix products, arithmetic and copies ran while one was open for 1% of the time, Pallas kernels for 16%

profile of v1, /device:TPU:0, one launch (start us, length us, event | category | flops | bytes accessed | tf_op | source)
XLA Modules:
  0.0 77.8 jit_solution(6140619014801435032)
XLA Ops:
  0.6 1.5 %shard_map.113 = bf16[8,8,1088]{2,1,0:T(8,128)(2,1)} custom-call(f32[1,8,32]{2,1,0:T(8,128)} %logits_ref.1, s32[1,8,8]{2,1,0:T(8,128)} %ids_ref.1, bf16[1,8,960]{2,1,0:T(8,128)(2,1)} %rows_ref.1), custom_call_target="tpu_custom_call" | custom-call | tf_op jit(solution)/shard_map/pallas_call | solution.py:301
  2.1 11.0 %all_to_all.20 = bf16[8,8,1088]{2,1,0:T(8,128)(2,1)} all-to-all(bf16[8,8,1088]{2,1,0:T(8,128)(2,1)} %shard_map.113), channel_id=1, replica_groups=mesh['dp'=4,'expert'=8] {'expert'}, dimensions={0} | all-to-all | bytes 278528 | tf_op jit(solution)/shard_map/all_to_all | solution.py:307
  13.1 5.4 %shard_map.114 = (bf16[4,24,1024]{2,1,0:T(8,128)(2,1)}, bf16[64,96]{1,0:T(8,128)(2,1)}, bf16[64,96]{1,0:T(8,128)(2,1)}, f32[64,32]{1,0:T(8,128)}, f32[64,32]{1,0:T(8,128)}, /*index=5*/f32[64,32]{1,0:T(8,128)}) custom-call(bf16[64,1088]{1,0:T(8,128)(2,1)} %bitcast.20, bf16[4,960,1024]{2,1,0:T(8,128)(2,1)} %bitcast.19), custom_call_target="tpu_custom_call" | custom-call | tf_op jit(solution)/shard_map/pallas_call | solution.py:311
  18.5 1.5 %slice_bitcast_fusion = (bf16[24,1024]{1,0:T(8,128)(2,1)S(1)}, bf16[24,1024]{1,0:T(8,128)(2,1)S(1)}, bf16[24,1024]{1,0:T(8,128)(2,1)S(1)}, bf16[24,1024]{1,0:T(8,128)(2,1)}) fusion(bf16[4,24,1024]{2,1,0:T(8,128)(2,1)} %get-tuple-element.14), kind=kLoop, calls=%fused_computation.2 | loop fusion | bytes 393216 | tf_op jit(solution)/shard_map/squeeze | solution.py:253
  20.0 1.7 %collective-permute-start = (bf16[24,1024]{1,0:T(8,128)(2,1)S(1)}, bf16[24,1024]{1,0:T(8,128)(2,1)S(1)}, u32[]{:S(2)}, u32[]{:S(2)}) collective-permute-start(bf16[24,1024]{1,0:T(8,128)(2,1)S(1)} %get-tuple-element.24), channel_id=1, source_target_pairs={{0,8},{8,0},{16,24},{24,16},{1,9},{9,1},{17,25},{25,17},{2,10},{10... | collective-permute-start | bytes 147464 | tf_op jit(solution)/shard_map/ppermute | solution.py:253
  21.8 2.6 %collective-permute-start.1 = (bf16[24,1024]{1,0:T(8,128)(2,1)S(1)}, bf16[24,1024]{1,0:T(8,128)(2,1)S(1)}, u32[]{:S(2)}, u32[]{:S(2)}) collective-permute-start(bf16[24,1024]{1,0:T(8,128)(2,1)S(1)} %get-tuple-element.23), channel_id=1, source_target_pairs={{0,16},{8,24},{16,0},{24,8},{1,17},{9,25},{17,1},{25,9},{2,18},{10... | collective-permute-start | bytes 147464 | tf_op jit(solution)/shard_map/ppermute | solution.py:253
  24.4 3.0 %collective-permute-done.1.refs_2_ = bf16[24,1024]{1,0:T(8,128)(2,1)S(1)} collective-permute-done((bf16[24,1024]{1,0:T(8,128)(2,1)S(1)}, bf16[24,1024]{1,0:T(8,128)(2,1)S(1)}, u32[]{:S(2)}, u32[]{:S(2)}) %collective-permute-start.1) | collective-permute-done | bytes 49184 | tf_op jit(solution)/shard_map/ppermute | solution.py:253
  27.4 2.8 %collective-permute-done.2.refs_3_ = bf16[24,1024]{1,0:T(8,128)(2,1)S(1)} collective-permute-done((bf16[24,1024]{1,0:T(8,128)(2,1)S(1)}, bf16[24,1024]{1,0:T(8,128)(2,1)S(1)}, u32[]{:S(2)}, u32[]{:S(2)}) %collective-permute-start.2) | collective-permute-done | bytes 49184 | tf_op jit(solution)/shard_map/ppermute | solution.py:253
  30.9 2.4 %shard_map.115 = (bf16[24,1024]{1,0:T(8,128)(2,1)}, f32[32,1,128]{2,1,0:T(1,128)}) custom-call(bf16[4,24,1024]{2,1,0:T(8,128)(2,1)} %gate_ref.3, bf16[4,24,1024]{2,1,0:T(8,128)(2,1)} %up_ref.3, bf16[24,1024]{1,0:T(8,128)(2,1)} %get-tuple-element.25.refs_0_, bf16[24,1024]{1,0:T(8,128)(2,1)} %copy-done.1, bf16[24,1024]{1,0:T(8,128)(2,1)} %copy-done.2, ...), custom_call_target="tpu_custom_call" | custom-call | tf_op jit(solution)/shard_map/pallas_call | solution.py:330
  33.3 2.6 %all-to-all-start.2 = ((f32[32,1,128]{2,1,0:T(1,128)}), f32[32,1,128]{2,1,0:T(1,128)S(1)}, u32[]{:S(2)}, u32[]{:S(2)}) async-start(f32[32,1,128]{2,1,0:T(1,128)} %get-tuple-element.16), calls=%async_computation.2 | async-start | bytes 32768 | tf_op jit(solution)/shard_map/all_to_all | solution.py:346
  36.0 7.0 %all-to-all-done.2.shares_ref = f32[32,1,128]{2,1,0:T(1,128)S(1)} async-done(((f32[32,1,128]{2,1,0:T(1,128)}), f32[32,1,128]{2,1,0:T(1,128)S(1)}, u32[]{:S(2)}, u32[]{:S(2)}) %all-to-all-start.2) | async-done | bytes 16416 | tf_op jit(solution)/shard_map/all_to_all | solution.py:346
  43.1 0.7 broadcast_in_dim.4
  43.8 2.6 %all-to-all-start.3 = ((bf16[32,2,960]{2,1,0:T(2,128)(2,1)}), bf16[32,2,960]{2,1,0:T(2,128)(2,1)S(1)}, u32[]{:S(2)}, u32[]{:S(2)}) async-start(bf16[32,2,960]{2,1,0:T(2,128)(2,1)} %bitcast.7), calls=%async_computation.3 | async-start | bytes 262144 | tf_op jit(solution)/shard_map/all_to_all | solution.py:295
  46.4 1.8 %collective-permute-start.3 = (bf16[24,1024]{1,0:T(8,128)(2,1)}, bf16[24,1024]{1,0:T(8,128)(2,1)S(1)}, u32[]{:S(2)}, u32[]{:S(2)}) collective-permute-start(bf16[24,1024]{1,0:T(8,128)(2,1)} %get-tuple-element.15.refs_0_), channel_id=1, source_target_pairs={{0,8},{8,0},{16,24},{24,16},{1,9},{9,1},{17,25},{25,17},{2,10},{10... | collective-permute-start | bytes 147464 | tf_op jit(solution)/shard_map/ppermute | solution.py:261
  48.1 2.5 %collective-permute-start.4 = (bf16[24,1024]{1,0:T(8,128)(2,1)}, bf16[24,1024]{1,0:T(8,128)(2,1)S(1)}, u32[]{:S(2)}, u32[]{:S(2)}) collective-permute-start(bf16[24,1024]{1,0:T(8,128)(2,1)} %get-tuple-element.15.refs_0_), channel_id=1, source_target_pairs={{0,16},{8,24},{16,0},{24,8},{1,17},{9,25},{17,1},{25,9},{2,18},{10... | collective-permute-start | bytes 147464 | tf_op jit(solution)/shard_map/ppermute | solution.py:261
  50.8 0.9 %collective-permute-done.3.refs_1_ = bf16[24,1024]{1,0:T(8,128)(2,1)S(1)} collective-permute-done((bf16[24,1024]{1,0:T(8,128)(2,1)}, bf16[24,1024]{1,0:T(8,128)(2,1)S(1)}, u32[]{:S(2)}, u32[]{:S(2)}) %collective-permute-start.3) | collective-permute-done | bytes 49184 | tf_op jit(solution)/shard_map/ppermute | solution.py:261
  51.7 3.0 %collective-permute-done.4.refs_2_ = bf16[24,1024]{1,0:T(8,128)(2,1)S(1)} collective-permute-done((bf16[24,1024]{1,0:T(8,128)(2,1)}, bf16[24,1024]{1,0:T(8,128)(2,1)S(1)}, u32[]{:S(2)}, u32[]{:S(2)}) %collective-permute-start.4) | collective-permute-done | bytes 49184 | tf_op jit(solution)/shard_map/ppermute | solution.py:261
  54.7 2.0 %collective-permute-done.5.refs_3_ = bf16[24,1024]{1,0:T(8,128)(2,1)S(1)} collective-permute-done((bf16[24,1024]{1,0:T(8,128)(2,1)}, bf16[24,1024]{1,0:T(8,128)(2,1)S(1)}, u32[]{:S(2)}, u32[]{:S(2)}) %collective-permute-start.5) | collective-permute-done | bytes 49184 | tf_op jit(solution)/shard_map/ppermute | solution.py:261
  57.3 9.9 %shard_map.116 = bf16[8,8,960]{2,1,0:T(8,128)(2,1)} custom-call(bf16[4,960,1024]{2,1,0:T(8,128)(2,1)} %gate_w_ref.1, bf16[4,960,1024]{2,1,0:T(8,128)(2,1)} %up_w_ref.1, bf16[64,96]{1,0:T(8,128)(2,1)} %get-tuple-element.12.high_ref, bf16[64,96]{1,0:T(8,128)(2,1)} %get-tuple-element.13.low_ref, bf16[4,24,1024]{2,1,0:T(8,128)(2,1)} %gate_ref.3, ...), custom_call_target="tpu_custom_call" | custom-call | tf_op jit(solution)/shard_map/pallas_call | solution.py:348
  67.2 3.7 %all-to-all-start.1 = ((bf16[8,8,960]{2,1,0:T(8,128)(2,1)}), bf16[8,8,960]{2,1,0:T(8,128)(2,1)S(1)}, u32[]{:S(2)}, u32[]{:S(2)}) async-start(bf16[8,8,960]{2,1,0:T(8,128)(2,1)} %shard_map.116), calls=%async_computation.1 | async-start | bytes 262144 | tf_op jit(solution)/shard_map/all_to_all | solution.py:361
  71.1 0.7 reshape.24.inputs_ref
  71.8 2.6 %shard_map.117 = (f32[4,960]{1,0:T(4,128)}, f32[8,960]{1,0:T(8,128)}) custom-call(f32[32,1,128]{2,1,0:T(1,128)} %copy-done, f32[64,32]{1,0:T(8,128)} %get-tuple-element.17.gates_ref, f32[64,32]{1,0:T(8,128)} %get-tuple-element.18.slope_ref, f32[64,32]{1,0:T(8,128)} %get-tuple-element.19.slot_ref, bf16[64,960]{1,0:T(8,128)(2,1)} %reshape.24.inputs_ref, ...), custom_call_target="tpu_custom_call" | custom-call | tf_op jit(solution)/shard_map/pallas_call | solution.py:363
  74.5 2.0 %all-to-all-done.1 = bf16[8,8,960]{2,1,0:T(8,128)(2,1)S(1)} async-done(((bf16[8,8,960]{2,1,0:T(8,128)(2,1)}), bf16[8,8,960]{2,1,0:T(8,128)(2,1)S(1)}, u32[]{:S(2)}, u32[]{:S(2)}) %all-to-all-start.1) | async-done | bytes 122912 | tf_op jit(solution)/shard_map/all_to_all | solution.py:361
  76.5 1.4 %fusion = bf16[1,8,960]{2,1,0:T(8,128)(2,1)} fusion(f32[8,960]{1,0:T(8,128)S(1)} %convert_reduce_fusion, f32[8,960]{1,0:T(8,128)} %get-tuple-element.20), kind=kLoop, calls=%fused_computation.7 | loop fusion | flops 15360 | bytes 76800 | tf_op jit(solution)/shard_map/broadcast_in_dim | solution.py:370
  (25 shorter events, 1.8 us)
Async XLA Ops:
  0.6 35.3 %copy-start.7 = (bf16[1,2,3840]{2,1,0:T(2,128)(2,1)S(1)}, bf16[1,2,3840]{2,1,0:T(2,128)(2,1)}, u32[]{:S(2)}) copy-start(bf16[1,2,3840]{2,1,0:T(2,128)(2,1)} %param.13) | copy-start | bytes 46084
  20.0 4.4 %collective-permute-start = (bf16[24,1024]{1,0:T(8,128)(2,1)S(1)}, bf16[24,1024]{1,0:T(8,128)(2,1)S(1)}, u32[]{:S(2)}, u32[]{:S(2)}) collective-permute-start(bf16[24,1024]{1,0:T(8,128)(2,1)S(1)} %get-tuple-element.24), channel_id=1, source_target_pairs={{0,8},{8,0},{16,24},{24,16},{1,9},{9,1},{17,25},{25,17},{2,10},{10... | collective-permute-start | bytes 147464 | tf_op jit(solution)/shard_map/ppermute | solution.py:253
  21.8 5.6 %collective-permute-start.1 = (bf16[24,1024]{1,0:T(8,128)(2,1)S(1)}, bf16[24,1024]{1,0:T(8,128)(2,1)S(1)}, u32[]{:S(2)}, u32[]{:S(2)}) collective-permute-start(bf16[24,1024]{1,0:T(8,128)(2,1)S(1)} %get-tuple-element.23), channel_id=1, source_target_pairs={{0,16},{8,24},{16,0},{24,8},{1,17},{9,25},{17,1},{25,9},{2,18},{10... | collective-permute-start | bytes 147464 | tf_op jit(solution)/shard_map/ppermute | solution.py:253
  24.4 5.9 %collective-permute-start.2 = (bf16[24,1024]{1,0:T(8,128)(2,1)S(1)}, bf16[24,1024]{1,0:T(8,128)(2,1)S(1)}, u32[]{:S(2)}, u32[]{:S(2)}) collective-permute-start(bf16[24,1024]{1,0:T(8,128)(2,1)S(1)} %get-tuple-element.22), channel_id=1, source_target_pairs={{0,24},{8,16},{16,8},{24,0},{1,25},{9,17},{17,9},{25,1},{2,26},{10... | collective-permute-start | bytes 147464 | tf_op jit(solution)/shard_map/ppermute | solution.py:253
  24.4 5.8 %copy-start.1 = (bf16[24,1024]{1,0:T(8,128)(2,1)}, bf16[24,1024]{1,0:T(8,128)(2,1)S(1)}, u32[]{:S(2)}) copy-start(bf16[24,1024]{1,0:T(8,128)(2,1)S(1)} %collective-permute-done.refs_1_) | copy-start | bytes 147460
  27.4 2.9 %copy-start.2 = (bf16[24,1024]{1,0:T(8,128)(2,1)}, bf16[24,1024]{1,0:T(8,128)(2,1)S(1)}, u32[]{:S(2)}) copy-start(bf16[24,1024]{1,0:T(8,128)(2,1)S(1)} %collective-permute-done.1.refs_2_) | copy-start | bytes 147460
  30.3 0.6 copy-start.3
  33.3 9.7 %all-to-all-start.2 = ((f32[32,1,128]{2,1,0:T(1,128)}), f32[32,1,128]{2,1,0:T(1,128)S(1)}, u32[]{:S(2)}, u32[]{:S(2)}) async-start(f32[32,1,128]{2,1,0:T(1,128)} %get-tuple-element.16), calls=%async_computation.2 | async-start | bytes 32768 | tf_op jit(solution)/shard_map/all_to_all | solution.py:346
  43.1 24.1 %copy-start = (f32[32,1,128]{2,1,0:T(1,128)}, f32[32,1,128]{2,1,0:T(1,128)S(1)}, u32[]{:S(2)}) copy-start(f32[32,1,128]{2,1,0:T(1,128)S(1)} %all-to-all-done.2.shares_ref) | copy-start | bytes 49156
  43.8 23.4 %all-to-all-start.3 = ((bf16[32,2,960]{2,1,0:T(2,128)(2,1)}), bf16[32,2,960]{2,1,0:T(2,128)(2,1)S(1)}, u32[]{:S(2)}, u32[]{:S(2)}) async-start(bf16[32,2,960]{2,1,0:T(2,128)(2,1)} %bitcast.7), calls=%async_computation.3 | async-start | bytes 262144 | tf_op jit(solution)/shard_map/all_to_all | solution.py:295
  46.4 5.3 %collective-permute-start.3 = (bf16[24,1024]{1,0:T(8,128)(2,1)}, bf16[24,1024]{1,0:T(8,128)(2,1)S(1)}, u32[]{:S(2)}, u32[]{:S(2)}) collective-permute-start(bf16[24,1024]{1,0:T(8,128)(2,1)} %get-tuple-element.15.refs_0_), channel_id=1, source_target_pairs={{0,8},{8,0},{16,24},{24,16},{1,9},{9,1},{17,25},{25,17},{2,10},{10... | collective-permute-start | bytes 147464 | tf_op jit(solution)/shard_map/ppermute | solution.py:261
  48.1 6.6 %collective-permute-start.4 = (bf16[24,1024]{1,0:T(8,128)(2,1)}, bf16[24,1024]{1,0:T(8,128)(2,1)S(1)}, u32[]{:S(2)}, u32[]{:S(2)}) collective-permute-start(bf16[24,1024]{1,0:T(8,128)(2,1)} %get-tuple-element.15.refs_0_), channel_id=1, source_target_pairs={{0,16},{8,24},{16,0},{24,8},{1,17},{9,25},{17,1},{25,9},{2,18},{10... | collective-permute-start | bytes 147464 | tf_op jit(solution)/shard_map/ppermute | solution.py:261
  50.6 6.1 %collective-permute-start.5 = (bf16[24,1024]{1,0:T(8,128)(2,1)}, bf16[24,1024]{1,0:T(8,128)(2,1)S(1)}, u32[]{:S(2)}, u32[]{:S(2)}) collective-permute-start(bf16[24,1024]{1,0:T(8,128)(2,1)} %get-tuple-element.15.refs_0_), channel_id=1, source_target_pairs={{0,24},{8,16},{16,8},{24,0},{1,25},{9,17},{17,9},{25,1},{2,26},{10... | collective-permute-start | bytes 147464 | tf_op jit(solution)/shard_map/ppermute | solution.py:261
  51.7 5.0 %copy-start.4 = (bf16[24,1024]{1,0:T(8,128)(2,1)}, bf16[24,1024]{1,0:T(8,128)(2,1)S(1)}, u32[]{:S(2)}) copy-start(bf16[24,1024]{1,0:T(8,128)(2,1)S(1)} %collective-permute-done.3.refs_1_) | copy-start | bytes 147460
  54.7 2.0 %copy-start.5 = (bf16[24,1024]{1,0:T(8,128)(2,1)}, bf16[24,1024]{1,0:T(8,128)(2,1)S(1)}, u32[]{:S(2)}) copy-start(bf16[24,1024]{1,0:T(8,128)(2,1)S(1)} %collective-permute-done.4.refs_2_) | copy-start | bytes 147460
  56.7 0.6 copy-start.6
  67.2 9.2 %all-to-all-start.1 = ((bf16[8,8,960]{2,1,0:T(8,128)(2,1)}), bf16[8,8,960]{2,1,0:T(8,128)(2,1)S(1)}, u32[]{:S(2)}, u32[]{:S(2)}) async-start(bf16[8,8,960]{2,1,0:T(8,128)(2,1)} %shard_map.116), calls=%async_computation.1 | async-start | bytes 262144 | tf_op jit(solution)/shard_map/all_to_all | solution.py:361

commit v2 on v0

v2 whole, which is shorter than its diff:
```python
import functools

import jax
import jax.numpy as jnp
from jax import lax
from jax.experimental import pallas as pl
from jax.experimental.pallas import tpu as pltpu
from jax.sharding import PartitionSpec as P

route_scale = 2.5
LANES = 128
HIGH = lax.Precision.HIGHEST
VMEM = pltpu.VMEM
ROWS_ROWS = (((1,), (1,)), ((), ()))


def iota(shape, dim):
    return lax.broadcasted_iota(jnp.int32, shape, dim)


def place_of(block, me, paired):
    return lax.bitwise_xor(block, me) if paired else block


def call(kernel, outs, args, scratch=(), flops=0, far_args=False, far_outs=False):
    far, near = pl.BlockSpec(memory_space=pltpu.HBM), pl.BlockSpec(memory_space=VMEM)
    several = isinstance(outs[0][0], tuple)
    space = pltpu.HBM if far_outs else VMEM
    out_spec = far if far_outs else near
    arg_space = pltpu.HBM if far_args else VMEM
    return pl.pallas_call(
        kernel,
        out_shape=tuple(space(*out) for out in outs) if several else space(*outs),
        in_specs=[far if far_args else near] * len(args),
        out_specs=(out_spec,) * len(outs) if several else out_spec,
        scratch_shapes=list(scratch),
        compiler_params=pltpu.CompilerParams(vmem_limit_bytes=12 << 20),
        cost_estimate=pl.CostEstimate(flops=flops, bytes_accessed=0, transcendentals=0),
    )(*[pltpu.with_memory_space_constraint(arg, arg_space) for arg in args])


def pack_kernel(
    expert_total, logits_far, ids_far, rows_far, out_ref, logits_ref, ids_ref, rows_ref, sems
):
    pairs = ((logits_far, logits_ref), (ids_far, ids_ref), (rows_far, rows_ref))
    fetches = [pltpu.make_async_copy(*pair, sems.at[n]) for n, pair in enumerate(pairs)]
    for fetch in fetches:
        fetch.start()
    for fetch in fetches:
        fetch.wait()
    copies, group, width = out_ref.shape
    top = ids_ref.shape[2]
    aux = width - rows_ref.shape[2]
    logits = logits_ref[0]
    first = logits.astype(jnp.bfloat16).astype(jnp.float32)
    rest = logits - first
    second = rest.astype(jnp.bfloat16).astype(jnp.float32)
    pieces = [first, second, rest - second, ids_ref[0].astype(jnp.float32)]
    spare = aux - 3 * expert_total - top
    if spare:
        pieces.append(jnp.zeros((group, spare), jnp.float32))
    head = jnp.concatenate(pieces, axis=1).astype(jnp.bfloat16)
    rows = rows_ref[0]
    for copy in range(copies):
        out_ref[copy, :, :aux] = head
        out_ref[copy, :, aux:] = rows


def routing(head, sizes):
    group, expert_total, top, depth = sizes
    tokens = head.shape[0]
    lane = iota((tokens, expert_total), 1)
    named = jnp.zeros((tokens, expert_total), jnp.float32)
    for k in range(top):
        at = 3 * expert_total + k
        named = named + (head[:, at : at + 1].astype(jnp.int32) == lane).astype(jnp.float32)
    row_at, col_at = iota((tokens, tokens), 0), iota((tokens, tokens), 1)
    earlier = (lax.div(row_at, group) == lax.div(col_at, group)) & (col_at < row_at)
    rank = jnp.dot(
        earlier.astype(jnp.bfloat16), named.astype(jnp.bfloat16), preferred_element_type=jnp.float32
    )
    first_slot = (lax.div(iota((tokens, expert_total), 0), group) * depth).astype(jnp.float32)
    return named, jnp.where(named > 0.5, first_slot + rank, -1.0)


def down_kernel(sizes, aux, paired, tokens_ref, weight_ref, *send_refs):
    expert_total = sizes[1]
    tokens = tokens_ref.shape[0]
    local_experts = weight_ref.shape[0]
    slots = send_refs[0].shape[0]
    me = lax.axis_index("dp")
    base = lax.axis_index("expert") * local_experts
    _, slot = routing(tokens_ref[:, :aux].astype(jnp.float32), sizes)
    order = place_of(iota((8, expert_total), 0), me, paired)
    pick = (iota((8, expert_total), 1) == base + order).astype(jnp.bfloat16)
    slot_rows = lax.dot_general(
        pick, slot.astype(jnp.bfloat16), ROWS_ROWS, preferred_element_type=jnp.float32
    )
    features = tokens_ref[:, aux:]
    slot_at = iota((slots, tokens), 0).astype(jnp.float32)
    for k, send_ref in enumerate(send_refs):
        chosen = (slot_at == slot_rows[k : k + 1, :]).astype(jnp.bfloat16)
        sent = jnp.dot(chosen, features, preferred_element_type=jnp.float32).astype(jnp.bfloat16)
        weight = weight_ref[place_of(k, me, paired)]
        send_ref[...] = jnp.dot(sent, weight, preferred_element_type=jnp.float32).astype(jnp.bfloat16)


def table_kernel(sizes, local_experts, paired, head_ref, inputs_ref, full_ref, slope_ref, *piece_refs):
    _, expert_total, _, _ = sizes
    tokens, rows = full_ref.shape
    slots = rows // local_experts
    dp_count = lax.axis_size("dp")
    me = lax.axis_index("dp")
    base = lax.axis_index("expert") * local_experts
    head = head_ref[...].astype(jnp.float32)
    logits = (
        head[:, :expert_total]
        + head[:, expert_total : 2 * expert_total]
        + head[:, 2 * expert_total : 3 * expert_total]
    )
    named, slot = routing(head, sizes)
    scores = jax.nn.sigmoid(logits)
    total = jnp.sum(named * scores, axis=1, keepdims=True)
    gates = route_scale * (named * scores) / total
    slope_ref[...] = named * scores * (1.0 - scores) / total
    order = place_of(lax.div(iota((expert_total, rows), 1), slots), me, paired)
    spread = (iota((expert_total, rows), 0) == base + order).astype(jnp.float32)
    slot_wide = jnp.dot(slot, spread, precision=HIGH, preferred_element_type=jnp.float32)
    gates_wide = jnp.dot(gates, spread, precision=HIGH, preferred_element_type=jnp.float32)
    wanted = lax.rem(iota((tokens, rows), 1), slots).astype(jnp.float32)
    full_ref[...] = jnp.where(slot_wide == wanted, gates_wide, 0.0)
    share = inputs_ref.shape[2] // dp_count
    pieces = [inputs_ref[0, :, d * share : (d + 1) * share] for d in range(dp_count)]
    if paired:
        for k, piece_ref in enumerate(piece_refs):
            found = pieces[0]
            for d in range(1, dp_count):
                found = jnp.where(lax.bitwise_xor(k, me) == d, pieces[d], found)
            piece_ref[...] = found
    else:
        for d in range(dp_count):
            piece_refs[0][d] = pieces[d]


def expert_parts(k, paired, gate_w_ref, up_w_ref, gate_ref, up_ref, block_ref, row_ref, share_ref):
    expert = place_of(k, lax.axis_index("dp"), paired)
    hidden_grad = block_ref[...].astype(jnp.float32)
    gate_value = gate_ref[expert].astype(jnp.float32)
    up_value = up_ref[expert].astype(jnp.float32)
    sig = jax.nn.sigmoid(gate_value)
    activated = gate_value * sig
    gate_part = (hidden_grad * up_value * sig * (1.0 + gate_value * (1.0 - sig))).astype(jnp.bfloat16)
    up_part = (hidden_grad * activated).astype(jnp.bfloat16)
    value = lax.dot_general(
        gate_part, gate_w_ref[expert], ROWS_ROWS, preferred_element_type=jnp.float32
    ) + lax.dot_general(up_part, up_w_ref[expert], ROWS_ROWS, preferred_element_type=jnp.float32)
    row_ref[...] = value
    hidden = (activated * up_value).astype(jnp.bfloat16).astype(jnp.float32)
    given = jnp.sum(hidden * hidden_grad, axis=1, keepdims=True)
    slots, width = hidden_grad.shape[0], share_ref.shape[1]
    across = iota((slots, width), 0) + k * slots == iota((slots, width), 1)
    share_ref[...] = jnp.sum(jnp.where(across, given, 0.0), axis=0, keepdims=True)


def input_kernel(k, paired, *refs):
    expert_parts(k, paired, *refs)


def split(values):
    upper = values.astype(jnp.bfloat16)
    return upper, (values - upper.astype(jnp.float32)).astype(jnp.bfloat16)


def mix_kernel(k, paired, piece_count, full_ref, *refs):
    weights, rest = refs[:5], refs[5:]
    piece_refs, rest = rest[:piece_count], rest[piece_count:]
    earlier, (out_ref, own_ref, held_ref, share_ref) = rest[:-4], rest[-4:]
    slots = weights[4].shape[0]
    expert_parts(k, paired, *weights, held_ref.at[pl.ds(k * slots, slots)], share_ref)
    shares = share_ref[...]
    for at in range(k):
        held_ref[at * slots : (at + 1) * slots] = earlier[2 * at][...]
        shares = shares + earlier[2 * at + 1][...]
    full = full_ref[...]
    tokens, rows = full.shape
    local_experts = k + 1
    copies, double, width = out_ref.shape
    group = double // 2
    share = held_ref.shape[1]
    high, low = split(full)
    given = shares[:, :rows]
    mixture = jnp.sum(full * given, axis=1, keepdims=True)
    held_lane = jnp.where(full != 0.0, given, 0.0)
    expert_of = lax.div(iota((tokens, rows), 1), slots)
    own = jnp.zeros((tokens, LANES), jnp.float32)
    for e in range(local_experts):
        dg = jnp.sum(jnp.where(expert_of == e, held_lane, 0.0), axis=1, keepdims=True)
        own = own + jnp.where(iota((tokens, LANES), 1) == e, dg, 0.0)
    own_ref[...] = own
    row_group = lax.div(iota((tokens, LANES), 0), group)
    spread = jnp.where(row_group == iota((tokens, LANES), 1), mixture, 0.0)
    mix_high, mix_low = split(spread)
    same = lax.rem(iota((tokens, tokens), 0), group) == lax.rem(iota((tokens, tokens), 1), group)
    same = same.astype(jnp.bfloat16)
    mix_high = jnp.dot(same, mix_high, preferred_element_type=jnp.float32)
    mix_low = jnp.dot(same, mix_low, preferred_element_type=jnp.float32)
    own_high, own_low = split(own)
    extra = jnp.concatenate(
        [
            mix_high[:, :copies],
            mix_low[:, :copies],
            own_high[:, :local_experts].astype(jnp.float32),
            own_low[:, :local_experts].astype(jnp.float32),
            jnp.zeros((tokens, width - share - 2 * copies - 2 * local_experts), jnp.float32),
        ],
        axis=1,
    ).astype(jnp.bfloat16)
    values = held_ref[...].astype(jnp.bfloat16)
    mixed = jnp.dot(high, values, preferred_element_type=jnp.float32)
    mixed = mixed + jnp.dot(low, values, preferred_element_type=jnp.float32)
    if piece_count == 1:
        routed = piece_refs[0][...].reshape(group, share)
    else:
        routed = jnp.concatenate([ref[...].astype(jnp.float32) for ref in piece_refs], axis=0)
        routed = routed.astype(jnp.bfloat16)
    for q in range(copies):
        lines = slice(q * group, (q + 1) * group)
        out_ref[q, :group, :share] = mixed[lines].astype(jnp.bfloat16)
        out_ref[q, :group, share:] = extra[lines]
        out_ref[q, group:, :share] = routed
        out_ref[q, group:, share:] = jnp.zeros((group, width - share), jnp.bfloat16)


def final_kernel(
    sizes,
    paired,
    got_ref,
    own_ref,
    slope_ref,
    weight_ref,
    input_far,
    router_far,
    input_ref,
    router_ref,
    sems,
):
    group, expert_total, _, _ = sizes
    tokens = slope_ref.shape[0]
    copies = got_ref.shape[0]
    local_experts, share = router_ref.shape
    dp_count = lax.axis_size("dp")
    dp_me, me = lax.axis_index("dp"), lax.axis_index("expert")
    mixed = jnp.zeros((group, share), jnp.float32)
    sums = jnp.zeros((group, 2 * copies), jnp.float32)
    given = jnp.zeros((group, expert_total), jnp.float32)
    own_at = share + 2 * copies
    own_end = own_at + 2 * local_experts
    part = (2 * local_experts, expert_total)
    order = place_of(lax.rem(iota(part, 0), local_experts), dp_me, paired)
    for j in range(copies):
        mixed = mixed + got_ref[j, :group, :share].astype(jnp.float32)
        tail = got_ref[j, :group, share:]
        sums = sums + tail[:, : 2 * copies].astype(jnp.float32)
        to_expert = (iota(part, 1) == j * local_experts + order).astype(jnp.bfloat16)
        given = given + jnp.dot(
            tail[:, 2 * copies : own_end - share], to_expert, preferred_element_type=jnp.float32
        )
    mixture = sums[:, :copies] + sums[:, copies:]
    choose = (iota((tokens, group), 1) == lax.rem(iota((tokens, group), 0), group)).astype(jnp.float32)
    wide = jnp.dot(choose, mixture, precision=HIGH, preferred_element_type=jnp.float32)
    own_group = lax.div(iota((tokens, copies), 0), group) == iota((tokens, copies), 1)
    all_mixture = jnp.sum(jnp.where(own_group, wide, 0.0), axis=1, keepdims=True)
    my_mixture = jnp.sum(
        jnp.where(iota((group, copies), 1) == me, mixture, 0.0), axis=1, keepdims=True
    )
    slope = slope_ref[...]
    my_slope = slope_ref[pl.ds(pl.multiple_of(me * group, group), group), :]
    my_grad = (my_slope * (route_scale * given - my_mixture)).astype(jnp.bfloat16)
    routed = jnp.dot(my_grad, weight_ref[...], preferred_element_type=jnp.float32)
    input_ref[0] = (mixed + routed).astype(jnp.bfloat16)
    store = pltpu.make_async_copy(input_ref, input_far, sems.at[0])
    store.start()
    part = (LANES, expert_total)
    order = place_of(iota(part, 0), dp_me, paired)
    to_expert = (
        (iota(part, 1) == me * local_experts + order) & (iota(part, 0) < local_experts)
    ).astype(jnp.float32)
    mine = jnp.dot(own_ref[...], to_expert, precision=HIGH, preferred_element_type=jnp.float32)
    grads = (slope * (route_scale * mine - all_mixture)).astype(jnp.bfloat16)
    pick = (
        iota((8, expert_total), 1) == me * local_experts + iota((8, expert_total), 0)
    ).astype(jnp.bfloat16)
    lines = lax.dot_general(pick, grads, ROWS_ROWS, preferred_element_type=jnp.float32)
    row, token = iota((tokens, tokens), 1), iota((tokens, tokens), 0)
    own_tokens = group // dp_count
    within = lax.rem(row, group)
    source = lax.div(row, group) * group + (
        place_of(lax.div(within, own_tokens), dp_me, paired) * own_tokens
    ) + lax.rem(within, own_tokens)
    lines = jnp.dot(
        lines.astype(jnp.bfloat16),
        (token == source).astype(jnp.bfloat16),
        preferred_element_type=jnp.float32,
    ).astype(jnp.bfloat16)
    inputs = jnp.concatenate(
        [got_ref[j, group:, :share].astype(jnp.float32) for j in range(copies)], axis=0
    ).astype(jnp.bfloat16)
    router_ref[...] = jnp.dot(lines, inputs, preferred_element_type=jnp.float32)[:local_experts]
    last = pltpu.make_async_copy(router_ref, router_far, sems.at[1])
    last.start()
    store.wait()
    last.wait()


def local(
    grad_output,
    router_logits,
    expert_ids,
    router_input,
    router_weight,
    gate_weight,
    up_weight,
    down_weight,
    gate_saved,
    up_saved,
):
    expert_count, dp_count = lax.axis_size("expert"), lax.axis_size("dp")
    _, group, share = grad_output.shape
    expert_total = router_logits.shape[2]
    top = expert_ids.shape[2]
    local_experts, slots, hidden_size = gate_saved.shape
    depth = slots // expert_count
    rows = local_experts * slots
    piece = rows // dp_count
    tokens = expert_count * group
    aux = -(-(3 * expert_total + top) // LANES) * LANES
    bf16, f32 = jnp.bfloat16, jnp.float32
    paired = dp_count == local_experts and dp_count & (dp_count - 1) == 0
    sizes = (group, expert_total, top, depth)
    swaps = [[(j, j ^ k) for j in range(dp_count)] for k in range(dp_count)]

    packed = call(
        functools.partial(pack_kernel, expert_total),
        ((expert_count, group, aux + share), bf16),
        (router_logits, expert_ids, grad_output),
        scratch=(
            VMEM(router_logits.shape, f32),
            VMEM(expert_ids.shape, jnp.int32),
            VMEM(grad_output.shape, bf16),
            pltpu.SemaphoreType.DMA((3,)),
        ),
        flops=4 * 10**10,
        far_args=True,
    )
    gathered = lax.all_to_all(packed, "expert", 0, 0, tiled=True).reshape(tokens, aux + share)
    sends = call(
        functools.partial(down_kernel, sizes, aux, paired),
        (((slots, hidden_size), bf16),) * local_experts,
        (gathered, down_weight.swapaxes(1, 2)),
    )
    if paired:
        parts = [sends[0]]
        for k in range(1, dp_count):
            parts.append(lax.ppermute(sends[k], "dp", swaps[k]))
    else:
        stacked = jnp.concatenate(sends, axis=0).reshape(dp_count, piece, hidden_size)
        parts = list(lax.all_to_all(stacked, "dp", 0, 0, tiled=True))
    own_tokens = router_input.shape[1]
    if paired:
        piece_shapes = (((own_tokens, share), bf16),) * dp_count
    else:
        piece_shapes = (((dp_count, own_tokens, share), bf16),)
    full, slope, *pieces = call(
        functools.partial(table_kernel, sizes, local_experts, paired),
        (((tokens, rows), f32), ((tokens, expert_total), f32), *piece_shapes),
        (gathered[:, :aux], router_input),
    )
    if paired:
        for k in range(1, dp_count):
            pieces[k] = lax.ppermute(pieces[k], "dp", swaps[k])
    else:
        pieces = [lax.all_to_all(pieces[0], "dp", 0, 0, tiled=True)]

    hidden = sum(part.astype(f32) for part in parts).astype(bf16)
    if paired:
        blocks = [hidden]
        for k in range(1, dp_count):
            blocks.append(lax.ppermute(hidden, "dp", swaps[k]))
    else:
        spread = lax.all_gather(hidden, "dp", axis=0, tiled=True)
        blocks = list(spread.reshape(local_experts, slots, hidden_size))

    weights = (gate_weight, up_weight, gate_saved, up_saved)
    lanes = -(-rows // LANES) * LANES
    done = []
    for k in range(local_experts - 1):
        done += call(
            functools.partial(input_kernel, k, paired),
            (((slots, share), f32), ((1, lanes), f32)),
            (*weights, blocks[k]),
        )
    extra = 2 * expert_count + 2 * local_experts
    width = -(-(share + extra) // LANES) * LANES
    mixed, own = call(
        functools.partial(mix_kernel, local_experts - 1, paired, len(pieces)),
        (((expert_count, 2 * group, width), bf16), ((tokens, LANES), f32)),
        (full, *weights, blocks[-1], *pieces, *done),
        scratch=(VMEM((rows, share), f32), VMEM((1, lanes), f32)),
    )
    got = lax.all_to_all(mixed, "expert", 0, 0, tiled=True)
    grad_input, grad_router = call(
        functools.partial(final_kernel, sizes, paired),
        (((1, group, share), bf16), ((local_experts, share), f32)),
        (got, own, slope, router_weight),
        scratch=(
            VMEM((1, group, share), bf16),
            VMEM((local_experts, share), f32),
            pltpu.SemaphoreType.DMA((2,)),
        ),
        far_outs=True,
    )
    return grad_input, grad_router


def solution(mesh):
    placed = (
        P("expert", None, "dp"),
        P("expert", None, None),
        P("expert", None, None),
        P("expert", "dp", None),
        P(None, "dp"),
        P("expert", "dp", None),
        P("expert", "dp", None),
        P("expert", None, "dp"),
        P("expert", None, None),
        P("expert", None, None),
    )

    return jax.shard_map(
        local,
        mesh=mesh,
        in_specs=placed,
        out_specs=(P("expert", None, "dp"), P("expert", "dp")),
        check_vma=False,
    )
```

time: 148 us -> 50.7 us (0.34)
  waiting for transfers between devices: 84.4 us -> 5.7 us
  blocking collectives: 0 us -> 20.2 us
  matrix products: 19.4 us -> 0 us
  between operations: 14.9 us -> 0.76 us
  Pallas kernels: 0 us -> 10.3 us
  local copies, waits for them, and re-layouts: 7.53 us -> 0.04 us
  starting transfers between devices: 17.8 us -> 13.3 us
  other arithmetic: 3.35 us -> 0.03 us
    unnamed x3 -> x0, waiting for transfers between devices: 42.6 us -> none
    psum x1 -> x0, waiting for transfers between devices: 36.3 us -> none  [local(): hidden_grad = lax.psum(partial_hidden.reshape(row_total, hidden_size), 'dp')]
    all_to_all x0 -> x2, blocking collectives: none -> 20.2 us  [the longest x1 10.9 us: local(): lax.all_to_all(packed, 'expert', 0, 0, tiled=True)]
    dot_general x8 -> x0, matrix products: 19.4 us -> none  [the longest x1 5.39 us: local(): jnp.einsum('esf,edf->esd', grad_up, up_weight, preferred_element_type=jnp...]
    all_to_all x4 -> x0, starting transfers between devices: 17.8 us -> none  [the longest x1 5.2 us: local(): lax.all_to_all(outgoing.reshape(expert_total, slot_depth, feature_share),...]
    ppermute x0 -> x9, starting transfers between devices: none -> 13.3 us  [the longest x3 4.45 us: local(): blocks.append(lax.ppermute(hidden, 'dp', swaps[k]))]
    pallas_call x0 -> x8, Pallas kernels: none -> 10.3 us  [call(): pl.pallas_call(kernel, out_shape=tuple((space(*out) for out in outs)) if...]
    ppermute x0 -> x9, waiting for transfers between devices: none -> 5.7 us  [the longest x3 5.66 us: local(): parts.append(lax.ppermute(sends[k], 'dp', swaps[k]))]
  transfers between devices with their start and end apart: 6 -> 9, of which waited for: 3 -> 2; matrix products, arithmetic and copies ran while one was open for 13% -> 0% of each run, Pallas kernels for 0% -> 8%
where the time goes in v2:
time: 50.7 us; the launch traced here: 50.4 us
  blocking collectives  20.2 us (40%)
  starting transfers between devices  13.3 us (26%)
  Pallas kernels  10.3 us (20%)
  waiting for transfers between devices  5.7 us (11%)
  between operations  0.76 us (1%)
    all_to_all x1, blocking collectives, local(): lax.all_to_all(packed, 'expert', 0, 0, tiled=True)  10.9 us
    pallas_call x8, Pallas kernels, call(): pl.pallas_call(kernel, out_shape=tuple((space(*out) for out in outs)) if...  10.3 us
    all_to_all x1, blocking collectives, local(): got = lax.all_to_all(mixed, 'expert', 0, 0, tiled=True)  9.32 us
    ppermute x3, waiting for transfers between devices, local(): parts.append(lax.ppermute(sends[k], 'dp', swaps[k]))  5.66 us
    ppermute x3, starting transfers between devices, local(): blocks.append(lax.ppermute(hidden, 'dp', swaps[k]))  4.45 us
    ppermute x3, starting transfers between devices, local(): pieces[k] = lax.ppermute(pieces[k], 'dp', swaps[k])  4.45 us
    ppermute x3, starting transfers between devices, local(): parts.append(lax.ppermute(sends[k], 'dp', swaps[k]))  4.4 us
  transfers between devices with their start and end apart: 9, of which 2 were waited for; matrix products, arithmetic and copies ran while one was open for 0% of the time, Pallas kernels for 8%

profile of v2, /device:TPU:0, one launch (start us, length us, event | category | flops | bytes accessed | tf_op | source)
XLA Modules:
  0.0 50.4 jit_solution(13617585816221125666)
XLA Ops:
  0.7 1.0 %shard_map.113 = bf16[8,8,1088]{2,1,0:T(8,128)(2,1)S(1)} custom-call(f32[1,8,32]{2,1,0:T(8,128)} %logits_far.1, s32[1,8,8]{2,1,0:T(8,128)} %ids_far.1, bf16[1,8,960]{2,1,0:T(8,128)(2,1)} %rows_far.1), custom_call_target="tpu_custom_call" | custom-call | flops 40000000000 | tf_op jit(solution)/shard_map/pallas_call | solution.py:31
  1.7 0.0 copy-start.6
  1.7 0.0 copy-start.4
  1.7 10.9 %all_to_all.10 = bf16[8,8,1088]{2,1,0:T(8,128)(2,1)S(1)} all-to-all(bf16[8,8,1088]{2,1,0:T(8,128)(2,1)S(1)} %shard_map.113), channel_id=1, replica_groups=mesh['dp'=4,'expert'=8] {'expert'}, dimensions={0} | all-to-all | bytes 278528 | tf_op jit(solution)/shard_map/all_to_all | solution.py:355
  12.7 2.2 %shard_map.115 = (bf16[24,1024]{1,0:T(8,128)(2,1)S(1)}, bf16[24,1024]{1,0:T(8,128)(2,1)S(1)}, bf16[24,1024]{1,0:T(8,128)(2,1)S(1)}, bf16[24,1024]{1,0:T(8,128)(2,1)S(1)}) custom-call(bf16[64,1088]{1,0:T(8,128)(2,1)S(1)} %bitcast.3, bf16[4,960,1024]{2,1,0:T(8,128)(2,1)S(1)} %bitcast.2), custom_call_target="tpu_custom_call" | custom-call | tf_op jit(solution)/shard_map/pallas_call | solution.py:31
  14.9 1.6 %collective-permute-start = (bf16[24,1024]{1,0:T(8,128)(2,1)S(1)}, bf16[24,1024]{1,0:T(8,128)(2,1)S(1)}, u32[]{:S(2)}, u32[]{:S(2)}) collective-permute-start(bf16[24,1024]{1,0:T(8,128)(2,1)S(1)} %get-tuple-element.22), channel_id=1, source_target_pairs={{0,8},{8,0},{16,24},{24,16},{1,9},{9,1},{17,25},{25,17},{2,10},{10... | collective-permute-start | bytes 147464 | tf_op jit(solution)/shard_map/ppermute | solution.py:364
  16.5 2.6 %collective-permute-start.1 = (bf16[24,1024]{1,0:T(8,128)(2,1)S(1)}, bf16[24,1024]{1,0:T(8,128)(2,1)S(1)}, u32[]{:S(2)}, u32[]{:S(2)}) collective-permute-start(bf16[24,1024]{1,0:T(8,128)(2,1)S(1)} %get-tuple-element.23), channel_id=1, source_target_pairs={{0,16},{8,24},{16,0},{24,8},{1,17},{9,25},{17,1},{25,9},{2,18},{10... | collective-permute-start | bytes 147464 | tf_op jit(solution)/shard_map/ppermute | solution.py:364
  19.1 0.2 collective-permute-start.2
  19.3 2.8 %collective-permute-done.1 = bf16[24,1024]{1,0:T(8,128)(2,1)S(1)} collective-permute-done((bf16[24,1024]{1,0:T(8,128)(2,1)S(1)}, bf16[24,1024]{1,0:T(8,128)(2,1)S(1)}, u32[]{:S(2)}, u32[]{:S(2)}) %collective-permute-start.1) | collective-permute-done | bytes 49184 | tf_op jit(solution)/shard_map/ppermute | solution.py:364
  22.1 2.8 %collective-permute-done.2 = bf16[24,1024]{1,0:T(8,128)(2,1)S(1)} collective-permute-done((bf16[24,1024]{1,0:T(8,128)(2,1)S(1)}, bf16[24,1024]{1,0:T(8,128)(2,1)S(1)}, u32[]{:S(2)}, u32[]{:S(2)}) %collective-permute-start.2) | collective-permute-done | bytes 49184 | tf_op jit(solution)/shard_map/ppermute | solution.py:364
  25.0 0.1 collective-permute-start.8
  25.1 1.1 %collective-permute-start.7 = (bf16[24,1024]{1,0:T(8,128)(2,1)S(1)}, bf16[24,1024]{1,0:T(8,128)(2,1)S(1)}, u32[]{:S(2)}, u32[]{:S(2)}) collective-permute-start(bf16[24,1024]{1,0:T(8,128)(2,1)S(1)} %add_convert_fusion.refs_4_), channel_id=1, source_target_pairs={{0,8},{8,0},{16,24},{24,16},{1,9},{9,1},{17,25},{25,17},{2,10},{10... | collective-permute-start | bytes 147464 | tf_op jit(solution)/shard_map/ppermute | solution.py:388
  26.3 3.2 %collective-permute-start.3 = (bf16[24,1024]{1,0:T(8,128)(2,1)S(1)}, bf16[24,1024]{1,0:T(8,128)(2,1)S(1)}, u32[]{:S(2)}, u32[]{:S(2)}) collective-permute-start(bf16[24,1024]{1,0:T(8,128)(2,1)S(1)} %add_convert_fusion.refs_4_), channel_id=1, source_target_pairs={{0,24},{8,16},{16,8},{24,0},{1,25},{9,17},{17,9},{25,1},{2,26},{10... | collective-permute-start | bytes 147464 | tf_op jit(solution)/shard_map/ppermute | solution.py:388
  29.5 0.5 shard_map.114
  29.9 0.1 collective-permute-start.4
  30.0 1.2 %collective-permute-start.5 = (bf16[2,960]{1,0:T(2,128)(2,1)S(1)}, bf16[2,960]{1,0:T(2,128)(2,1)S(1)}, u32[]{:S(2)}, u32[]{:S(2)}) collective-permute-start(bf16[2,960]{1,0:T(2,128)(2,1)S(1)} %get-tuple-element.27), channel_id=1, source_target_pairs={{0,16},{8,24},{16,0},{24,8},{1,17},{9,25},{17,1},{25,9},{2,18},{10... | collective-permute-start | bytes 11528 | tf_op jit(solution)/shard_map/ppermute | solution.py:380
  31.2 3.2 %collective-permute-start.6 = (bf16[2,960]{1,0:T(2,128)(2,1)S(1)}, bf16[2,960]{1,0:T(2,128)(2,1)S(1)}, u32[]{:S(2)}, u32[]{:S(2)}) collective-permute-start(bf16[2,960]{1,0:T(2,128)(2,1)S(1)} %get-tuple-element.28), channel_id=1, source_target_pairs={{0,24},{8,16},{16,8},{24,0},{1,25},{9,17},{17,9},{25,1},{2,26},{10... | collective-permute-start | bytes 11528 | tf_op jit(solution)/shard_map/ppermute | solution.py:380
  34.4 1.2 %shard_map.116 = (f32[24,960]{1,0:T(8,128)S(1)}, f32[1,128]{1,0:T(1,128)S(1)}) custom-call(bf16[4,960,1024]{2,1,0:T(8,128)(2,1)S(1)} %copy-done, bf16[4,960,1024]{2,1,0:T(8,128)(2,1)S(1)} %copy-done.1, bf16[4,24,1024]{2,1,0:T(8,128)(2,1)S(1)} %copy-done.3, bf16[4,24,1024]{2,1,0:T(8,128)(2,1)S(1)} %copy-done.4, bf16[24,1024]{1,0:T(8,128)(2,1)S(1)} %add_convert_fusion.refs_4_), custom_call_target="tpu_custom_call" | custom-call | tf_op jit(solution)/shard_map/pallas_call | solution.py:31
  35.6 1.2 %shard_map.118 = (f32[24,960]{1,0:T(8,128)S(1)}, f32[1,128]{1,0:T(1,128)S(1)}) custom-call(bf16[4,960,1024]{2,1,0:T(8,128)(2,1)S(1)} %copy-done, bf16[4,960,1024]{2,1,0:T(8,128)(2,1)S(1)} %copy-done.1, bf16[4,24,1024]{2,1,0:T(8,128)(2,1)S(1)} %copy-done.3, bf16[4,24,1024]{2,1,0:T(8,128)(2,1)S(1)} %copy-done.4, ...), custom_call_target="tpu_custom_call" | custom-call | tf_op jit(solution)/shard_map/pallas_call | solution.py:31
  36.8 1.2 %shard_map.117 = (f32[24,960]{1,0:T(8,128)S(1)}, f32[1,128]{1,0:T(1,128)S(1)}) custom-call(bf16[4,960,1024]{2,1,0:T(8,128)(2,1)S(1)} %copy-done, bf16[4,960,1024]{2,1,0:T(8,128)(2,1)S(1)} %copy-done.1, bf16[4,24,1024]{2,1,0:T(8,128)(2,1)S(1)} %copy-done.3, bf16[4,24,1024]{2,1,0:T(8,128)(2,1)S(1)} %copy-done.4, ...), custom_call_target="tpu_custom_call" | custom-call | tf_op jit(solution)/shard_map/pallas_call | solution.py:31
  38.1 0.0 collective-permute-done.5.refs_7_
  38.1 1.5 %shard_map.119 = (bf16[8,16,1024]{2,1,0:T(8,128)(2,1)S(1)}, f32[64,128]{1,0:T(8,128)S(1)}) custom-call(f32[64,96]{1,0:T(8,128)S(1)} %get-tuple-element.20.full_ref, bf16[4,960,1024]{2,1,0:T(8,128)(2,1)S(1)} %copy-done, bf16[4,960,1024]{2,1,0:T(8,128)(2,1)S(1)} %copy-done.1, bf16[4,24,1024]{2,1,0:T(8,128)(2,1)S(1)} %copy-done.3, ...), custom_call_target="tpu_custom_call" | custom-call | tf_op jit(solution)/shard_map/pallas_call | solution.py:31
  39.7 9.3 %all_to_all.11.got_ref = bf16[8,16,1024]{2,1,0:T(8,128)(2,1)S(1)} all-to-all(bf16[8,16,1024]{2,1,0:T(8,128)(2,1)S(1)} %get-tuple-element.35), channel_id=1, replica_groups=mesh['dp'=4,'expert'=8] {'expert'}, dimensions={0} | all-to-all | bytes 524288 | tf_op jit(solution)/shard_map/all_to_all | solution.py:410
  49.0 1.4 %shard_map.120 = (bf16[1,8,960]{2,1,0:T(8,128)(2,1)}, f32[4,960]{1,0:T(4,128)}) custom-call(bf16[8,16,1024]{2,1,0:T(8,128)(2,1)S(1)} %all_to_all.11.got_ref, f32[64,128]{1,0:T(8,128)S(1)} %get-tuple-element.36.own_ref, f32[64,32]{1,0:T(8,128)S(1)} %get-tuple-element.37.slope_ref, bf16[32,960]{1,0:T(8,128)(2,1)S(1)} %copy-done.5), custom_call_target="tpu_custom_call" | custom-call | tf_op jit(solution)/shard_map/pallas_call | solution.py:31
  (20 shorter events, 0.1 us)
Async XLA Ops:
  0.6 12.0 %copy-start.2 = (bf16[4,1024,960]{1,2,0:T(8,128)(2,1)S(1)}, bf16[4,1024,960]{1,2,0:T(8,128)(2,1)}, u32[]{:S(2)}) copy-start(bf16[4,1024,960]{1,2,0:T(8,128)(2,1)} %param.17) | copy-start | bytes 23592964
  0.6 33.8 %copy-start.1 = (bf16[4,960,1024]{2,1,0:T(8,128)(2,1)S(1)}, bf16[4,960,1024]{2,1,0:T(8,128)(2,1)}, u32[]{:S(2)}) copy-start(bf16[4,960,1024]{2,1,0:T(8,128)(2,1)} %refs_1_.7) | copy-start | bytes 23592964
  1.7 27.8 %copy-start.6 = (bf16[1,2,3840]{2,1,0:T(2,128)(2,1)S(1)}, bf16[1,2,3840]{2,1,0:T(2,128)(2,1)}, u32[]{:S(2)}) copy-start(bf16[1,2,3840]{2,1,0:T(2,128)(2,1)} %inputs_ref.1) | copy-start | bytes 46084
  1.7 32.7 %copy-start = (bf16[4,960,1024]{2,1,0:T(8,128)(2,1)S(1)}, bf16[4,960,1024]{2,1,0:T(8,128)(2,1)}, u32[]{:S(2)}) copy-start(bf16[4,960,1024]{2,1,0:T(8,128)(2,1)} %refs_0_.7) | copy-start | bytes 23592964
  1.7 32.7 %copy-start.3 = (bf16[4,24,1024]{2,1,0:T(8,128)(2,1)S(1)}, bf16[4,24,1024]{2,1,0:T(8,128)(2,1)}, u32[]{:S(2)}) copy-start(bf16[4,24,1024]{2,1,0:T(8,128)(2,1)} %refs_2_.7) | copy-start | bytes 589828
  1.7 32.7 %copy-start.4 = (bf16[4,24,1024]{2,1,0:T(8,128)(2,1)S(1)}, bf16[4,24,1024]{2,1,0:T(8,128)(2,1)}, u32[]{:S(2)}) copy-start(bf16[4,24,1024]{2,1,0:T(8,128)(2,1)} %refs_3_.7) | copy-start | bytes 589828
  14.9 4.4 %collective-permute-start = (bf16[24,1024]{1,0:T(8,128)(2,1)S(1)}, bf16[24,1024]{1,0:T(8,128)(2,1)S(1)}, u32[]{:S(2)}, u32[]{:S(2)}) collective-permute-start(bf16[24,1024]{1,0:T(8,128)(2,1)S(1)} %get-tuple-element.22), channel_id=1, source_target_pairs={{0,8},{8,0},{16,24},{24,16},{1,9},{9,1},{17,25},{25,17},{2,10},{10... | collective-permute-start | bytes 147464 | tf_op jit(solution)/shard_map/ppermute | solution.py:364
  16.5 5.6 %collective-permute-start.1 = (bf16[24,1024]{1,0:T(8,128)(2,1)S(1)}, bf16[24,1024]{1,0:T(8,128)(2,1)S(1)}, u32[]{:S(2)}, u32[]{:S(2)}) collective-permute-start(bf16[24,1024]{1,0:T(8,128)(2,1)S(1)} %get-tuple-element.23), channel_id=1, source_target_pairs={{0,16},{8,24},{16,0},{24,8},{1,17},{9,25},{17,1},{25,9},{2,18},{10... | collective-permute-start | bytes 147464 | tf_op jit(solution)/shard_map/ppermute | solution.py:364
  19.1 5.9 %collective-permute-start.2 = (bf16[24,1024]{1,0:T(8,128)(2,1)S(1)}, bf16[24,1024]{1,0:T(8,128)(2,1)S(1)}, u32[]{:S(2)}, u32[]{:S(2)}) collective-permute-start(bf16[24,1024]{1,0:T(8,128)(2,1)S(1)} %get-tuple-element.24), channel_id=1, source_target_pairs={{0,24},{8,16},{16,8},{24,0},{1,25},{9,17},{17,9},{25,1},{2,26},{10... | collective-permute-start | bytes 147464 | tf_op jit(solution)/shard_map/ppermute | solution.py:364
  25.0 6.2 %collective-permute-start.8 = (bf16[24,1024]{1,0:T(8,128)(2,1)S(1)}, bf16[24,1024]{1,0:T(8,128)(2,1)S(1)}, u32[]{:S(2)}, u32[]{:S(2)}) collective-permute-start(bf16[24,1024]{1,0:T(8,128)(2,1)S(1)} %add_convert_fusion.refs_4_), channel_id=1, source_target_pairs={{0,16},{8,24},{16,0},{24,8},{1,17},{9,25},{17,1},{25,9},{2,18},{10... | collective-permute-start | bytes 147464 | tf_op jit(solution)/shard_map/ppermute | solution.py:388
  25.1 11.7 %collective-permute-start.7 = (bf16[24,1024]{1,0:T(8,128)(2,1)S(1)}, bf16[24,1024]{1,0:T(8,128)(2,1)S(1)}, u32[]{:S(2)}, u32[]{:S(2)}) collective-permute-start(bf16[24,1024]{1,0:T(8,128)(2,1)S(1)} %add_convert_fusion.refs_4_), channel_id=1, source_target_pairs={{0,8},{8,0},{16,24},{24,16},{1,9},{9,1},{17,25},{25,17},{2,10},{10... | collective-permute-start | bytes 147464 | tf_op jit(solution)/shard_map/ppermute | solution.py:388
  26.3 11.9 %collective-permute-start.3 = (bf16[24,1024]{1,0:T(8,128)(2,1)S(1)}, bf16[24,1024]{1,0:T(8,128)(2,1)S(1)}, u32[]{:S(2)}, u32[]{:S(2)}) collective-permute-start(bf16[24,1024]{1,0:T(8,128)(2,1)S(1)} %add_convert_fusion.refs_4_), channel_id=1, source_target_pairs={{0,24},{8,16},{16,8},{24,0},{1,25},{9,17},{17,9},{25,1},{2,26},{10... | collective-permute-start | bytes 147464 | tf_op jit(solution)/shard_map/ppermute | solution.py:388
  29.9 8.1 %collective-permute-start.4 = (bf16[2,960]{1,0:T(2,128)(2,1)S(1)}, bf16[2,960]{1,0:T(2,128)(2,1)S(1)}, u32[]{:S(2)}, u32[]{:S(2)}) collective-permute-start(bf16[2,960]{1,0:T(2,128)(2,1)S(1)} %get-tuple-element.26), channel_id=1, source_target_pairs={{0,8},{8,0},{16,24},{24,16},{1,9},{9,1},{17,25},{25,17},{2,10},{10... | collective-permute-start | bytes 11528 | tf_op jit(solution)/shard_map/ppermute | solution.py:380
  30.0 8.1 %collective-permute-start.5 = (bf16[2,960]{1,0:T(2,128)(2,1)S(1)}, bf16[2,960]{1,0:T(2,128)(2,1)S(1)}, u32[]{:S(2)}, u32[]{:S(2)}) collective-permute-start(bf16[2,960]{1,0:T(2,128)(2,1)S(1)} %get-tuple-element.27), channel_id=1, source_target_pairs={{0,16},{8,24},{16,0},{24,8},{1,17},{9,25},{17,1},{25,9},{2,18},{10... | collective-permute-start | bytes 11528 | tf_op jit(solution)/shard_map/ppermute | solution.py:380
  31.2 6.9 %collective-permute-start.6 = (bf16[2,960]{1,0:T(2,128)(2,1)S(1)}, bf16[2,960]{1,0:T(2,128)(2,1)S(1)}, u32[]{:S(2)}, u32[]{:S(2)}) collective-permute-start(bf16[2,960]{1,0:T(2,128)(2,1)S(1)} %get-tuple-element.28), channel_id=1, source_target_pairs={{0,24},{8,16},{16,8},{24,0},{1,25},{9,17},{17,9},{25,1},{2,26},{10... | collective-permute-start | bytes 11528 | tf_op jit(solution)/shard_map/ppermute | solution.py:380
  38.1 10.9 %copy-start.5 = (bf16[32,960]{1,0:T(8,128)(2,1)S(1)}, bf16[32,960]{1,0:T(8,128)(2,1)}, u32[]{:S(2)}) copy-start(bf16[32,960]{1,0:T(8,128)(2,1)} %weight_ref.1) | copy-start | bytes 184324

commit v3 on v2

v3 whole, which is shorter than its diff:
```python
import functools

import jax
import jax.numpy as jnp
from jax import lax
from jax.experimental import pallas as pl
from jax.experimental.pallas import tpu as pltpu
from jax.sharding import PartitionSpec as P

route_scale = 2.5
LANES = 128
HIGH = lax.Precision.HIGHEST
VMEM = pltpu.VMEM
ROWS_ROWS = (((1,), (1,)), ((), ()))


def iota(shape, dim):
    return lax.broadcasted_iota(jnp.int32, shape, dim)


def place_of(block, me, paired):
    return lax.bitwise_xor(block, me) if paired else block


def call(kernel, outs, args, scratch=(), flops=0, far_args=False, far_outs=False):
    far, near = pl.BlockSpec(memory_space=pltpu.HBM), pl.BlockSpec(memory_space=VMEM)
    several = isinstance(outs[0][0], tuple)
    space = pltpu.HBM if far_outs else VMEM
    out_spec = far if far_outs else near
    arg_space = pltpu.HBM if far_args else VMEM
    return pl.pallas_call(
        kernel,
        out_shape=tuple(space(*out) for out in outs) if several else space(*outs),
        in_specs=[far if far_args else near] * len(args),
        out_specs=(out_spec,) * len(outs) if several else out_spec,
        scratch_shapes=list(scratch),
        compiler_params=pltpu.CompilerParams(vmem_limit_bytes=12 << 20),
        cost_estimate=pl.CostEstimate(flops=flops, bytes_accessed=0, transcendentals=0),
    )(*[pltpu.with_memory_space_constraint(arg, arg_space) for arg in args])


def group_of(block, count, cubed):
    if not cubed:
        return block
    doubled = 2 * block
    return lax.bitwise_xor(
        lax.rem(doubled, count) + lax.div(doubled, count), lax.axis_index("expert")
    )


def stacked(refs, columns):
    if len(refs) == 1:
        return refs[0][:, columns]
    parts = [ref[:, columns].astype(jnp.float32) for ref in refs]
    return jnp.concatenate(parts, axis=0).astype(refs[0].dtype)


def split(values):
    upper = values.astype(jnp.bfloat16)
    return upper, (values - upper.astype(jnp.float32)).astype(jnp.bfloat16)


def pack_kernel(expert_total, *refs):
    far, out_ref, held, sems = refs[:3], refs[3], refs[4:7], refs[7]
    fetches = [pltpu.make_async_copy(*pair, sems.at[n]) for n, pair in enumerate(zip(far, held))]
    for fetch in fetches:
        fetch.start()
    for fetch in fetches:
        fetch.wait()
    logits_ref, ids_ref, rows_ref = held
    group, width = out_ref.shape
    top = ids_ref.shape[2]
    aux = width - rows_ref.shape[2]
    logits = logits_ref[0]
    first = logits.astype(jnp.bfloat16).astype(jnp.float32)
    rest = logits - first
    second = rest.astype(jnp.bfloat16).astype(jnp.float32)
    pieces = [first, second, rest - second, ids_ref[0].astype(jnp.float32)]
    spare = aux - 3 * expert_total - top
    if spare:
        pieces.append(jnp.zeros((group, spare), jnp.float32))
    out_ref[:, :aux] = jnp.concatenate(pieces, axis=1).astype(jnp.bfloat16)
    out_ref[:, aux:] = rows_ref[0]


def routing(head, sizes, cubed):
    group, expert_total, top, depth = sizes
    tokens = head.shape[0]
    lane = iota((tokens, expert_total), 1)
    named = jnp.zeros((tokens, expert_total), jnp.float32)
    for k in range(top):
        at = 3 * expert_total + k
        named = named + (head[:, at : at + 1].astype(jnp.int32) == lane).astype(jnp.float32)
    row_at, col_at = iota((tokens, tokens), 0), iota((tokens, tokens), 1)
    earlier = (lax.div(row_at, group) == lax.div(col_at, group)) & (col_at < row_at)
    rank = jnp.dot(
        earlier.astype(jnp.bfloat16), named.astype(jnp.bfloat16), preferred_element_type=jnp.float32
    )
    block = lax.div(iota((tokens, expert_total), 0), group)
    first_slot = (group_of(block, tokens // group, cubed) * depth).astype(jnp.float32)
    return named, jnp.where(named > 0.5, first_slot + rank, -1.0)


def down_kernel(sizes, aux, paired, cubed, token_count, *refs):
    token_refs, weight_ref, send_refs = refs[:token_count], refs[token_count], refs[token_count + 1 :]
    expert_total = sizes[1]
    local_experts, share, _ = weight_ref.shape
    slots = send_refs[0].shape[0]
    me = lax.axis_index("dp")
    base = lax.axis_index("expert") * local_experts
    features = stacked(token_refs, slice(aux, aux + share))
    tokens = features.shape[0]
    early = tokens <= 256
    _, slot = routing(stacked(token_refs, slice(0, aux)).astype(jnp.float32), sizes, cubed)
    order = place_of(iota((8, expert_total), 0), me, paired)
    pick = (iota((8, expert_total), 1) == base + order).astype(jnp.bfloat16)
    slot_rows = lax.dot_general(
        pick, slot.astype(jnp.bfloat16), ROWS_ROWS, preferred_element_type=jnp.float32
    )
    slot_at = iota((slots, tokens), 0).astype(jnp.float32)
    for k, send_ref in enumerate(send_refs):
        chosen = (slot_at == slot_rows[k : k + 1, :]).astype(jnp.bfloat16)
        weight = weight_ref[place_of(k, me, paired)]
        if early:
            product = jnp.dot(features, weight, preferred_element_type=jnp.float32)
            value = jnp.dot(chosen, product.astype(jnp.bfloat16), preferred_element_type=jnp.float32)
        else:
            sent = jnp.dot(chosen, features, preferred_element_type=jnp.float32).astype(jnp.bfloat16)
            value = jnp.dot(sent, weight, preferred_element_type=jnp.float32)
        send_ref[...] = value.astype(jnp.bfloat16)


def table_kernel(sizes, aux, local_experts, paired, cubed, token_count, input_count, *refs):
    token_refs, refs = refs[:token_count], refs[token_count:]
    input_refs, (full_ref, slope_ref, *piece_refs) = refs[:input_count], refs[input_count:]
    expert_total = sizes[1]
    tokens, rows = full_ref.shape
    slots = rows // local_experts
    me = lax.axis_index("dp")
    base = lax.axis_index("expert") * local_experts
    head = stacked(token_refs, slice(0, aux)).astype(jnp.float32)
    logits = (
        head[:, :expert_total]
        + head[:, expert_total : 2 * expert_total]
        + head[:, 2 * expert_total : 3 * expert_total]
    )
    named, slot = routing(head, sizes, cubed)
    scores = jax.nn.sigmoid(logits)
    total = jnp.sum(named * scores, axis=1, keepdims=True)
    gates = route_scale * (named * scores) / total
    slope_ref[...] = named * scores * (1.0 - scores) / total
    order = place_of(lax.div(iota((expert_total, rows), 1), slots), me, paired)
    spread = (iota((expert_total, rows), 0) == base + order).astype(jnp.float32)
    slot_wide = jnp.dot(slot, spread, precision=HIGH, preferred_element_type=jnp.float32)
    gates_wide = jnp.dot(gates, spread, precision=HIGH, preferred_element_type=jnp.float32)
    wanted = lax.rem(iota((tokens, rows), 1), slots).astype(jnp.float32)
    full_ref[...] = jnp.where(slot_wide == wanted, gates_wide, 0.0)
    dp_count = lax.axis_size("dp")
    raw = [ref[0] for ref in input_refs]
    share = raw[0].shape[1] // dp_count
    if not cubed:
        for d in range(dp_count):
            piece_refs[0][d] = raw[0][:, d * share : (d + 1) * share]
        return
    both = jnp.concatenate([value.astype(jnp.float32) for value in raw], axis=0)
    lines = [both[:, d * share : (d + 1) * share] for d in range(dp_count)]
    for k, piece_ref in enumerate(piece_refs):
        found = lines[0]
        for d in range(1, dp_count):
            found = jnp.where(place_of(k, me, paired) == d, lines[d], found)
        piece_ref[...] = found.astype(jnp.bfloat16)


def expert_parts(k, paired, gate_w_ref, up_w_ref, gate_ref, up_ref, block_ref, row_ref, share_ref):
    expert = place_of(k, lax.axis_index("dp"), paired)
    hidden_grad = block_ref[...].astype(jnp.float32)
    gate_value = gate_ref[expert].astype(jnp.float32)
    up_value = up_ref[expert].astype(jnp.float32)
    sig = jax.nn.sigmoid(gate_value)
    activated = gate_value * sig
    gate_part = (hidden_grad * up_value * sig * (1.0 + gate_value * (1.0 - sig))).astype(jnp.bfloat16)
    up_part = (hidden_grad * activated).astype(jnp.bfloat16)
    value = lax.dot_general(
        gate_part, gate_w_ref[expert], ROWS_ROWS, preferred_element_type=jnp.float32
    ) + lax.dot_general(up_part, up_w_ref[expert], ROWS_ROWS, preferred_element_type=jnp.float32)
    row_ref[...] = value
    hidden = (activated * up_value).astype(jnp.bfloat16).astype(jnp.float32)
    given = jnp.sum(hidden * hidden_grad, axis=1, keepdims=True)
    slots, width = hidden_grad.shape[0], share_ref.shape[1]
    across = iota((slots, width), 0) + k * slots == iota((slots, width), 1)
    share_ref[...] = jnp.sum(jnp.where(across, given, 0.0), axis=0, keepdims=True)


def input_kernel(k, paired, *refs):
    expert_parts(k, paired, *refs)


def mix_kernel(k, group, paired, cubed, full_ref, *refs):
    weights, rest = refs[:5], refs[5:]
    earlier, out_refs, (held_ref, share_ref) = rest[: 2 * k], rest[2 * k : -2], rest[-2:]
    slots = weights[4].shape[0]
    expert_parts(k, paired, *weights, held_ref.at[pl.ds(k * slots, slots)], share_ref)
    shares = share_ref[...]
    for at in range(k):
        held_ref[at * slots : (at + 1) * slots] = earlier[2 * at][...]
        shares = shares + earlier[2 * at + 1][...]
    full = full_ref[...]
    tokens, rows = full.shape
    local_experts = k + 1
    count = tokens // group
    share, width = held_ref.shape[1], out_refs[0].shape[2]
    given = shares[:, :rows]
    mixture = jnp.sum(full * given, axis=1, keepdims=True)
    held_lane = jnp.where(full != 0.0, given, 0.0)
    expert_at = lax.div(iota((tokens, rows), 1), slots)
    lane = iota((tokens, LANES), 1)
    own = jnp.zeros((tokens, LANES), jnp.float32)
    for e in range(local_experts):
        dg = jnp.sum(jnp.where(expert_at == e, held_lane, 0.0), axis=1, keepdims=True)
        own = own + jnp.where(lane == e, dg, 0.0)
    own_ref = out_refs[-1]
    own_ref[...] = own
    first_core = lax.rem(lax.axis_index("expert"), 2) == 0
    few = own[:, :local_experts]
    none = jnp.zeros_like(few)
    both = jnp.concatenate([jnp.where(first_core, few, none), jnp.where(first_core, none, few)], axis=1)
    row_group = group_of(lax.div(iota((tokens, count), 0), group), count, cubed)
    spread = jnp.where(row_group == iota((tokens, count), 1), mixture, 0.0)
    same = lax.rem(iota((tokens, tokens), 0), group) == lax.rem(iota((tokens, tokens), 1), group)
    same = same.astype(jnp.bfloat16)
    mix_high, mix_low = [
        jnp.dot(same, part, preferred_element_type=jnp.float32) for part in split(spread)
    ]
    own_high, own_low = [part.astype(jnp.float32) for part in split(both)]
    spare = jnp.zeros((tokens, width - share - 2 * count - 4 * local_experts), jnp.float32)
    extra = jnp.concatenate([mix_high, mix_low, own_high, own_low, spare], axis=1)
    values = held_ref[...].astype(jnp.bfloat16)
    high, low = split(full)
    mixed = jnp.dot(high, values, preferred_element_type=jnp.float32)
    mixed = mixed + jnp.dot(low, values, preferred_element_type=jnp.float32)
    at = 0
    for out_ref in out_refs[:-1]:
        for q in range(out_ref.shape[0]):
            lines = slice(at * group, (at + 1) * group)
            out_ref[q, :, :share] = mixed[lines].astype(out_ref.dtype)
            out_ref[q, :, share:] = extra[lines].astype(out_ref.dtype)
            at = at + 1


def pair_kernel(share, count, local_experts, near_ref, far_ref, *refs):
    piece_refs, out_refs = refs[: -near_ref.shape[0]], refs[-near_ref.shape[0] :]
    group, width = near_ref.shape[1:]
    own = group // len(piece_refs)
    pieces = [ref[...].astype(jnp.float32) for ref in piece_refs]
    routed = jnp.concatenate([p[:own] for p in pieces] + [p[own:] for p in pieces], axis=0)
    routed = routed.astype(jnp.bfloat16)
    ends = (0, count, 2 * count, 2 * count + 2 * local_experts, 2 * count + 4 * local_experts)
    for q, out_ref in enumerate(out_refs):
        total = near_ref[q] + far_ref[q].astype(jnp.float32)
        out_ref[:group, :share] = total[:, :share].astype(jnp.bfloat16)
        tail = total[:, share:]
        terms = [tail[:, i:j] for i, j in zip(ends, ends[1:])]
        sums = [terms[0] + terms[1], terms[2] + terms[3]]
        parts = [part.astype(jnp.float32) for value in sums for part in split(value)]
        parts.append(jnp.zeros((group, width - share - ends[-1]), jnp.float32))
        out_ref[:group, share:] = jnp.concatenate(parts, axis=1).astype(jnp.bfloat16)
        out_ref[group:, :share] = routed
        out_ref[group:, share:] = jnp.zeros((2 * group, width - share), jnp.bfloat16)


def final_kernel(sizes, paired, cubed, got_count, input_count, local_experts, *refs):
    got_refs, rest = refs[:got_count], refs[got_count:]
    input_refs, rest = rest[:input_count], rest[input_count:]
    own_ref, slope_ref, weight_ref, input_far, router_far, input_ref, router_ref, sems = rest
    group, expert_total, _, _ = sizes
    tokens = slope_ref.shape[0]
    count = tokens // group
    share = router_ref.shape[1]
    dp_count = lax.axis_size("dp")
    dp_me, me = lax.axis_index("dp"), lax.axis_index("expert")
    if cubed:
        sources = [(ref[:group], lax.bitwise_xor(me, 2 * b)) for b, ref in enumerate(got_refs)]
    else:
        sources = [(got_refs[0][j], j) for j in range(count)]
    mixed = jnp.zeros((group, share), jnp.float32)
    sums = jnp.zeros((group, 2 * count), jnp.float32)
    given = jnp.zeros((group, expert_total), jnp.float32)
    part = (4 * local_experts, expert_total)
    place = lax.rem(iota(part, 0), 2 * local_experts)
    order = place_of(lax.rem(place, local_experts), dp_me, paired)
    for got, source in sources:
        mixed = mixed + got[:, :share].astype(jnp.float32)
        sums = sums + got[:, share : share + 2 * count].astype(jnp.float32)
        first = (source - lax.rem(source, 2) + lax.div(place, local_experts)) * local_experts
        to_expert = (iota(part, 1) == first + order).astype(jnp.bfloat16)
        shares = got[:, share + 2 * count : share + 2 * count + 4 * local_experts]
        given = given + jnp.dot(shares, to_expert, preferred_element_type=jnp.float32)
    mixture = sums[:, :count] + sums[:, count:]
    choose = (iota((tokens, group), 1) == lax.rem(iota((tokens, group), 0), group)).astype(jnp.float32)
    wide = jnp.dot(choose, mixture, precision=HIGH, preferred_element_type=jnp.float32)
    row_group = group_of(lax.div(iota((tokens, count), 0), group), count, cubed)
    all_mixture = jnp.sum(
        jnp.where(row_group == iota((tokens, count), 1), wide, 0.0), axis=1, keepdims=True
    )
    my_mixture = jnp.sum(
        jnp.where(iota((group, count), 1) == me, mixture, 0.0), axis=1, keepdims=True
    )
    slope = slope_ref[...]
    if cubed:
        my_slope = slope[:group]
    else:
        my_slope = slope_ref[pl.ds(pl.multiple_of(me * group, group), group), :]
    my_grad = (my_slope * (route_scale * given - my_mixture)).astype(jnp.bfloat16)
    routed = jnp.dot(my_grad, weight_ref[...], preferred_element_type=jnp.float32)
    input_ref[0] = (mixed + routed).astype(jnp.bfloat16)
    store = pltpu.make_async_copy(input_ref, input_far, sems.at[0])
    store.start()
    part = (LANES, expert_total)
    order = place_of(iota(part, 0), dp_me, paired)
    to_expert = (
        (iota(part, 1) == me * local_experts + order) & (iota(part, 0) < local_experts)
    ).astype(jnp.float32)
    mine = jnp.dot(own_ref[...], to_expert, precision=HIGH, preferred_element_type=jnp.float32)
    grads = (slope * (route_scale * mine - all_mixture)).astype(jnp.bfloat16)
    pick = (
        iota((8, expert_total), 1) == me * local_experts + iota((8, expert_total), 0)
    ).astype(jnp.bfloat16)
    lines = lax.dot_general(pick, grads, ROWS_ROWS, preferred_element_type=jnp.float32)
    row, token = iota((tokens, tokens), 1), iota((tokens, tokens), 0)
    own_tokens = group // dp_count
    within = lax.rem(row, group)
    source = lax.div(row, group) * group + (
        place_of(lax.div(within, own_tokens), dp_me, paired) * own_tokens
    ) + lax.rem(within, own_tokens)
    lines = jnp.dot(
        lines.astype(jnp.bfloat16),
        (token == source).astype(jnp.bfloat16),
        preferred_element_type=jnp.float32,
    ).astype(jnp.bfloat16)
    if cubed:
        parts = [
            ref[half * group : (half + 1) * group, :share].astype(jnp.float32)
            for half in (1, 2)
            for ref in got_refs
        ]
        inputs = jnp.concatenate(parts, axis=0).astype(jnp.bfloat16)
    else:
        inputs = input_refs[0][...]
    router_ref[...] = jnp.dot(lines, inputs, preferred_element_type=jnp.float32)[:local_experts]
    last = pltpu.make_async_copy(router_ref, router_far, sems.at[1])
    last.start()
    store.wait()
    last.wait()


def local(
    grad_output,
    router_logits,
    expert_ids,
    router_input,
    router_weight,
    gate_weight,
    up_weight,
    down_weight,
    gate_saved,
    up_saved,
):
    expert_count, dp_count = lax.axis_size("expert"), lax.axis_size("dp")
    _, group, share = grad_output.shape
    expert_total = router_logits.shape[2]
    top = expert_ids.shape[2]
    local_experts, slots, hidden_size = gate_saved.shape
    depth = slots // expert_count
    rows = local_experts * slots
    piece = rows // dp_count
    tokens = expert_count * group
    aux = -(-(3 * expert_total + top) // LANES) * LANES
    bf16, f32 = jnp.bfloat16, jnp.float32
    paired = dp_count == local_experts and dp_count & (dp_count - 1) == 0
    cubed = paired and expert_count == 8
    sizes = (group, expert_total, top, depth)
    own_tokens = router_input.shape[1]

    def swap(value, axis, k):
        count = lax.axis_size(axis)
        return lax.ppermute(value, axis, [(j, j ^ k) for j in range(count)])

    def gather(value):
        if not cubed:
            return [lax.all_gather(value, "expert", axis=0, tiled=True)]
        parts = [value] + [swap(value, "expert", k) for k in (2, 4, 6)]
        joined = jnp.concatenate(parts, axis=0)
        return parts + [swap(joined, "expert", 1)]

    packed = call(
        functools.partial(pack_kernel, expert_total),
        ((group, aux + share), bf16),
        (router_logits, expert_ids, grad_output),
        scratch=(
            VMEM(router_logits.shape, f32),
            VMEM(expert_ids.shape, jnp.int32),
            VMEM(grad_output.shape, bf16),
            pltpu.SemaphoreType.DMA((3,)),
        ),
        flops=4 * 10**10,
        far_args=True,
    )
    token_parts = gather(packed)
    raw = [router_input] + ([swap(router_input, "expert", 1)] if cubed else [])
    sends = call(
        functools.partial(down_kernel, sizes, aux, paired, cubed, len(token_parts)),
        (((slots, hidden_size), bf16),) * local_experts,
        (*token_parts, down_weight.swapaxes(1, 2)),
    )
    if paired:
        parts = [sends[0]] + [swap(sends[k], "dp", k) for k in range(1, dp_count)]
    else:
        all_sends = jnp.concatenate(sends, axis=0).reshape(dp_count, piece, hidden_size)
        parts = list(lax.all_to_all(all_sends, "dp", 0, 0, tiled=True))
    if cubed:
        piece_shapes = (((2 * own_tokens, share), bf16),) * dp_count
    else:
        piece_shapes = (((dp_count, own_tokens, share), bf16),)
    full, slope, *pieces = call(
        functools.partial(
            table_kernel, sizes, aux, local_experts, paired, cubed, len(token_parts), len(raw)
        ),
        (((tokens, rows), f32), ((tokens, expert_total), f32), *piece_shapes),
        (*token_parts, *raw),
    )
    if cubed:
        pieces = [pieces[0]] + [swap(pieces[k], "dp", k) for k in range(1, dp_count)]
        inputs = []
    else:
        inputs = lax.all_to_all(pieces[0], "dp", 0, 0, tiled=True).reshape(group, share)
        inputs = gather(inputs)
    hidden = sum(part.astype(f32) for part in parts).astype(bf16)
    if paired:
        blocks = [hidden] + [swap(hidden, "dp", k) for k in range(1, dp_count)]
    else:
        spread = lax.all_gather(hidden, "dp", axis=0, tiled=True)
        blocks = list(spread.reshape(local_experts, slots, hidden_size))

    weights = (gate_weight, up_weight, gate_saved, up_saved)
    lanes = -(-rows // LANES) * LANES
    done = []
    for k in range(local_experts - 1):
        done += call(
            functools.partial(input_kernel, k, paired),
            (((slots, share), f32), ((1, lanes), f32)),
            (*weights, blocks[k]),
        )
    width = -(-(share + 2 * expert_count + 4 * local_experts) // LANES) * LANES
    if cubed:
        half = (expert_count // 2, group, width)
        mix_shapes = ((half, f32), (half, bf16))
    else:
        mix_shapes = (((expert_count, group, width), bf16),)
    *mixed, own = call(
        functools.partial(mix_kernel, local_experts - 1, group, paired, cubed),
        (*mix_shapes, ((tokens, LANES), f32)),
        (full, *weights, blocks[-1], *done),
        scratch=(VMEM((rows, share), f32), VMEM((1, lanes), f32)),
    )
    if cubed:
        far = swap(mixed[1], "expert", 1)
        sums = call(
            functools.partial(pair_kernel, share, expert_count, local_experts),
            (((3 * group, width), bf16),) * (expert_count // 2),
            (mixed[0], far, *pieces),
        )
        got = [sums[0]] + [swap(sums[k], "expert", 2 * k) for k in (1, 2, 3)]
    else:
        got = [lax.all_to_all(mixed[0], "expert", 0, 0, tiled=True)]
    grad_input, grad_router = call(
        functools.partial(final_kernel, sizes, paired, cubed, len(got), len(inputs), local_experts),
        (((1, group, share), bf16), ((local_experts, share), f32)),
        (*got, *inputs, own, slope, router_weight),
        scratch=(
            VMEM((1, group, share), bf16),
            VMEM((local_experts, share), f32),
            pltpu.SemaphoreType.DMA((2,)),
        ),
        far_outs=True,
    )
    return grad_input, grad_router


def solution(mesh):
    placed = (
        P("expert", None, "dp"),
        P("expert", None, None),
        P("expert", None, None),
        P("expert", "dp", None),
        P(None, "dp"),
        P("expert", "dp", None),
        P("expert", "dp", None),
        P("expert", None, "dp"),
        P("expert", None, None),
        P("expert", None, None),
    )

    return jax.shard_map(
        local,
        mesh=mesh,
        in_specs=placed,
        out_specs=(P("expert", None, "dp"), P("expert", "dp")),
        check_vma=False,
    )
```

time: 50.7 us -> 51.2 us (level)
  blocking collectives: 20.2 us -> 0 us
  waiting for transfers between devices: 5.7 us -> 18 us
  starting transfers between devices: 13.3 us -> 21.7 us
    all_to_all x2 -> x0, blocking collectives: 20.2 us -> none  [the longest x1 10.9 us: local(): lax.all_to_all(packed, 'expert', 0, 0, tiled=True)]
    ppermute x9 -> x18, waiting for transfers between devices: 5.7 us -> 18 us  [swap(): return lax.ppermute(value, axis, [(j, j ^ k) for j in range(count)])]
    ppermute x9 -> x18, starting transfers between devices: 13.3 us -> 21.7 us  [swap(): return lax.ppermute(value, axis, [(j, j ^ k) for j in range(count)])]
    pallas_call x8 -> x9, Pallas kernels: 10.3 us -> 10.5 us  [call(): pl.pallas_call(kernel, out_shape=tuple((space(*out) for out in outs)) if...]
  transfers between devices with their start and end apart: 9 -> 18, of which waited for: 2 -> 12; matrix products, arithmetic and copies ran while one was open for 0% -> 0% of each run, Pallas kernels for 8% -> 8%
where the time goes in v3:
time: 51.2 us; the launch traced here: 51 us
  starting transfers between devices  21.7 us (42%)
  waiting for transfers between devices  18 us (35%)
  Pallas kernels  10.5 us (21%)
  between operations  0.77 us (2%)
    ppermute x18, starting transfers between devices, swap(): return lax.ppermute(value, axis, [(j, j ^ k) for j in range(count)])  21.7 us
    ppermute x18, waiting for transfers between devices, swap(): return lax.ppermute(value, axis, [(j, j ^ k) for j in range(count)])  18 us
    pallas_call x9, Pallas kernels, call(): pl.pallas_call(kernel, out_shape=tuple((space(*out) for out in outs)) if...  10.5 us
  transfers between devices with their start and end apart: 18, of which 12 were waited for; matrix products, arithmetic and copies ran while one was open for 0% of the time, Pallas kernels for 8%

profile of v3, /device:TPU:0, one launch (start us, length us, event | category | flops | bytes accessed | tf_op | source)
XLA Modules:
  0.0 51.0 jit_solution(17106286746496545166)
XLA Ops:
  0.7 1.0 %shard_map.113.refs_0_ = bf16[8,1088]{1,0:T(8,128)(2,1)S(1)} custom-call(f32[1,8,32]{2,1,0:T(8,128)} %refs_0_.5, s32[1,8,8]{2,1,0:T(8,128)} %refs_1_.5, bf16[1,8,960]{2,1,0:T(8,128)(2,1)} %refs_2_.5), custom_call_target="tpu_custom_call" | custom-call | flops 40000000000 | tf_op jit(solution)/shard_map/pallas_call | solution.py:31
  1.7 4.0 %collective-permute-start.2 = (bf16[8,1088]{1,0:T(8,128)(2,1)S(1)}, bf16[8,1088]{1,0:T(8,128)(2,1)S(1)}, u32[]{:S(2)}, u32[]{:S(2)}) collective-permute-start(bf16[8,1088]{1,0:T(8,128)(2,1)S(1)} %shard_map.113.refs_0_), channel_id=1, source_target_pairs={{0,6},{1,7},{2,4},{3,5},{4,2},{5,3},{6,0},{7,1},{8,14},{9,15},{10,... | collective-permute-start | bytes 52232 | tf_op jit(solution)/shard_map/ppermute | solution.py:386
  6.3 1.1 %collective-permute-done.2.refs_3_ = bf16[8,1088]{1,0:T(8,128)(2,1)S(1)} collective-permute-done((bf16[8,1088]{1,0:T(8,128)(2,1)S(1)}, bf16[8,1088]{1,0:T(8,128)(2,1)S(1)}, u32[]{:S(2)}, u32[]{:S(2)}) %collective-permute-start.2) | collective-permute-done | bytes 17440 | tf_op jit(solution)/shard_map/ppermute | solution.py:386
  7.4 2.0 %collective-permute-done.1.refs_2_ = bf16[8,1088]{1,0:T(8,128)(2,1)S(1)} collective-permute-done((bf16[8,1088]{1,0:T(8,128)(2,1)S(1)}, bf16[8,1088]{1,0:T(8,128)(2,1)S(1)}, u32[]{:S(2)}, u32[]{:S(2)}) %collective-permute-start.1) | collective-permute-done | bytes 17440 | tf_op jit(solution)/shard_map/ppermute | solution.py:386
  10.1 1.3 %collective-permute-done.3.refs_4_ = bf16[32,1088]{1,0:T(8,128)(2,1)S(1)} collective-permute-done((bf16[32,1088]{1,0:T(8,128)(2,1)S(1)}, bf16[32,1088]{1,0:T(8,128)(2,1)S(1)}, u32[]{:S(2)}, u32[]{:S(2)}) %collective-permute-start.3) | collective-permute-done | bytes 69664 | tf_op jit(solution)/shard_map/ppermute | solution.py:386
  11.3 2.1 %shard_map.115 = (bf16[24,1024]{1,0:T(8,128)(2,1)S(1)}, bf16[24,1024]{1,0:T(8,128)(2,1)S(1)}, bf16[24,1024]{1,0:T(8,128)(2,1)S(1)}, bf16[24,1024]{1,0:T(8,128)(2,1)S(1)}) custom-call(bf16[8,1088]{1,0:T(8,128)(2,1)S(1)} %shard_map.113.refs_0_, bf16[8,1088]{1,0:T(8,128)(2,1)S(1)} %collective-permute-done.refs_1_, ...), custom_call_target="tpu_custom_call" | custom-call | tf_op jit(solution)/shard_map/pallas_call | solution.py:31
  13.4 1.6 %collective-permute-start.5 = (bf16[24,1024]{1,0:T(8,128)(2,1)S(1)}, bf16[24,1024]{1,0:T(8,128)(2,1)S(1)}, u32[]{:S(2)}, u32[]{:S(2)}) collective-permute-start(bf16[24,1024]{1,0:T(8,128)(2,1)S(1)} %get-tuple-element.27), channel_id=1, source_target_pairs={{0,8},{8,0},{16,24},{24,16},{1,9},{9,1},{17,25},{25,17},{2,10},{10... | collective-permute-start | bytes 147464 | tf_op jit(solution)/shard_map/ppermute | solution.py:386
  15.0 2.6 %collective-permute-start.6 = (bf16[24,1024]{1,0:T(8,128)(2,1)S(1)}, bf16[24,1024]{1,0:T(8,128)(2,1)S(1)}, u32[]{:S(2)}, u32[]{:S(2)}) collective-permute-start(bf16[24,1024]{1,0:T(8,128)(2,1)S(1)} %get-tuple-element.28), channel_id=1, source_target_pairs={{0,16},{8,24},{16,0},{24,8},{1,17},{9,25},{17,1},{25,9},{2,18},{10... | collective-permute-start | bytes 147464 | tf_op jit(solution)/shard_map/ppermute | solution.py:386
  17.8 3.0 %collective-permute-done.6 = bf16[24,1024]{1,0:T(8,128)(2,1)S(1)} collective-permute-done((bf16[24,1024]{1,0:T(8,128)(2,1)S(1)}, bf16[24,1024]{1,0:T(8,128)(2,1)S(1)}, u32[]{:S(2)}, u32[]{:S(2)}) %collective-permute-start.6) | collective-permute-done | bytes 49184 | tf_op jit(solution)/shard_map/ppermute | solution.py:386
  20.9 2.6 %collective-permute-done.7 = bf16[24,1024]{1,0:T(8,128)(2,1)S(1)} collective-permute-done((bf16[24,1024]{1,0:T(8,128)(2,1)S(1)}, bf16[24,1024]{1,0:T(8,128)(2,1)S(1)}, u32[]{:S(2)}, u32[]{:S(2)}) %collective-permute-start.7) | collective-permute-done | bytes 49184 | tf_op jit(solution)/shard_map/ppermute | solution.py:386
  24.3 0.9 %collective-permute-start.9 = (bf16[24,1024]{1,0:T(8,128)(2,1)S(1)}, bf16[24,1024]{1,0:T(8,128)(2,1)S(1)}, u32[]{:S(2)}, u32[]{:S(2)}) collective-permute-start(bf16[24,1024]{1,0:T(8,128)(2,1)S(1)} %add_convert_fusion.refs_4_), channel_id=1, source_target_pairs={{0,8},{8,0},{16,24},{24,16},{1,9},{9,1},{17,25},{25,17},{2,10},{10... | collective-permute-start | bytes 147464 | tf_op jit(solution)/shard_map/ppermute | solution.py:386
  25.2 2.8 %collective-permute-start.8 = (bf16[24,1024]{1,0:T(8,128)(2,1)S(1)}, bf16[24,1024]{1,0:T(8,128)(2,1)S(1)}, u32[]{:S(2)}, u32[]{:S(2)}) collective-permute-start(bf16[24,1024]{1,0:T(8,128)(2,1)S(1)} %add_convert_fusion.refs_4_), channel_id=1, source_target_pairs={{0,24},{8,16},{16,8},{24,0},{1,25},{9,17},{17,9},{25,1},{2,26},{10... | collective-permute-start | bytes 147464 | tf_op jit(solution)/shard_map/ppermute | solution.py:386
  28.0 1.2 %collective-permute-done.4.refs_6_ = bf16[1,2,3840]{2,1,0:T(2,128)(2,1)S(1)} collective-permute-done((bf16[1,2,3840]{2,1,0:T(2,128)(2,1)S(1)}, bf16[1,2,3840]{2,1,0:T(2,128)(2,1)S(1)}, u32[]{:S(2)}, u32[]{:S(2)}) %collective-permute-start.4) | collective-permute-done | bytes 15392 | tf_op jit(solution)/shard_map/ppermute | solution.py:386
  29.7 1.2 %shard_map.116 = (f32[24,960]{1,0:T(8,128)S(1)}, f32[1,128]{1,0:T(1,128)S(1)}) custom-call(bf16[4,960,1024]{2,1,0:T(8,128)(2,1)S(1)} %copy-done, bf16[4,960,1024]{2,1,0:T(8,128)(2,1)S(1)} %copy-done.1, bf16[4,24,1024]{2,1,0:T(8,128)(2,1)S(1)} %copy-done.3, bf16[4,24,1024]{2,1,0:T(8,128)(2,1)S(1)} %copy-done.4, bf16[24,1024]{1,0:T(8,128)(2,1)S(1)} %add_convert_fusion.refs_4_), custom_call_target="tpu_custom_call" | custom-call | tf_op jit(solution)/shard_map/pallas_call | solution.py:31
  30.9 1.2 %shard_map.118 = (f32[24,960]{1,0:T(8,128)S(1)}, f32[1,128]{1,0:T(1,128)S(1)}) custom-call(bf16[4,960,1024]{2,1,0:T(8,128)(2,1)S(1)} %copy-done, bf16[4,960,1024]{2,1,0:T(8,128)(2,1)S(1)} %copy-done.1, bf16[4,24,1024]{2,1,0:T(8,128)(2,1)S(1)} %copy-done.3, bf16[4,24,1024]{2,1,0:T(8,128)(2,1)S(1)} %copy-done.4, ...), custom_call_target="tpu_custom_call" | custom-call | tf_op jit(solution)/shard_map/pallas_call | solution.py:31
  32.2 1.2 %shard_map.117 = (f32[24,960]{1,0:T(8,128)S(1)}, f32[1,128]{1,0:T(1,128)S(1)}) custom-call(bf16[4,960,1024]{2,1,0:T(8,128)(2,1)S(1)} %copy-done, bf16[4,960,1024]{2,1,0:T(8,128)(2,1)S(1)} %copy-done.1, bf16[4,24,1024]{2,1,0:T(8,128)(2,1)S(1)} %copy-done.3, bf16[4,24,1024]{2,1,0:T(8,128)(2,1)S(1)} %copy-done.4, ...), custom_call_target="tpu_custom_call" | custom-call | tf_op jit(solution)/shard_map/pallas_call | solution.py:31
  33.4 1.5 %shard_map.119 = (f32[4,8,1024]{2,1,0:T(8,128)S(1)}, bf16[4,8,1024]{2,1,0:T(8,128)(2,1)S(1)}, f32[64,128]{1,0:T(8,128)S(1)}) custom-call(f32[64,96]{1,0:T(8,128)S(1)} %get-tuple-element.25.full_ref, bf16[4,960,1024]{2,1,0:T(8,128)(2,1)S(1)} %copy-done, bf16[4,960,1024]{2,1,0:T(8,128)(2,1)S(1)} %copy-done.1, bf16[4,24,1024]{2,1,0:T(8,128)(2,1)S(1)} %copy-done.3, ...), custom_call_target="tpu_custom_call" | custom-call | tf_op jit(solution)/shard_map/pallas_call | solution.py:31
  35.2 1.6 %collective-permute-start.13 = (bf16[4,960]{1,0:T(4,128)(2,1)S(1)}, bf16[4,960]{1,0:T(4,128)(2,1)S(1)}, u32[]{:S(2)}, u32[]{:S(2)}) collective-permute-start(bf16[4,960]{1,0:T(4,128)(2,1)S(1)} %get-tuple-element.40), channel_id=1, source_target_pairs={{0,16},{8,24},{16,0},{24,8},{1,17},{9,25},{17,1},{25,9},{2,18},{10... | collective-permute-start | bytes 23048 | tf_op jit(solution)/shard_map/ppermute | solution.py:386
  36.8 2.8 %collective-permute-start.14 = (bf16[4,960]{1,0:T(4,128)(2,1)S(1)}, bf16[4,960]{1,0:T(4,128)(2,1)S(1)}, u32[]{:S(2)}, u32[]{:S(2)}) collective-permute-start(bf16[4,960]{1,0:T(4,128)(2,1)S(1)} %get-tuple-element.41), channel_id=1, source_target_pairs={{0,24},{8,16},{16,8},{24,0},{1,25},{9,17},{17,9},{25,1},{2,26},{10... | collective-permute-start | bytes 23048 | tf_op jit(solution)/shard_map/ppermute | solution.py:386
  39.8 2.5 %collective-permute-done.14.refs_3_ = bf16[4,960]{1,0:T(4,128)(2,1)S(1)} collective-permute-done((bf16[4,960]{1,0:T(4,128)(2,1)S(1)}, bf16[4,960]{1,0:T(4,128)(2,1)S(1)}, u32[]{:S(2)}, u32[]{:S(2)}) %collective-permute-start.14) | collective-permute-done | bytes 7712 | tf_op jit(solution)/shard_map/ppermute | solution.py:386
  43.1 1.5 %collective-permute-start.16 = (bf16[24,1024]{1,0:T(8,128)(2,1)S(1)}, bf16[24,1024]{1,0:T(8,128)(2,1)S(1)}, u32[]{:S(2)}, u32[]{:S(2)}) collective-permute-start(bf16[24,1024]{1,0:T(8,128)(2,1)S(1)} %get-tuple-element.44), channel_id=1, source_target_pairs={{0,4},{1,5},{2,6},{3,7},{4,0},{5,1},{6,2},{7,3},{8,12},{9,13},{10,... | collective-permute-start | bytes 147464 | tf_op jit(solution)/shard_map/ppermute | solution.py:386
  44.6 1.4 %collective-permute-start.17 = (bf16[24,1024]{1,0:T(8,128)(2,1)S(1)}, bf16[24,1024]{1,0:T(8,128)(2,1)S(1)}, u32[]{:S(2)}, u32[]{:S(2)}) collective-permute-start(bf16[24,1024]{1,0:T(8,128)(2,1)S(1)} %get-tuple-element.45), channel_id=1, source_target_pairs={{0,6},{1,7},{2,4},{3,5},{4,2},{5,3},{6,0},{7,1},{8,14},{9,15},{10,... | collective-permute-start | bytes 147464 | tf_op jit(solution)/shard_map/ppermute | solution.py:386
  47.2 2.4 %collective-permute-done.17.refs_3_ = bf16[24,1024]{1,0:T(8,128)(2,1)S(1)} collective-permute-done((bf16[24,1024]{1,0:T(8,128)(2,1)S(1)}, bf16[24,1024]{1,0:T(8,128)(2,1)S(1)}, u32[]{:S(2)}, u32[]{:S(2)}) %collective-permute-start.17) | collective-permute-done | bytes 49184 | tf_op jit(solution)/shard_map/ppermute | solution.py:386
  49.6 1.4 %shard_map.121 = (bf16[1,8,960]{2,1,0:T(8,128)(2,1)}, f32[4,960]{1,0:T(4,128)}) custom-call(bf16[24,1024]{1,0:T(8,128)(2,1)S(1)} %get-tuple-element.42.refs_0_, bf16[24,1024]{1,0:T(8,128)(2,1)S(1)} %collective-permute-done.15.refs_1_, bf16[24,1024]{1,0:T(8,128)(2,1)S(1)} %collective-permute-done.16.refs_2_, ...), custom_call_target="tpu_custom_call" | custom-call | tf_op jit(solution)/shard_map/pallas_call | solution.py:31
  (37 shorter events, 5.2 us)
Async XLA Ops:
  0.6 29.1 %copy-start.1 = (bf16[4,960,1024]{2,1,0:T(8,128)(2,1)S(1)}, bf16[4,960,1024]{2,1,0:T(8,128)(2,1)}, u32[]{:S(2)}) copy-start(bf16[4,960,1024]{2,1,0:T(8,128)(2,1)} %refs_1_.9) | copy-start | bytes 23592964
  1.7 26.3 %copy-start.6 = (bf16[1,2,3840]{2,1,0:T(2,128)(2,1)S(1)}, bf16[1,2,3840]{2,1,0:T(2,128)(2,1)}, u32[]{:S(2)}) copy-start(bf16[1,2,3840]{2,1,0:T(2,128)(2,1)} %refs_5_.1) | copy-start | bytes 46084
  1.7 28.0 %copy-start = (bf16[4,960,1024]{2,1,0:T(8,128)(2,1)S(1)}, bf16[4,960,1024]{2,1,0:T(8,128)(2,1)}, u32[]{:S(2)}) copy-start(bf16[4,960,1024]{2,1,0:T(8,128)(2,1)} %refs_0_.9) | copy-start | bytes 23592964
  1.7 28.0 %copy-start.3 = (bf16[4,24,1024]{2,1,0:T(8,128)(2,1)S(1)}, bf16[4,24,1024]{2,1,0:T(8,128)(2,1)}, u32[]{:S(2)}) copy-start(bf16[4,24,1024]{2,1,0:T(8,128)(2,1)} %refs_2_.9) | copy-start | bytes 589828
  1.7 28.0 %copy-start.4 = (bf16[4,24,1024]{2,1,0:T(8,128)(2,1)S(1)}, bf16[4,24,1024]{2,1,0:T(8,128)(2,1)}, u32[]{:S(2)}) copy-start(bf16[4,24,1024]{2,1,0:T(8,128)(2,1)} %refs_3_.7) | copy-start | bytes 589828
  1.7 5.7 %collective-permute-start.2 = (bf16[8,1088]{1,0:T(8,128)(2,1)S(1)}, bf16[8,1088]{1,0:T(8,128)(2,1)S(1)}, u32[]{:S(2)}, u32[]{:S(2)}) collective-permute-start(bf16[8,1088]{1,0:T(8,128)(2,1)S(1)} %shard_map.113.refs_0_), channel_id=1, source_target_pairs={{0,6},{1,7},{2,4},{3,5},{4,2},{5,3},{6,0},{7,1},{8,14},{9,15},{10,... | collective-permute-start | bytes 52232 | tf_op jit(solution)/shard_map/ppermute | solution.py:386
  5.7 3.8 %collective-permute-start.1 = (bf16[8,1088]{1,0:T(8,128)(2,1)S(1)}, bf16[8,1088]{1,0:T(8,128)(2,1)S(1)}, u32[]{:S(2)}, u32[]{:S(2)}) collective-permute-start(bf16[8,1088]{1,0:T(8,128)(2,1)S(1)} %shard_map.113.refs_0_), channel_id=1, source_target_pairs={{0,4},{1,5},{2,6},{3,7},{4,0},{5,1},{6,2},{7,3},{8,12},{9,13},{10,... | collective-permute-start | bytes 52232 | tf_op jit(solution)/shard_map/ppermute | solution.py:386
  6.2 3.8 %collective-permute-start = (bf16[8,1088]{1,0:T(8,128)(2,1)S(1)}, bf16[8,1088]{1,0:T(8,128)(2,1)S(1)}, u32[]{:S(2)}, u32[]{:S(2)}) collective-permute-start(bf16[8,1088]{1,0:T(8,128)(2,1)S(1)} %shard_map.113.refs_0_), channel_id=1, source_target_pairs={{0,2},{1,3},{2,0},{3,1},{4,6},{5,7},{6,4},{7,5},{8,10},{9,11},{10,... | collective-permute-start | bytes 52232 | tf_op jit(solution)/shard_map/ppermute | solution.py:386
  10.0 1.3 %collective-permute-start.3 = (bf16[32,1088]{1,0:T(8,128)(2,1)S(1)}, bf16[32,1088]{1,0:T(8,128)(2,1)S(1)}, u32[]{:S(2)}, u32[]{:S(2)}) collective-permute-start(bf16[32,1088]{1,0:T(8,128)(2,1)S(1)} %pad_maximum_fusion), channel_id=1, source_target_pairs={{0,1},{1,0},{2,3},{3,2},{4,5},{5,4},{6,7},{7,6},{8,9},{9,8},{10,11... | collective-permute-start | bytes 208904 | tf_op jit(solution)/shard_map/ppermute | solution.py:386
  13.4 4.4 %collective-permute-start.5 = (bf16[24,1024]{1,0:T(8,128)(2,1)S(1)}, bf16[24,1024]{1,0:T(8,128)(2,1)S(1)}, u32[]{:S(2)}, u32[]{:S(2)}) collective-permute-start(bf16[24,1024]{1,0:T(8,128)(2,1)S(1)} %get-tuple-element.27), channel_id=1, source_target_pairs={{0,8},{8,0},{16,24},{24,16},{1,9},{9,1},{17,25},{25,17},{2,10},{10... | collective-permute-start | bytes 147464 | tf_op jit(solution)/shard_map/ppermute | solution.py:386
  15.0 5.9 %collective-permute-start.6 = (bf16[24,1024]{1,0:T(8,128)(2,1)S(1)}, bf16[24,1024]{1,0:T(8,128)(2,1)S(1)}, u32[]{:S(2)}, u32[]{:S(2)}) collective-permute-start(bf16[24,1024]{1,0:T(8,128)(2,1)S(1)} %get-tuple-element.28), channel_id=1, source_target_pairs={{0,16},{8,24},{16,0},{24,8},{1,17},{9,25},{17,1},{25,9},{2,18},{10... | collective-permute-start | bytes 147464 | tf_op jit(solution)/shard_map/ppermute | solution.py:386
  17.6 5.9 %collective-permute-start.7 = (bf16[24,1024]{1,0:T(8,128)(2,1)S(1)}, bf16[24,1024]{1,0:T(8,128)(2,1)S(1)}, u32[]{:S(2)}, u32[]{:S(2)}) collective-permute-start(bf16[24,1024]{1,0:T(8,128)(2,1)S(1)} %get-tuple-element.29), channel_id=1, source_target_pairs={{0,24},{8,16},{16,8},{24,0},{1,25},{9,17},{17,9},{25,1},{2,26},{10... | collective-permute-start | bytes 147464 | tf_op jit(solution)/shard_map/ppermute | solution.py:386
  23.5 7.4 %collective-permute-start.10 = (bf16[24,1024]{1,0:T(8,128)(2,1)S(1)}, bf16[24,1024]{1,0:T(8,128)(2,1)S(1)}, u32[]{:S(2)}, u32[]{:S(2)}) collective-permute-start(bf16[24,1024]{1,0:T(8,128)(2,1)S(1)} %add_convert_fusion.refs_4_), channel_id=1, source_target_pairs={{0,16},{8,24},{16,0},{24,8},{1,17},{9,25},{17,1},{25,9},{2,18},{10... | collective-permute-start | bytes 147464 | tf_op jit(solution)/shard_map/ppermute | solution.py:386
  24.3 7.9 %collective-permute-start.9 = (bf16[24,1024]{1,0:T(8,128)(2,1)S(1)}, bf16[24,1024]{1,0:T(8,128)(2,1)S(1)}, u32[]{:S(2)}, u32[]{:S(2)}) collective-permute-start(bf16[24,1024]{1,0:T(8,128)(2,1)S(1)} %add_convert_fusion.refs_4_), channel_id=1, source_target_pairs={{0,8},{8,0},{16,24},{24,16},{1,9},{9,1},{17,25},{25,17},{2,10},{10... | collective-permute-start | bytes 147464 | tf_op jit(solution)/shard_map/ppermute | solution.py:386
  25.2 8.2 %collective-permute-start.8 = (bf16[24,1024]{1,0:T(8,128)(2,1)S(1)}, bf16[24,1024]{1,0:T(8,128)(2,1)S(1)}, u32[]{:S(2)}, u32[]{:S(2)}) collective-permute-start(bf16[24,1024]{1,0:T(8,128)(2,1)S(1)} %add_convert_fusion.refs_4_), channel_id=1, source_target_pairs={{0,24},{8,16},{16,8},{24,0},{1,25},{9,17},{17,9},{25,1},{2,26},{10... | collective-permute-start | bytes 147464 | tf_op jit(solution)/shard_map/ppermute | solution.py:386
  28.0 1.2 %collective-permute-start.4 = (bf16[1,2,3840]{2,1,0:T(2,128)(2,1)S(1)}, bf16[1,2,3840]{2,1,0:T(2,128)(2,1)S(1)}, u32[]{:S(2)}, u32[]{:S(2)}) collective-permute-start(bf16[1,2,3840]{2,1,0:T(2,128)(2,1)S(1)} %copy-done.6), channel_id=1, source_target_pairs={{0,1},{1,0},{2,3},{3,2},{4,5},{5,4},{6,7},{7,6},{8,9},{9,8},{10,11... | collective-permute-start | bytes 46088 | tf_op jit(solution)/shard_map/ppermute | solution.py:386
  33.4 16.2 %copy-start.5 = (bf16[32,960]{1,0:T(8,128)(2,1)S(1)}, bf16[32,960]{1,0:T(8,128)(2,1)}, u32[]{:S(2)}) copy-start(bf16[32,960]{1,0:T(8,128)(2,1)} %refs_6_.1) | copy-start | bytes 184324
  35.0 7.3 %collective-permute-start.11 = (bf16[4,8,1024]{2,1,0:T(8,128)(2,1)S(1)}, bf16[4,8,1024]{2,1,0:T(8,128)(2,1)S(1)}, u32[]{:S(2)}, u32[]{:S(2)}) collective-permute-start(bf16[4,8,1024]{2,1,0:T(8,128)(2,1)S(1)} %get-tuple-element.37), channel_id=1, source_target_pairs={{0,1},{1,0},{2,3},{3,2},{4,5},{5,4},{6,7},{7,6},{8,9},{9,8},{10,11... | collective-permute-start | bytes 196616 | tf_op jit(solution)/shard_map/ppermute | solution.py:386
  35.2 4.4 %collective-permute-start.12 = (bf16[4,960]{1,0:T(4,128)(2,1)S(1)}, bf16[4,960]{1,0:T(4,128)(2,1)S(1)}, u32[]{:S(2)}, u32[]{:S(2)}) collective-permute-start(bf16[4,960]{1,0:T(4,128)(2,1)S(1)} %get-tuple-element.39), channel_id=1, source_target_pairs={{0,8},{8,0},{16,24},{24,16},{1,9},{9,1},{17,25},{25,17},{2,10},{10... | collective-permute-start | bytes 23048 | tf_op jit(solution)/shard_map/ppermute | solution.py:386
  35.2 4.5 %collective-permute-start.13 = (bf16[4,960]{1,0:T(4,128)(2,1)S(1)}, bf16[4,960]{1,0:T(4,128)(2,1)S(1)}, u32[]{:S(2)}, u32[]{:S(2)}) collective-permute-start(bf16[4,960]{1,0:T(4,128)(2,1)S(1)} %get-tuple-element.40), channel_id=1, source_target_pairs={{0,16},{8,24},{16,0},{24,8},{1,17},{9,25},{17,1},{25,9},{2,18},{10... | collective-permute-start | bytes 23048 | tf_op jit(solution)/shard_map/ppermute | solution.py:386
  36.8 5.4 %collective-permute-start.14 = (bf16[4,960]{1,0:T(4,128)(2,1)S(1)}, bf16[4,960]{1,0:T(4,128)(2,1)S(1)}, u32[]{:S(2)}, u32[]{:S(2)}) collective-permute-start(bf16[4,960]{1,0:T(4,128)(2,1)S(1)} %get-tuple-element.41), channel_id=1, source_target_pairs={{0,24},{8,16},{16,8},{24,0},{1,25},{9,17},{17,9},{25,1},{2,26},{10... | collective-permute-start | bytes 23048 | tf_op jit(solution)/shard_map/ppermute | solution.py:386
  42.5 4.1 %collective-permute-start.15 = (bf16[24,1024]{1,0:T(8,128)(2,1)S(1)}, bf16[24,1024]{1,0:T(8,128)(2,1)S(1)}, u32[]{:S(2)}, u32[]{:S(2)}) collective-permute-start(bf16[24,1024]{1,0:T(8,128)(2,1)S(1)} %get-tuple-element.43), channel_id=1, source_target_pairs={{0,2},{1,3},{2,0},{3,1},{4,6},{5,7},{6,4},{7,5},{8,10},{9,11},{10,... | collective-permute-start | bytes 147464 | tf_op jit(solution)/shard_map/ppermute | solution.py:386
  43.1 4.1 %collective-permute-start.16 = (bf16[24,1024]{1,0:T(8,128)(2,1)S(1)}, bf16[24,1024]{1,0:T(8,128)(2,1)S(1)}, u32[]{:S(2)}, u32[]{:S(2)}) collective-permute-start(bf16[24,1024]{1,0:T(8,128)(2,1)S(1)} %get-tuple-element.44), channel_id=1, source_target_pairs={{0,4},{1,5},{2,6},{3,7},{4,0},{5,1},{6,2},{7,3},{8,12},{9,13},{10,... | collective-permute-start | bytes 147464 | tf_op jit(solution)/shard_map/ppermute | solution.py:386
  44.6 5.0 %collective-permute-start.17 = (bf16[24,1024]{1,0:T(8,128)(2,1)S(1)}, bf16[24,1024]{1,0:T(8,128)(2,1)S(1)}, u32[]{:S(2)}, u32[]{:S(2)}) collective-permute-start(bf16[24,1024]{1,0:T(8,128)(2,1)S(1)} %get-tuple-element.45), channel_id=1, source_target_pairs={{0,6},{1,7},{2,4},{3,5},{4,2},{5,3},{6,0},{7,1},{8,14},{9,15},{10,... | collective-permute-start | bytes 147464 | tf_op jit(solution)/shard_map/ppermute | solution.py:386
  (1 other events, 10.7 us)

commit v4 on v3

--- a/solution.py
+++ b/solution.py
@@ -34,7 +34,7 @@
         in_specs=[far if far_args else near] * len(args),
         out_specs=(out_spec,) * len(outs) if several else out_spec,
         scratch_shapes=list(scratch),
-        compiler_params=pltpu.CompilerParams(vmem_limit_bytes=12 << 20),
+        compiler_params=pltpu.CompilerParams(vmem_limit_bytes=14 << 20),
         cost_estimate=pl.CostEstimate(flops=flops, bytes_accessed=0, transcendentals=0),
     )(*[pltpu.with_memory_space_constraint(arg, arg_space) for arg in args])
 
@@ -48,11 +48,12 @@
     )
 
 
-def stacked(refs, columns):
-    if len(refs) == 1:
-        return refs[0][:, columns]
-    parts = [ref[:, columns].astype(jnp.float32) for ref in refs]
-    return jnp.concatenate(parts, axis=0).astype(refs[0].dtype)
+def stacked(refs, stride, first, rows, columns):
+    parts = []
+    for ref in refs:
+        for start in range(0, ref.shape[0], stride):
+            parts.append(ref[start + first : start + first + rows, columns].astype(jnp.float32))
+    return jnp.concatenate(parts, axis=0)
 
 
 def split(values):
@@ -60,17 +61,25 @@
     return upper, (values - upper.astype(jnp.float32)).astype(jnp.bfloat16)
 
 
-def pack_kernel(expert_total, *refs):
-    far, out_ref, held, sems = refs[:3], refs[3], refs[4:7], refs[7]
+def chosen_piece(lines, k, paired):
+    me = lax.axis_index("dp")
+    found = lines[0]
+    for d in range(1, len(lines)):
+        found = jnp.where(place_of(k, me, paired) == d, lines[d], found)
+    return found
+
+
+def pack_kernel(expert_total, cubed, *refs):
+    far, (out_ref, *piece_refs), held, sems = refs[:4], refs[4:-5], refs[-5:-1], refs[-1]
     fetches = [pltpu.make_async_copy(*pair, sems.at[n]) for n, pair in enumerate(zip(far, held))]
     for fetch in fetches:
         fetch.start()
     for fetch in fetches:
         fetch.wait()
-    logits_ref, ids_ref, rows_ref = held
-    group, width = out_ref.shape
+    logits_ref, ids_ref, rows_ref, inputs_ref = held
+    _, group, share = rows_ref.shape
+    aux = out_ref.shape[1] - share
     top = ids_ref.shape[2]
-    aux = width - rows_ref.shape[2]
     logits = logits_ref[0]
     first = logits.astype(jnp.bfloat16).astype(jnp.float32)
     rest = logits - first
@@ -79,8 +88,19 @@
     spare = aux - 3 * expert_total - top
     if spare:
         pieces.append(jnp.zeros((group, spare), jnp.float32))
-    out_ref[:, :aux] = jnp.concatenate(pieces, axis=1).astype(jnp.bfloat16)
-    out_ref[:, aux:] = rows_ref[0]
+    out_ref[:group, :aux] = jnp.concatenate(pieces, axis=1).astype(jnp.bfloat16)
+    out_ref[:group, aux:] = rows_ref[0]
+    inputs = inputs_ref[0].astype(jnp.float32)
+    lines = [inputs[:, d * share : (d + 1) * share] for d in range(inputs.shape[1] // share)]
+    if cubed:
+        same_ref, next_ref, across_ref = piece_refs
+        found = [chosen_piece(lines, k, cubed) for k in range(4)]
+        same_ref[...] = found[0].astype(jnp.bfloat16)
+        next_ref[...] = jnp.concatenate([found[1], found[3]], axis=0).astype(jnp.bfloat16)
+        across_ref[...] = found[2].astype(jnp.bfloat16)
+    else:
+        out_ref[group:, :aux] = jnp.zeros((group, aux), jnp.bfloat16)
+        out_ref[group:, aux:] = jnp.concatenate(lines, axis=0).astype(jnp.bfloat16)
 
 
 def routing(head, sizes, cubed):
@@ -102,16 +122,24 @@
 
 
 def down_kernel(sizes, aux, paired, cubed, token_count, *refs):
-    token_refs, weight_ref, send_refs = refs[:token_count], refs[token_count], refs[token_count + 1 :]
-    expert_total = sizes[1]
+    token_refs, weight_ref = refs[:token_count], refs[token_count]
+    send_refs, product_ref = refs[token_count + 1 : -1], refs[-1]
+    group, expert_total = sizes[:2]
     local_experts, share, _ = weight_ref.shape
     slots = send_refs[0].shape[0]
     me = lax.axis_index("dp")
     base = lax.axis_index("expert") * local_experts
-    features = stacked(token_refs, slice(aux, aux + share))
+    stride = group if cubed else 2 * group
+    features = stacked(token_refs, stride, 0, group, slice(aux, aux + share)).astype(jnp.bfloat16)
     tokens = features.shape[0]
-    early = tokens <= 256
-    _, slot = routing(stacked(token_refs, slice(0, aux)).astype(jnp.float32), sizes, cubed)
+
+    def multiply(k):
+        weight = weight_ref[place_of(k, me, paired)]
+        product = jnp.dot(features, weight, preferred_element_type=jnp.float32)
+        product_ref[k % 2] = product.astype(jnp.bfloat16)
+
+    multiply(0)
+    _, slot = routing(stacked(token_refs, stride, 0, group, slice(0, aux)), sizes, cubed)
     order = place_of(iota((8, expert_total), 0), me, paired)
     pick = (iota((8, expert_total), 1) == base + order).astype(jnp.bfloat16)
     slot_rows = lax.dot_general(
@@ -119,26 +147,22 @@
     )
     slot_at = iota((slots, tokens), 0).astype(jnp.float32)
     for k, send_ref in enumerate(send_refs):
+        if k + 1 < local_experts:
+            multiply(k + 1)
         chosen = (slot_at == slot_rows[k : k + 1, :]).astype(jnp.bfloat16)
-        weight = weight_ref[place_of(k, me, paired)]
-        if early:
-            product = jnp.dot(features, weight, preferred_element_type=jnp.float32)
-            value = jnp.dot(chosen, product.astype(jnp.bfloat16), preferred_element_type=jnp.float32)
-        else:
-            sent = jnp.dot(chosen, features, preferred_element_type=jnp.float32).astype(jnp.bfloat16)
-            value = jnp.dot(sent, weight, preferred_element_type=jnp.float32)
+        value = jnp.dot(chosen, product_ref[k % 2], preferred_element_type=jnp.float32)
         send_ref[...] = value.astype(jnp.bfloat16)
 
 
-def table_kernel(sizes, aux, local_experts, paired, cubed, token_count, input_count, *refs):
-    token_refs, refs = refs[:token_count], refs[token_count:]
-    input_refs, (full_ref, slope_ref, *piece_refs) = refs[:input_count], refs[input_count:]
-    expert_total = sizes[1]
+def table_kernel(sizes, aux, local_experts, paired, cubed, token_count, *refs):
+    token_refs, (*input_refs, full_ref, slope_ref, piece_ref) = refs[:token_count], refs[token_count:]
+    group, expert_total = sizes[:2]
+    stride = group if cubed else 2 * group
     tokens, rows = full_ref.shape
     slots = rows // local_experts
     me = lax.axis_index("dp")
     base = lax.axis_index("expert") * local_experts
-    head = stacked(token_refs, slice(0, aux)).astype(jnp.float32)
+    head = stacked(token_refs, stride, 0, group, slice(0, aux))
     logits = (
         head[:, :expert_total]
         + head[:, expert_total : 2 * expert_total]
@@ -156,19 +180,16 @@
     wanted = lax.rem(iota((tokens, rows), 1), slots).astype(jnp.float32)
     full_ref[...] = jnp.where(slot_wide == wanted, gates_wide, 0.0)
     dp_count = lax.axis_size("dp")
-    raw = [ref[0] for ref in input_refs]
-    share = raw[0].shape[1] // dp_count
-    if not cubed:
-        for d in range(dp_count):
-            piece_refs[0][d] = raw[0][:, d * share : (d + 1) * share]
+    own_tokens = group // dp_count
+    if cubed:
+        across_ref, got_ref = input_refs
+        parts = [across_ref[...].astype(jnp.float32), got_ref[own_tokens:].astype(jnp.float32)]
+        piece_ref[...] = jnp.concatenate(parts, axis=0).astype(jnp.bfloat16)
         return
-    both = jnp.concatenate([value.astype(jnp.float32) for value in raw], axis=0)
-    lines = [both[:, d * share : (d + 1) * share] for d in range(dp_count)]
-    for k, piece_ref in enumerate(piece_refs):
-        found = lines[0]
-        for d in range(1, dp_count):
-            found = jnp.where(place_of(k, me, paired) == d, lines[d], found)
-        piece_ref[...] = found.astype(jnp.bfloat16)
+    features = slice(aux, token_refs[0].shape[1])
+    for d in range(dp_count):
+        lines = stacked(token_refs, stride, group + d * own_tokens, own_tokens, features)
+        piece_ref[d] = lines.astype(jnp.bfloat16)
 
 
 def expert_parts(k, paired, gate_w_ref, up_w_ref, gate_ref, up_ref, block_ref, row_ref, share_ref):
@@ -197,6 +218,8 @@
 
 def mix_kernel(k, group, paired, cubed, full_ref, *refs):
     weights, rest = refs[:5], refs[5:]
+    if cubed:
+        input_refs, rest = rest[:3], rest[3:]
     earlier, out_refs, (held_ref, share_ref) = rest[: 2 * k], rest[2 * k : -2], rest[-2:]
     slots = weights[4].shape[0]
     expert_parts(k, paired, *weights, held_ref.at[pl.ds(k * slots, slots)], share_ref)
@@ -239,21 +262,26 @@
     mixed = jnp.dot(high, values, preferred_element_type=jnp.float32)
     mixed = mixed + jnp.dot(low, values, preferred_element_type=jnp.float32)
     at = 0
+    if cubed:
+        own_tokens = input_refs[0].shape[0]
+        same, near, far = [ref[...].astype(jnp.float32) for ref in input_refs]
+        routed = jnp.concatenate([same, near[:own_tokens], far], axis=0)
     for out_ref in out_refs[:-1]:
-        for q in range(out_ref.shape[0]):
+        blocks = out_ref.shape[0]
+        if cubed:
+            blocks = blocks - 1
+            out_ref[blocks, :, :share] = routed.astype(out_ref.dtype)
+            out_ref[blocks, :, share:] = jnp.zeros((group, width - share), out_ref.dtype)
+        for q in range(blocks):
             lines = slice(at * group, (at + 1) * group)
             out_ref[q, :, :share] = mixed[lines].astype(out_ref.dtype)
             out_ref[q, :, share:] = extra[lines].astype(out_ref.dtype)
             at = at + 1
 
 
-def pair_kernel(share, count, local_experts, near_ref, far_ref, *refs):
-    piece_refs, out_refs = refs[: -near_ref.shape[0]], refs[-near_ref.shape[0] :]
+def pair_kernel(share, count, local_experts, near_ref, far_ref, *out_refs):
     group, width = near_ref.shape[1:]
-    own = group // len(piece_refs)
-    pieces = [ref[...].astype(jnp.float32) for ref in piece_refs]
-    routed = jnp.concatenate([p[:own] for p in pieces] + [p[own:] for p in pieces], axis=0)
-    routed = routed.astype(jnp.bfloat16)
+    last = near_ref.shape[0] - 1
     ends = (0, count, 2 * count, 2 * count + 2 * local_experts, 2 * count + 4 * local_experts)
     for q, out_ref in enumerate(out_refs):
         total = near_ref[q] + far_ref[q].astype(jnp.float32)
@@ -264,50 +292,109 @@
         parts = [part.astype(jnp.float32) for value in sums for part in split(value)]
         parts.append(jnp.zeros((group, width - share - ends[-1]), jnp.float32))
         out_ref[:group, share:] = jnp.concatenate(parts, axis=1).astype(jnp.bfloat16)
-        out_ref[group:, :share] = routed
-        out_ref[group:, share:] = jnp.zeros((2 * group, width - share), jnp.bfloat16)
-
-
-def final_kernel(sizes, paired, cubed, got_count, input_count, local_experts, *refs):
+        out_ref[group : 2 * group] = near_ref[last].astype(jnp.bfloat16)
+        out_ref[2 * group :] = far_ref[last]
+
+
+def ready_kernel(sizes, paired, cubed, own_ref, slope_ref, *refs):
+    if cubed:
+        mine_ref, slope_rows_ref, place_ref = refs
+    else:
+        input_refs, (mine_ref, slope_rows_ref, place_ref, inputs_ref) = refs[:-4], refs[-4:]
+    group, expert_total, _, _ = sizes
+    tokens = slope_ref.shape[0]
+    count = tokens // group
+    dp_count = lax.axis_size("dp")
+    dp_me, me = lax.axis_index("dp"), lax.axis_index("expert")
+    own_tokens = group // dp_count
+    local_experts = expert_total // count
+    row, token = iota((tokens, tokens), 1), iota((tokens, tokens), 0)
+    if cubed:
+        block, piece = lax.div(row, group), lax.div(lax.rem(row, group), own_tokens)
+    else:
+        each = count * own_tokens
+        block, piece = lax.div(lax.rem(row, each), own_tokens), lax.div(row, each)
+    source = block * group + place_of(piece, dp_me, paired) * own_tokens + lax.rem(row, own_tokens)
+    to_row = (token == source).astype(jnp.float32)
+    pick = (iota((8, LANES), 0) == iota((8, LANES), 1)).astype(jnp.float32)
+    mine = lax.dot_general(
+        pick, own_ref[...], ROWS_ROWS, precision=HIGH, preferred_element_type=jnp.float32
+    )
+    expert = me * local_experts + place_of(iota((8, expert_total), 0), dp_me, paired)
+    pick = (iota((8, expert_total), 1) == expert).astype(jnp.float32)
+    slopes = lax.dot_general(
+        pick, slope_ref[...], ROWS_ROWS, precision=HIGH, preferred_element_type=jnp.float32
+    )
+    both = jnp.concatenate([route_scale * mine, slopes], axis=0)
+    both = jnp.dot(both, to_row, precision=HIGH, preferred_element_type=jnp.float32)
+    mine_ref[...] = both[:8]
+    slope_rows_ref[...] = both[8:]
+    group_at = group_of(lax.div(iota((count, tokens), 1), group), count, cubed)
+    to_group = (group_at == iota((count, tokens), 0)).astype(jnp.float32)
+    place_ref[:count] = jnp.dot(to_group, to_row, preferred_element_type=jnp.float32)
+    in_group = lax.rem(iota((group, tokens), 1), group) == iota((group, tokens), 0)
+    place_ref[count:] = jnp.dot(
+        in_group.astype(jnp.float32), to_row, preferred_element_type=jnp.float32
+    )
+    if not cubed:
+        parts = [ref[...].astype(jnp.float32) for ref in input_refs]
+        inputs_ref[...] = jnp.concatenate(parts, axis=0).astype(jnp.bfloat16)
+
+
+def final_kernel(sizes, paired, cubed, got_count, local_experts, *refs):
     got_refs, rest = refs[:got_count], refs[got_count:]
-    input_refs, rest = rest[:input_count], rest[input_count:]
-    own_ref, slope_ref, weight_ref, input_far, router_far, input_ref, router_ref, sems = rest
+    mine_ref, slope_rows_ref, place_ref, *input_refs, slope_ref, weight_ref = rest[:-5]
+    rest = rest[-5:]
+    input_far, router_far, input_ref, router_ref, sems = rest
     group, expert_total, _, _ = sizes
     tokens = slope_ref.shape[0]
     count = tokens // group
     share = router_ref.shape[1]
-    dp_count = lax.axis_size("dp")
     dp_me, me = lax.axis_index("dp"), lax.axis_index("expert")
     if cubed:
         sources = [(ref[:group], lax.bitwise_xor(me, 2 * b)) for b, ref in enumerate(got_refs)]
+        parts = [
+            ref[half * group : (half + 1) * group, :share].astype(jnp.float32)
+            for half in (1, 2)
+            for ref in got_refs
+        ]
+        inputs = jnp.concatenate(parts, axis=0).astype(jnp.bfloat16)
     else:
         sources = [(got_refs[0][j], j) for j in range(count)]
+        inputs = input_refs[0][...]
+    sums = jnp.zeros((group, 2 * count), jnp.float32)
+    for got, _ in sources:
+        sums = sums + got[:, share : share + 2 * count].astype(jnp.float32)
+    mixture = sums[:, :count] + sums[:, count:]
+    wide = jnp.dot(
+        mixture, place_ref[:count], precision=HIGH, preferred_element_type=jnp.float32
+    )
+    row_mixture = jnp.sum(wide * place_ref[count:], axis=0, keepdims=True)
+    lines = slope_rows_ref[...] * (mine_ref[...] - row_mixture)
+    grads = jnp.dot(
+        lines.astype(jnp.bfloat16), inputs, preferred_element_type=jnp.float32
+    )
+    for e in range(local_experts):
+        place = place_of(e, dp_me, paired)
+        router_ref[pl.ds(place, 1)] = grads[e : e + 1]
+    last = pltpu.make_async_copy(router_ref, router_far, sems.at[1])
+    last.start()
     mixed = jnp.zeros((group, share), jnp.float32)
-    sums = jnp.zeros((group, 2 * count), jnp.float32)
     given = jnp.zeros((group, expert_total), jnp.float32)
     part = (4 * local_experts, expert_total)
     place = lax.rem(iota(part, 0), 2 * local_experts)
     order = place_of(lax.rem(place, local_experts), dp_me, paired)
     for got, source in sources:
         mixed = mixed + got[:, :share].astype(jnp.float32)
-        sums = sums + got[:, share : share + 2 * count].astype(jnp.float32)
         first = (source - lax.rem(source, 2) + lax.div(place, local_experts)) * local_experts
         to_expert = (iota(part, 1) == first + order).astype(jnp.bfloat16)
         shares = got[:, share + 2 * count : share + 2 * count + 4 * local_experts]
         given = given + jnp.dot(shares, to_expert, preferred_element_type=jnp.float32)
-    mixture = sums[:, :count] + sums[:, count:]
-    choose = (iota((tokens, group), 1) == lax.rem(iota((tokens, group), 0), group)).astype(jnp.float32)
-    wide = jnp.dot(choose, mixture, precision=HIGH, preferred_element_type=jnp.float32)
-    row_group = group_of(lax.div(iota((tokens, count), 0), group), count, cubed)
-    all_mixture = jnp.sum(
-        jnp.where(row_group == iota((tokens, count), 1), wide, 0.0), axis=1, keepdims=True
-    )
     my_mixture = jnp.sum(
         jnp.where(iota((group, count), 1) == me, mixture, 0.0), axis=1, keepdims=True
     )
-    slope = slope_ref[...]
-    if cubed:
-        my_slope = slope[:group]
+    if cubed:
+        my_slope = slope_ref[:group, :]
     else:
         my_slope = slope_ref[pl.ds(pl.multiple_of(me * group, group), group), :]
     my_grad = (my_slope * (route_scale * given - my_mixture)).astype(jnp.bfloat16)
@@ -315,42 +402,8 @@
     input_ref[0] = (mixed + routed).astype(jnp.bfloat16)
     store = pltpu.make_async_copy(input_ref, input_far, sems.at[0])
     store.start()
-    part = (LANES, expert_total)
-    order = place_of(iota(part, 0), dp_me, paired)
-    to_expert = (
-        (iota(part, 1) == me * local_experts + order) & (iota(part, 0) < local_experts)
-    ).astype(jnp.float32)
-    mine = jnp.dot(own_ref[...], to_expert, precision=HIGH, preferred_element_type=jnp.float32)
-    grads = (slope * (route_scale * mine - all_mixture)).astype(jnp.bfloat16)
-    pick = (
-        iota((8, expert_total), 1) == me * local_experts + iota((8, expert_total), 0)
-    ).astype(jnp.bfloat16)
-    lines = lax.dot_general(pick, grads, ROWS_ROWS, preferred_element_type=jnp.float32)
-    row, token = iota((tokens, tokens), 1), iota((tokens, tokens), 0)
-    own_tokens = group // dp_count
-    within = lax.rem(row, group)
-    source = lax.div(row, group) * group + (
-        place_of(lax.div(within, own_tokens), dp_me, paired) * own_tokens
-    ) + lax.rem(within, own_tokens)
-    lines = jnp.dot(
-        lines.astype(jnp.bfloat16),
-        (token == source).astype(jnp.bfloat16),
-        preferred_element_type=jnp.float32,
-    ).astype(jnp.bfloat16)
-    if cubed:
-        parts = [
-            ref[half * group : (half + 1) * group, :share].astype(jnp.float32)
-            for half in (1, 2)
-            for ref in got_refs
-        ]
-        inputs = jnp.concatenate(parts, axis=0).astype(jnp.bfloat16)
-    else:
-        inputs = input_refs[0][...]
-    router_ref[...] = jnp.dot(lines, inputs, preferred_element_type=jnp.float32)[:local_experts]
-    last = pltpu.make_async_copy(router_ref, router_far, sems.at[1])
-    last.start()
+    last.wait()
     store.wait()
-    last.wait()
 
 
 def local(
@@ -377,7 +430,7 @@
     aux = -(-(3 * expert_total + top) // LANES) * LANES
     bf16, f32 = jnp.bfloat16, jnp.float32
     paired = dp_count == local_experts and dp_count & (dp_count - 1) == 0
-    cubed = paired and expert_count == 8
+    cubed = paired and dp_count == 4 and expert_count == 8
     sizes = (group, expert_total, top, depth)
     own_tokens = router_input.shape[1]
 
@@ -392,25 +445,32 @@
         joined = jnp.concatenate(parts, axis=0)
         return parts + [swap(joined, "expert", 1)]
 
-    packed = call(
-        functools.partial(pack_kernel, expert_total),
-        ((group, aux + share), bf16),
-        (router_logits, expert_ids, grad_output),
+    if cubed:
+        pack_shapes = ((group, aux + share),) + tuple((n * own_tokens, share) for n in (1, 2, 1))
+    else:
+        pack_shapes = ((2 * group, aux + share),)
+    packed, *pieces = call(
+        functools.partial(pack_kernel, expert_total, cubed),
+        tuple((shape, bf16) for shape in pack_shapes),
+        (router_logits, expert_ids, grad_output, router_input),
         scratch=(
             VMEM(router_logits.shape, f32),
             VMEM(expert_ids.shape, jnp.int32),
             VMEM(grad_output.shape, bf16),
-            pltpu.SemaphoreType.DMA((3,)),
+            VMEM(router_input.shape, bf16),
+            pltpu.SemaphoreType.DMA((4,)),
         ),
         flops=4 * 10**10,
         far_args=True,
     )
+    if cubed:
+        pieces[1] = swap(pieces[1], "dp", 1)
     token_parts = gather(packed)
-    raw = [router_input] + ([swap(router_input, "expert", 1)] if cubed else [])
     sends = call(
         functools.partial(down_kernel, sizes, aux, paired, cubed, len(token_parts)),
         (((slots, hidden_size), bf16),) * local_experts,
         (*token_parts, down_weight.swapaxes(1, 2)),
+        scratch=(VMEM((2, tokens, hidden_size), bf16),),
     )
     if paired:
         parts = [sends[0]] + [swap(sends[k], "dp", k) for k in range(1, dp_count)]
@@ -418,22 +478,18 @@
         all_sends = jnp.concatenate(sends, axis=0).reshape(dp_count, piece, hidden_size)
         parts = list(lax.all_to_all(all_sends, "dp", 0, 0, tiled=True))
     if cubed:
-        piece_shapes = (((2 * own_tokens, share), bf16),) * dp_count
-    else:
-        piece_shapes = (((dp_count, own_tokens, share), bf16),)
-    full, slope, *pieces = call(
-        functools.partial(
-            table_kernel, sizes, aux, local_experts, paired, cubed, len(token_parts), len(raw)
-        ),
-        (((tokens, rows), f32), ((tokens, expert_total), f32), *piece_shapes),
-        (*token_parts, *raw),
-    )
-    if cubed:
-        pieces = [pieces[0]] + [swap(pieces[k], "dp", k) for k in range(1, dp_count)]
-        inputs = []
-    else:
-        inputs = lax.all_to_all(pieces[0], "dp", 0, 0, tiled=True).reshape(group, share)
-        inputs = gather(inputs)
+        piece_shape = (2 * own_tokens, share)
+    else:
+        piece_shape = (dp_count, expert_count * own_tokens, share)
+    full, slope, piece_out = call(
+        functools.partial(table_kernel, sizes, aux, local_experts, paired, cubed, len(token_parts)),
+        (((tokens, rows), f32), ((tokens, expert_total), f32), (piece_shape, bf16)),
+        (*token_parts, *((pieces[2], pieces[1]) if cubed else ())),
+    )
+    if cubed:
+        pieces = [pieces[0], pieces[1], swap(piece_out, "dp", 2)]
+    else:
+        pieces = list(lax.all_to_all(piece_out, "dp", 0, 0, tiled=True))
     hidden = sum(part.astype(f32) for part in parts).astype(bf16)
     if paired:
         blocks = [hidden] + [swap(hidden, "dp", k) for k in range(1, dp_count)]
@@ -452,14 +508,14 @@
         )
     width = -(-(share + 2 * expert_count + 4 * local_experts) // LANES) * LANES
     if cubed:
-        half = (expert_count // 2, group, width)
+        half = (expert_count // 2 + 1, group, width)
         mix_shapes = ((half, f32), (half, bf16))
     else:
         mix_shapes = (((expert_count, group, width), bf16),)
     *mixed, own = call(
         functools.partial(mix_kernel, local_experts - 1, group, paired, cubed),
         (*mix_shapes, ((tokens, LANES), f32)),
-        (full, *weights, blocks[-1], *done),
+        (full, *weights, blocks[-1], *(pieces if cubed else ()), *done),
         scratch=(VMEM((rows, share), f32), VMEM((1, lanes), f32)),
     )
     if cubed:
@@ -467,15 +523,25 @@
         sums = call(
             functools.partial(pair_kernel, share, expert_count, local_experts),
             (((3 * group, width), bf16),) * (expert_count // 2),
-            (mixed[0], far, *pieces),
+            (mixed[0], far),
         )
         got = [sums[0]] + [swap(sums[k], "expert", 2 * k) for k in (1, 2, 3)]
     else:
         got = [lax.all_to_all(mixed[0], "expert", 0, 0, tiled=True)]
+    ready = call(
+        functools.partial(ready_kernel, sizes, paired, cubed),
+        (
+            ((8, tokens), f32),
+            ((8, tokens), f32),
+            ((expert_count + group, tokens), f32),
+            *(() if cubed else (((tokens, share), bf16),)),
+        ),
+        (own, slope, *(() if cubed else pieces)),
+    )
     grad_input, grad_router = call(
-        functools.partial(final_kernel, sizes, paired, cubed, len(got), len(inputs), local_experts),
+        functools.partial(final_kernel, sizes, paired, cubed, len(got), local_experts),
         (((1, group, share), bf16), ((local_experts, share), f32)),
-        (*got, *inputs, own, slope, router_weight),
+        (*got, *ready, slope, router_weight),
         scratch=(
             VMEM((1, group, share), bf16),
             VMEM((local_experts, share), f32),

time: 51.2 us -> 48 us (0.938)
  starting transfers between devices: 21.7 us -> 17.3 us
  waiting for transfers between devices: 18 us -> 19.5 us
    ppermute x18 -> x16, starting transfers between devices: 21.7 us -> 17.3 us  [swap(): return lax.ppermute(value, axis, [(j, j ^ k) for j in range(count)])]
    ppermute x18 -> x16, waiting for transfers between devices: 18 us -> 19.5 us  [swap(): return lax.ppermute(value, axis, [(j, j ^ k) for j in range(count)])]
    pallas_call x9 -> x10, Pallas kernels: 10.5 us -> 10.2 us  [call(): pl.pallas_call(kernel, out_shape=tuple((space(*out) for out in outs)) if...]
  transfers between devices with their start and end apart: 18 -> 16, of which waited for: 12 -> 12; matrix products, arithmetic and copies ran while one was open for 0% -> 0% of each run, Pallas kernels for 8% -> 9%
where the time goes in v4:
time: 48 us; the launch traced here: 47.7 us
  waiting for transfers between devices  19.5 us (41%)
  starting transfers between devices  17.3 us (36%)
  Pallas kernels  10.2 us (21%)
  between operations  0.74 us (2%)
    ppermute x16, waiting for transfers between devices, swap(): return lax.ppermute(value, axis, [(j, j ^ k) for j in range(count)])  19.5 us
    ppermute x16, starting transfers between devices, swap(): return lax.ppermute(value, axis, [(j, j ^ k) for j in range(count)])  17.3 us
    pallas_call x10, Pallas kernels, call(): pl.pallas_call(kernel, out_shape=tuple((space(*out) for out in outs)) if...  10.2 us
  transfers between devices with their start and end apart: 16, of which 12 were waited for; matrix products, arithmetic and copies ran while one was open for 0% of the time, Pallas kernels for 9%

profile of v4, /device:TPU:0, one launch (start us, length us, event | category | flops | bytes accessed | tf_op | source)
XLA Modules:
  0.0 47.7 jit_solution(10991040044398918069)
XLA Ops:
  0.7 1.0 %shard_map.113 = (bf16[8,1088]{1,0:T(8,128)(2,1)S(1)}, bf16[2,960]{1,0:T(2,128)(2,1)S(1)}, bf16[4,960]{1,0:T(4,128)(2,1)S(1)}, bf16[2,960]{1,0:T(2,128)(2,1)S(1)}) custom-call(f32[1,8,32]{2,1,0:T(8,128)} %refs_0_.5, s32[1,8,8]{2,1,0:T(8,128)} %refs_1_.5, bf16[1,8,960]{2,1,0:T(8,128)(2,1)} %refs_2_.5, bf16[1,2,3840]{2,1,0:T(2,128)(2,1)} %refs_3_.5), custom_call_target="tpu_custom_call" | custom-call | flops 40000000000 | tf_op jit(solution)/shard_map/pallas_call | solution.py:31
  1.7 4.0 %collective-permute-start.2 = (bf16[8,1088]{1,0:T(8,128)(2,1)S(1)}, bf16[8,1088]{1,0:T(8,128)(2,1)S(1)}, u32[]{:S(2)}, u32[]{:S(2)}) collective-permute-start(bf16[8,1088]{1,0:T(8,128)(2,1)S(1)} %get-tuple-element.29.refs_0_), channel_id=1, source_target_pairs={{0,6},{1,7},{2,4},{3,5},{4,2},{5,3},{6,0},{7,1},{8,14},{9,15},{10,... | collective-permute-start | bytes 52232 | tf_op jit(solution)/shard_map/ppermute | solution.py:439
  6.4 1.1 %collective-permute-done.2.refs_3_ = bf16[8,1088]{1,0:T(8,128)(2,1)S(1)} collective-permute-done((bf16[8,1088]{1,0:T(8,128)(2,1)S(1)}, bf16[8,1088]{1,0:T(8,128)(2,1)S(1)}, u32[]{:S(2)}, u32[]{:S(2)}) %collective-permute-start.2) | collective-permute-done | bytes 17440 | tf_op jit(solution)/shard_map/ppermute | solution.py:439
  7.5 2.0 %collective-permute-done.1.refs_2_ = bf16[8,1088]{1,0:T(8,128)(2,1)S(1)} collective-permute-done((bf16[8,1088]{1,0:T(8,128)(2,1)S(1)}, bf16[8,1088]{1,0:T(8,128)(2,1)S(1)}, u32[]{:S(2)}, u32[]{:S(2)}) %collective-permute-start.1) | collective-permute-done | bytes 17440 | tf_op jit(solution)/shard_map/ppermute | solution.py:439
  10.1 1.3 %collective-permute-done.3.refs_4_ = bf16[32,1088]{1,0:T(8,128)(2,1)S(1)} collective-permute-done((bf16[32,1088]{1,0:T(8,128)(2,1)S(1)}, bf16[32,1088]{1,0:T(8,128)(2,1)S(1)}, u32[]{:S(2)}, u32[]{:S(2)}) %collective-permute-start.3) | collective-permute-done | bytes 69664 | tf_op jit(solution)/shard_map/ppermute | solution.py:439
  11.3 1.7 %shard_map.115 = (bf16[24,1024]{1,0:T(8,128)(2,1)S(1)}, bf16[24,1024]{1,0:T(8,128)(2,1)S(1)}, bf16[24,1024]{1,0:T(8,128)(2,1)S(1)}, bf16[24,1024]{1,0:T(8,128)(2,1)S(1)}) custom-call(bf16[8,1088]{1,0:T(8,128)(2,1)S(1)} %get-tuple-element.29.refs_0_, bf16[8,1088]{1,0:T(8,128)(2,1)S(1)} %collective-permute-done.refs_1_, ...), custom_call_target="tpu_custom_call" | custom-call | tf_op jit(solution)/shard_map/pallas_call | solution.py:31
  13.1 1.6 %collective-permute-start.5 = (bf16[24,1024]{1,0:T(8,128)(2,1)S(1)}, bf16[24,1024]{1,0:T(8,128)(2,1)S(1)}, u32[]{:S(2)}, u32[]{:S(2)}) collective-permute-start(bf16[24,1024]{1,0:T(8,128)(2,1)S(1)} %get-tuple-element.34), channel_id=1, source_target_pairs={{0,8},{8,0},{16,24},{24,16},{1,9},{9,1},{17,25},{25,17},{2,10},{10... | collective-permute-start | bytes 147464 | tf_op jit(solution)/shard_map/ppermute | solution.py:439
  14.6 2.6 %collective-permute-start.6 = (bf16[24,1024]{1,0:T(8,128)(2,1)S(1)}, bf16[24,1024]{1,0:T(8,128)(2,1)S(1)}, u32[]{:S(2)}, u32[]{:S(2)}) collective-permute-start(bf16[24,1024]{1,0:T(8,128)(2,1)S(1)} %get-tuple-element.35), channel_id=1, source_target_pairs={{0,16},{8,24},{16,0},{24,8},{1,17},{9,25},{17,1},{25,9},{2,18},{10... | collective-permute-start | bytes 147464 | tf_op jit(solution)/shard_map/ppermute | solution.py:439
  17.5 3.0 %collective-permute-done.6 = bf16[24,1024]{1,0:T(8,128)(2,1)S(1)} collective-permute-done((bf16[24,1024]{1,0:T(8,128)(2,1)S(1)}, bf16[24,1024]{1,0:T(8,128)(2,1)S(1)}, u32[]{:S(2)}, u32[]{:S(2)}) %collective-permute-start.6) | collective-permute-done | bytes 49184 | tf_op jit(solution)/shard_map/ppermute | solution.py:439
  20.5 2.6 %collective-permute-done.7 = bf16[24,1024]{1,0:T(8,128)(2,1)S(1)} collective-permute-done((bf16[24,1024]{1,0:T(8,128)(2,1)S(1)}, bf16[24,1024]{1,0:T(8,128)(2,1)S(1)}, u32[]{:S(2)}, u32[]{:S(2)}) %collective-permute-start.7) | collective-permute-done | bytes 49184 | tf_op jit(solution)/shard_map/ppermute | solution.py:439
  23.1 0.7 %collective-permute-start.11 = (bf16[24,1024]{1,0:T(8,128)(2,1)S(1)}, bf16[24,1024]{1,0:T(8,128)(2,1)S(1)}, u32[]{:S(2)}, u32[]{:S(2)}) collective-permute-start(bf16[24,1024]{1,0:T(8,128)(2,1)S(1)} %add_convert_fusion.refs_4_), channel_id=1, source_target_pairs={{0,16},{8,24},{16,0},{24,8},{1,17},{9,25},{17,1},{25,9},{2,18},{10... | collective-permute-start | bytes 147464 | tf_op jit(solution)/shard_map/ppermute | solution.py:439
  23.9 0.9 %collective-permute-start.10 = (bf16[24,1024]{1,0:T(8,128)(2,1)S(1)}, bf16[24,1024]{1,0:T(8,128)(2,1)S(1)}, u32[]{:S(2)}, u32[]{:S(2)}) collective-permute-start(bf16[24,1024]{1,0:T(8,128)(2,1)S(1)} %add_convert_fusion.refs_4_), channel_id=1, source_target_pairs={{0,8},{8,0},{16,24},{24,16},{1,9},{9,1},{17,25},{25,17},{2,10},{10... | collective-permute-start | bytes 147464 | tf_op jit(solution)/shard_map/ppermute | solution.py:439
  24.8 2.8 %collective-permute-start.8 = (bf16[24,1024]{1,0:T(8,128)(2,1)S(1)}, bf16[24,1024]{1,0:T(8,128)(2,1)S(1)}, u32[]{:S(2)}, u32[]{:S(2)}) collective-permute-start(bf16[24,1024]{1,0:T(8,128)(2,1)S(1)} %add_convert_fusion.refs_4_), channel_id=1, source_target_pairs={{0,24},{8,16},{16,8},{24,0},{1,25},{9,17},{17,9},{25,1},{2,26},{10... | collective-permute-start | bytes 147464 | tf_op jit(solution)/shard_map/ppermute | solution.py:439
  27.6 3.6 %collective-permute-done.4.refs_6_ = bf16[4,960]{1,0:T(4,128)(2,1)S(1)} collective-permute-done((bf16[4,960]{1,0:T(4,128)(2,1)S(1)}, bf16[4,960]{1,0:T(4,128)(2,1)S(1)}, u32[]{:S(2)}, u32[]{:S(2)}) %collective-permute-start.4) | collective-permute-done | bytes 7712 | tf_op jit(solution)/shard_map/ppermute | solution.py:439
  31.9 1.2 %shard_map.116 = (f32[24,960]{1,0:T(8,128)S(1)}, f32[1,128]{1,0:T(1,128)S(1)}) custom-call(bf16[4,960,1024]{2,1,0:T(8,128)(2,1)S(1)} %copy-done, bf16[4,960,1024]{2,1,0:T(8,128)(2,1)S(1)} %copy-done.1, bf16[4,24,1024]{2,1,0:T(8,128)(2,1)S(1)} %copy-done.3, bf16[4,24,1024]{2,1,0:T(8,128)(2,1)S(1)} %copy-done.4, bf16[24,1024]{1,0:T(8,128)(2,1)S(1)} %add_convert_fusion.refs_4_), custom_call_target="tpu_custom_call" | custom-call | tf_op jit(solution)/shard_map/pallas_call | solution.py:31
  33.1 1.2 %shard_map.118 = (f32[24,960]{1,0:T(8,128)S(1)}, f32[1,128]{1,0:T(1,128)S(1)}) custom-call(bf16[4,960,1024]{2,1,0:T(8,128)(2,1)S(1)} %copy-done, bf16[4,960,1024]{2,1,0:T(8,128)(2,1)S(1)} %copy-done.1, bf16[4,24,1024]{2,1,0:T(8,128)(2,1)S(1)} %copy-done.3, bf16[4,24,1024]{2,1,0:T(8,128)(2,1)S(1)} %copy-done.4, ...), custom_call_target="tpu_custom_call" | custom-call | tf_op jit(solution)/shard_map/pallas_call | solution.py:31
  34.4 1.2 %shard_map.117 = (f32[24,960]{1,0:T(8,128)S(1)}, f32[1,128]{1,0:T(1,128)S(1)}) custom-call(bf16[4,960,1024]{2,1,0:T(8,128)(2,1)S(1)} %copy-done, bf16[4,960,1024]{2,1,0:T(8,128)(2,1)S(1)} %copy-done.1, bf16[4,24,1024]{2,1,0:T(8,128)(2,1)S(1)} %copy-done.3, bf16[4,24,1024]{2,1,0:T(8,128)(2,1)S(1)} %copy-done.4, ...), custom_call_target="tpu_custom_call" | custom-call | tf_op jit(solution)/shard_map/pallas_call | solution.py:31
  35.6 0.8 %collective-permute-done.9.refs_7_ = bf16[4,960]{1,0:T(4,128)(2,1)S(1)} collective-permute-done((bf16[4,960]{1,0:T(4,128)(2,1)S(1)}, bf16[4,960]{1,0:T(4,128)(2,1)S(1)}, u32[]{:S(2)}, u32[]{:S(2)}) %collective-permute-start.9) | collective-permute-done | bytes 7712 | tf_op jit(solution)/shard_map/ppermute | solution.py:439
  36.4 1.5 %shard_map.119 = (f32[5,8,1024]{2,1,0:T(8,128)S(1)}, bf16[5,8,1024]{2,1,0:T(8,128)(2,1)S(1)}, f32[64,128]{1,0:T(8,128)S(1)}) custom-call(f32[64,96]{1,0:T(8,128)S(1)} %get-tuple-element.32.full_ref, bf16[4,960,1024]{2,1,0:T(8,128)(2,1)S(1)} %copy-done, bf16[4,960,1024]{2,1,0:T(8,128)(2,1)S(1)} %copy-done.1, bf16[4,24,1024]{2,1,0:T(8,128)(2,1)S(1)} %copy-done.3, ...), custom_call_target="tpu_custom_call" | custom-call | tf_op jit(solution)/shard_map/pallas_call | solution.py:31
  38.0 1.3 %collective-permute-done.12.far_ref = bf16[5,8,1024]{2,1,0:T(8,128)(2,1)S(1)} collective-permute-done((bf16[5,8,1024]{2,1,0:T(8,128)(2,1)S(1)}, bf16[5,8,1024]{2,1,0:T(8,128)(2,1)S(1)}, u32[]{:S(2)}, u32[]{:S(2)}) %collective-permute-start.12) | collective-permute-done | bytes 81952 | tf_op jit(solution)/shard_map/ppermute | solution.py:439
  40.0 1.5 %collective-permute-start.14 = (bf16[24,1024]{1,0:T(8,128)(2,1)S(1)}, bf16[24,1024]{1,0:T(8,128)(2,1)S(1)}, u32[]{:S(2)}, u32[]{:S(2)}) collective-permute-start(bf16[24,1024]{1,0:T(8,128)(2,1)S(1)} %get-tuple-element.49), channel_id=1, source_target_pairs={{0,4},{1,5},{2,6},{3,7},{4,0},{5,1},{6,2},{7,3},{8,12},{9,13},{10,... | collective-permute-start | bytes 147464 | tf_op jit(solution)/shard_map/ppermute | solution.py:439
  41.6 1.4 %collective-permute-start.15 = (bf16[24,1024]{1,0:T(8,128)(2,1)S(1)}, bf16[24,1024]{1,0:T(8,128)(2,1)S(1)}, u32[]{:S(2)}, u32[]{:S(2)}) collective-permute-start(bf16[24,1024]{1,0:T(8,128)(2,1)S(1)} %get-tuple-element.50), channel_id=1, source_target_pairs={{0,6},{1,7},{2,4},{3,5},{4,2},{5,3},{6,0},{7,1},{8,14},{9,15},{10,... | collective-permute-start | bytes 147464 | tf_op jit(solution)/shard_map/ppermute | solution.py:439
  44.1 2.4 %collective-permute-done.15.refs_3_ = bf16[24,1024]{1,0:T(8,128)(2,1)S(1)} collective-permute-done((bf16[24,1024]{1,0:T(8,128)(2,1)S(1)}, bf16[24,1024]{1,0:T(8,128)(2,1)S(1)}, u32[]{:S(2)}, u32[]{:S(2)}) %collective-permute-start.15) | collective-permute-done | bytes 49184 | tf_op jit(solution)/shard_map/ppermute | solution.py:439
  46.6 1.2 %shard_map.122 = (bf16[1,8,960]{2,1,0:T(8,128)(2,1)}, f32[4,960]{1,0:T(4,128)}) custom-call(bf16[24,1024]{1,0:T(8,128)(2,1)S(1)} %get-tuple-element.47.refs_0_, bf16[24,1024]{1,0:T(8,128)(2,1)S(1)} %collective-permute-done.13.refs_1_, bf16[24,1024]{1,0:T(8,128)(2,1)S(1)} %collective-permute-done.14.refs_2_, ...), custom_call_target="tpu_custom_call" | custom-call | tf_op jit(solution)/shard_map/pallas_call | solution.py:31
  (32 shorter events, 4.2 us)
Async XLA Ops:
  0.6 10.7 %copy-start.2 = (bf16[4,1024,960]{1,2,0:T(8,128)(2,1)S(1)}, bf16[4,1024,960]{1,2,0:T(8,128)(2,1)}, u32[]{:S(2)}) copy-start(bf16[4,1024,960]{1,2,0:T(8,128)(2,1)} %param.17) | copy-start | bytes 23592964
  0.6 31.3 %copy-start.1 = (bf16[4,960,1024]{2,1,0:T(8,128)(2,1)S(1)}, bf16[4,960,1024]{2,1,0:T(8,128)(2,1)}, u32[]{:S(2)}) copy-start(bf16[4,960,1024]{2,1,0:T(8,128)(2,1)} %refs_1_.9) | copy-start | bytes 23592964
  1.7 30.2 %copy-start = (bf16[4,960,1024]{2,1,0:T(8,128)(2,1)S(1)}, bf16[4,960,1024]{2,1,0:T(8,128)(2,1)}, u32[]{:S(2)}) copy-start(bf16[4,960,1024]{2,1,0:T(8,128)(2,1)} %refs_0_.9) | copy-start | bytes 23592964
  1.7 30.2 %copy-start.3 = (bf16[4,24,1024]{2,1,0:T(8,128)(2,1)S(1)}, bf16[4,24,1024]{2,1,0:T(8,128)(2,1)}, u32[]{:S(2)}) copy-start(bf16[4,24,1024]{2,1,0:T(8,128)(2,1)} %refs_2_.9) | copy-start | bytes 589828
  1.7 30.2 %copy-start.4 = (bf16[4,24,1024]{2,1,0:T(8,128)(2,1)S(1)}, bf16[4,24,1024]{2,1,0:T(8,128)(2,1)}, u32[]{:S(2)}) copy-start(bf16[4,24,1024]{2,1,0:T(8,128)(2,1)} %refs_3_.9) | copy-start | bytes 589828
  1.7 5.7 %collective-permute-start.2 = (bf16[8,1088]{1,0:T(8,128)(2,1)S(1)}, bf16[8,1088]{1,0:T(8,128)(2,1)S(1)}, u32[]{:S(2)}, u32[]{:S(2)}) collective-permute-start(bf16[8,1088]{1,0:T(8,128)(2,1)S(1)} %get-tuple-element.29.refs_0_), channel_id=1, source_target_pairs={{0,6},{1,7},{2,4},{3,5},{4,2},{5,3},{6,0},{7,1},{8,14},{9,15},{10,... | collective-permute-start | bytes 52232 | tf_op jit(solution)/shard_map/ppermute | solution.py:439
  5.7 3.8 %collective-permute-start.1 = (bf16[8,1088]{1,0:T(8,128)(2,1)S(1)}, bf16[8,1088]{1,0:T(8,128)(2,1)S(1)}, u32[]{:S(2)}, u32[]{:S(2)}) collective-permute-start(bf16[8,1088]{1,0:T(8,128)(2,1)S(1)} %get-tuple-element.29.refs_0_), channel_id=1, source_target_pairs={{0,4},{1,5},{2,6},{3,7},{4,0},{5,1},{6,2},{7,3},{8,12},{9,13},{10,... | collective-permute-start | bytes 52232 | tf_op jit(solution)/shard_map/ppermute | solution.py:439
  6.2 3.8 %collective-permute-start = (bf16[8,1088]{1,0:T(8,128)(2,1)S(1)}, bf16[8,1088]{1,0:T(8,128)(2,1)S(1)}, u32[]{:S(2)}, u32[]{:S(2)}) collective-permute-start(bf16[8,1088]{1,0:T(8,128)(2,1)S(1)} %get-tuple-element.29.refs_0_), channel_id=1, source_target_pairs={{0,2},{1,3},{2,0},{3,1},{4,6},{5,7},{6,4},{7,5},{8,10},{9,11},{10,... | collective-permute-start | bytes 52232 | tf_op jit(solution)/shard_map/ppermute | solution.py:439
  10.0 1.3 %collective-permute-start.3 = (bf16[32,1088]{1,0:T(8,128)(2,1)S(1)}, bf16[32,1088]{1,0:T(8,128)(2,1)S(1)}, u32[]{:S(2)}, u32[]{:S(2)}) collective-permute-start(bf16[32,1088]{1,0:T(8,128)(2,1)S(1)} %pad_maximum_fusion), channel_id=1, source_target_pairs={{0,1},{1,0},{2,3},{3,2},{4,5},{5,4},{6,7},{7,6},{8,9},{9,8},{10,11... | collective-permute-start | bytes 208904 | tf_op jit(solution)/shard_map/ppermute | solution.py:439
  13.1 4.4 %collective-permute-start.5 = (bf16[24,1024]{1,0:T(8,128)(2,1)S(1)}, bf16[24,1024]{1,0:T(8,128)(2,1)S(1)}, u32[]{:S(2)}, u32[]{:S(2)}) collective-permute-start(bf16[24,1024]{1,0:T(8,128)(2,1)S(1)} %get-tuple-element.34), channel_id=1, source_target_pairs={{0,8},{8,0},{16,24},{24,16},{1,9},{9,1},{17,25},{25,17},{2,10},{10... | collective-permute-start | bytes 147464 | tf_op jit(solution)/shard_map/ppermute | solution.py:439
  14.6 5.9 %collective-permute-start.6 = (bf16[24,1024]{1,0:T(8,128)(2,1)S(1)}, bf16[24,1024]{1,0:T(8,128)(2,1)S(1)}, u32[]{:S(2)}, u32[]{:S(2)}) collective-permute-start(bf16[24,1024]{1,0:T(8,128)(2,1)S(1)} %get-tuple-element.35), channel_id=1, source_target_pairs={{0,16},{8,24},{16,0},{24,8},{1,17},{9,25},{17,1},{25,9},{2,18},{10... | collective-permute-start | bytes 147464 | tf_op jit(solution)/shard_map/ppermute | solution.py:439
  17.2 5.9 %collective-permute-start.7 = (bf16[24,1024]{1,0:T(8,128)(2,1)S(1)}, bf16[24,1024]{1,0:T(8,128)(2,1)S(1)}, u32[]{:S(2)}, u32[]{:S(2)}) collective-permute-start(bf16[24,1024]{1,0:T(8,128)(2,1)S(1)} %get-tuple-element.36), channel_id=1, source_target_pairs={{0,24},{8,16},{16,8},{24,0},{1,25},{9,17},{17,9},{25,1},{2,26},{10... | collective-permute-start | bytes 147464 | tf_op jit(solution)/shard_map/ppermute | solution.py:439
  23.1 10.0 %collective-permute-start.11 = (bf16[24,1024]{1,0:T(8,128)(2,1)S(1)}, bf16[24,1024]{1,0:T(8,128)(2,1)S(1)}, u32[]{:S(2)}, u32[]{:S(2)}) collective-permute-start(bf16[24,1024]{1,0:T(8,128)(2,1)S(1)} %add_convert_fusion.refs_4_), channel_id=1, source_target_pairs={{0,16},{8,24},{16,0},{24,8},{1,17},{9,25},{17,1},{25,9},{2,18},{10... | collective-permute-start | bytes 147464 | tf_op jit(solution)/shard_map/ppermute | solution.py:439
  23.9 10.5 %collective-permute-start.10 = (bf16[24,1024]{1,0:T(8,128)(2,1)S(1)}, bf16[24,1024]{1,0:T(8,128)(2,1)S(1)}, u32[]{:S(2)}, u32[]{:S(2)}) collective-permute-start(bf16[24,1024]{1,0:T(8,128)(2,1)S(1)} %add_convert_fusion.refs_4_), channel_id=1, source_target_pairs={{0,8},{8,0},{16,24},{24,16},{1,9},{9,1},{17,25},{25,17},{2,10},{10... | collective-permute-start | bytes 147464 | tf_op jit(solution)/shard_map/ppermute | solution.py:439
  24.8 11.6 %collective-permute-start.8 = (bf16[24,1024]{1,0:T(8,128)(2,1)S(1)}, bf16[24,1024]{1,0:T(8,128)(2,1)S(1)}, u32[]{:S(2)}, u32[]{:S(2)}) collective-permute-start(bf16[24,1024]{1,0:T(8,128)(2,1)S(1)} %add_convert_fusion.refs_4_), channel_id=1, source_target_pairs={{0,24},{8,16},{16,8},{24,0},{1,25},{9,17},{17,9},{25,1},{2,26},{10... | collective-permute-start | bytes 147464 | tf_op jit(solution)/shard_map/ppermute | solution.py:439
  27.6 3.7 %collective-permute-start.4 = (bf16[4,960]{1,0:T(4,128)(2,1)S(1)}, bf16[4,960]{1,0:T(4,128)(2,1)S(1)}, u32[]{:S(2)}, u32[]{:S(2)}) collective-permute-start(bf16[4,960]{1,0:T(4,128)(2,1)S(1)} %get-tuple-element.31), channel_id=1, source_target_pairs={{0,8},{8,0},{16,24},{24,16},{1,9},{9,1},{17,25},{25,17},{2,10},{10... | collective-permute-start | bytes 23048 | tf_op jit(solution)/shard_map/ppermute | solution.py:439
  31.7 4.7 %collective-permute-start.9 = (bf16[4,960]{1,0:T(4,128)(2,1)S(1)}, bf16[4,960]{1,0:T(4,128)(2,1)S(1)}, u32[]{:S(2)}, u32[]{:S(2)}) collective-permute-start(bf16[4,960]{1,0:T(4,128)(2,1)S(1)} %get-tuple-element.38), channel_id=1, source_target_pairs={{0,16},{8,24},{16,0},{24,8},{1,17},{9,25},{17,1},{25,9},{2,18},{10... | collective-permute-start | bytes 23048 | tf_op jit(solution)/shard_map/ppermute | solution.py:439
  36.4 10.2 %copy-start.5 = (bf16[32,960]{1,0:T(8,128)(2,1)S(1)}, bf16[32,960]{1,0:T(8,128)(2,1)}, u32[]{:S(2)}) copy-start(bf16[32,960]{1,0:T(8,128)(2,1)} %refs_8_.1) | copy-start | bytes 184324
  37.9 1.3 %collective-permute-start.12 = (bf16[5,8,1024]{2,1,0:T(8,128)(2,1)S(1)}, bf16[5,8,1024]{2,1,0:T(8,128)(2,1)S(1)}, u32[]{:S(2)}, u32[]{:S(2)}) collective-permute-start(bf16[5,8,1024]{2,1,0:T(8,128)(2,1)S(1)} %get-tuple-element.46), channel_id=1, source_target_pairs={{0,1},{1,0},{2,3},{3,2},{4,5},{5,4},{6,7},{7,6},{8,9},{9,8},{10,11... | collective-permute-start | bytes 245768 | tf_op jit(solution)/shard_map/ppermute | solution.py:439
  39.5 4.1 %collective-permute-start.13 = (bf16[24,1024]{1,0:T(8,128)(2,1)S(1)}, bf16[24,1024]{1,0:T(8,128)(2,1)S(1)}, u32[]{:S(2)}, u32[]{:S(2)}) collective-permute-start(bf16[24,1024]{1,0:T(8,128)(2,1)S(1)} %get-tuple-element.48), channel_id=1, source_target_pairs={{0,2},{1,3},{2,0},{3,1},{4,6},{5,7},{6,4},{7,5},{8,10},{9,11},{10,... | collective-permute-start | bytes 147464 | tf_op jit(solution)/shard_map/ppermute | solution.py:439
  40.0 4.1 %collective-permute-start.14 = (bf16[24,1024]{1,0:T(8,128)(2,1)S(1)}, bf16[24,1024]{1,0:T(8,128)(2,1)S(1)}, u32[]{:S(2)}, u32[]{:S(2)}) collective-permute-start(bf16[24,1024]{1,0:T(8,128)(2,1)S(1)} %get-tuple-element.49), channel_id=1, source_target_pairs={{0,4},{1,5},{2,6},{3,7},{4,0},{5,1},{6,2},{7,3},{8,12},{9,13},{10,... | collective-permute-start | bytes 147464 | tf_op jit(solution)/shard_map/ppermute | solution.py:439
  41.6 5.0 %collective-permute-start.15 = (bf16[24,1024]{1,0:T(8,128)(2,1)S(1)}, bf16[24,1024]{1,0:T(8,128)(2,1)S(1)}, u32[]{:S(2)}, u32[]{:S(2)}) collective-permute-start(bf16[24,1024]{1,0:T(8,128)(2,1)S(1)} %get-tuple-element.50), channel_id=1, source_target_pairs={{0,6},{1,7},{2,4},{3,5},{4,2},{5,3},{6,0},{7,1},{8,14},{9,15},{10,... | collective-permute-start | bytes 147464 | tf_op jit(solution)/shard_map/ppermute | solution.py:439

commit v5 on v4

--- a/solution.py
+++ b/solution.py
@@ -42,10 +42,10 @@
 def group_of(block, count, cubed):
     if not cubed:
         return block
-    doubled = 2 * block
-    return lax.bitwise_xor(
-        lax.rem(doubled, count) + lax.div(doubled, count), lax.axis_index("expert")
-    )
+    one = jnp.ones_like(block)
+    row = lax.rem(block, count // 2)
+    offset = lax.bitwise_xor(2 * row + lax.min(row, one), lax.div(block, count // 2))
+    return lax.bitwise_xor(offset, lax.axis_index("expert"))
 
 
 def stacked(refs, stride, first, rows, columns):
@@ -216,20 +216,22 @@
     expert_parts(k, paired, *refs)
 
 
-def mix_kernel(k, group, paired, cubed, full_ref, *refs):
+def mix_kernel(turns, group, paired, cubed, full_ref, *refs):
+    k = turns[-1]
     weights, rest = refs[:5], refs[5:]
     if cubed:
         input_refs, rest = rest[:3], rest[3:]
-    earlier, out_refs, (held_ref, share_ref) = rest[: 2 * k], rest[2 * k : -2], rest[-2:]
+    before = 2 * len(turns) - 2
+    earlier, out_refs, (held_ref, share_ref) = rest[:before], rest[before:-2], rest[-2:]
     slots = weights[4].shape[0]
     expert_parts(k, paired, *weights, held_ref.at[pl.ds(k * slots, slots)], share_ref)
     shares = share_ref[...]
-    for at in range(k):
-        held_ref[at * slots : (at + 1) * slots] = earlier[2 * at][...]
-        shares = shares + earlier[2 * at + 1][...]
+    for turn, at in enumerate(turns[:-1]):
+        held_ref[at * slots : (at + 1) * slots] = earlier[2 * turn][...]
+        shares = shares + earlier[2 * turn + 1][...]
     full = full_ref[...]
     tokens, rows = full.shape
-    local_experts = k + 1
+    local_experts = len(turns)
     count = tokens // group
     share, width = held_ref.shape[1], out_refs[0].shape[2]
     given = shares[:, :rows]
@@ -273,7 +275,10 @@
             out_ref[blocks, :, :share] = routed.astype(out_ref.dtype)
             out_ref[blocks, :, share:] = jnp.zeros((group, width - share), out_ref.dtype)
         for q in range(blocks):
-            lines = slice(at * group, (at + 1) * group)
+            block = at
+            if cubed and at % (count // 2):
+                block = (at + count // 2) % count
+            lines = slice(block * group, (block + 1) * group)
             out_ref[q, :, :share] = mixed[lines].astype(out_ref.dtype)
             out_ref[q, :, share:] = extra[lines].astype(out_ref.dtype)
             at = at + 1
@@ -310,7 +315,9 @@
     local_experts = expert_total // count
     row, token = iota((tokens, tokens), 1), iota((tokens, tokens), 0)
     if cubed:
-        block, piece = lax.div(row, group), lax.div(lax.rem(row, group), own_tokens)
+        place, piece = lax.div(row, group), lax.div(lax.rem(row, group), own_tokens)
+        other = lax.rem(place + count // 2, count)
+        block = jnp.where(lax.rem(place, count // 2) == 0, place, other)
     else:
         each = count * own_tokens
         block, piece = lax.div(lax.rem(row, each), own_tokens), lax.div(row, each)
@@ -438,10 +445,14 @@
         count = lax.axis_size(axis)
         return lax.ppermute(value, axis, [(j, j ^ k) for j in range(count)])
 
+    def cross(value, k):
+        there = [(d ^ k) * expert_count + (e ^ 1) for d in range(dp_count) for e in range(expert_count)]
+        return lax.ppermute(value, ("dp", "expert"), list(enumerate(there)))
+
     def gather(value):
         if not cubed:
             return [lax.all_gather(value, "expert", axis=0, tiled=True)]
-        parts = [value] + [swap(value, "expert", k) for k in (2, 4, 6)]
+        parts = [value] + [swap(value, "expert", k) for k in (3, 5, 7)]
         joined = jnp.concatenate(parts, axis=0)
         return parts + [swap(joined, "expert", 1)]
 
@@ -472,7 +483,9 @@
         (*token_parts, down_weight.swapaxes(1, 2)),
         scratch=(VMEM((2, tokens, hidden_size), bf16),),
     )
-    if paired:
+    if cubed:
+        parts = [cross(sends[k], k) for k in range(dp_count)]
+    elif paired:
         parts = [sends[0]] + [swap(sends[k], "dp", k) for k in range(1, dp_count)]
     else:
         all_sends = jnp.concatenate(sends, axis=0).reshape(dp_count, piece, hidden_size)
@@ -491,7 +504,9 @@
     else:
         pieces = list(lax.all_to_all(piece_out, "dp", 0, 0, tiled=True))
     hidden = sum(part.astype(f32) for part in parts).astype(bf16)
-    if paired:
+    if cubed:
+        blocks = [cross(hidden, k) for k in range(dp_count)]
+    elif paired:
         blocks = [hidden] + [swap(hidden, "dp", k) for k in range(1, dp_count)]
     else:
         spread = lax.all_gather(hidden, "dp", axis=0, tiled=True)
@@ -500,7 +515,8 @@
     weights = (gate_weight, up_weight, gate_saved, up_saved)
     lanes = -(-rows // LANES) * LANES
     done = []
-    for k in range(local_experts - 1):
+    turns = (0, 2, 3, 1) if cubed else tuple(range(local_experts))
+    for k in turns[:-1]:
         done += call(
             functools.partial(input_kernel, k, paired),
             (((slots, share), f32), ((1, lanes), f32)),
@@ -513,9 +529,9 @@
     else:
         mix_shapes = (((expert_count, group, width), bf16),)
     *mixed, own = call(
-        functools.partial(mix_kernel, local_experts - 1, group, paired, cubed),
+        functools.partial(mix_kernel, turns, group, paired, cubed),
         (*mix_shapes, ((tokens, LANES), f32)),
-        (full, *weights, blocks[-1], *(pieces if cubed else ()), *done),
+        (full, *weights, blocks[turns[-1]], *(pieces if cubed else ()), *done),
         scratch=(VMEM((rows, share), f32), VMEM((1, lanes), f32)),
     )
     if cubed:

time: 48 us -> 46.7 us (0.973)
  waiting for transfers between devices: 19.5 us -> 17.9 us
    ppermute x0 -> x8, starting transfers between devices: none -> 8.52 us  [cross(): return lax.ppermute(value, ('dp', 'expert'), list(enumerate(there)))]
    ppermute x16 -> x10, starting transfers between devices: 17.3 us -> 9.09 us  [swap(): return lax.ppermute(value, axis, [(j, j ^ k) for j in range(count)])]
    ppermute x16 -> x10, waiting for transfers between devices: 19.5 us -> 12.7 us  [swap(): return lax.ppermute(value, axis, [(j, j ^ k) for j in range(count)])]
    ppermute x0 -> x8, waiting for transfers between devices: none -> 5.14 us  [cross(): return lax.ppermute(value, ('dp', 'expert'), list(enumerate(there)))]
  transfers between devices with their start and end apart: 16 -> 18, of which waited for: 12 -> 12; matrix products, arithmetic and copies ran while one was open for 0% -> 0% of each run, Pallas kernels for 9% -> 10%
where the time goes in v5:
time: 46.7 us; the launch traced here: 46.5 us
  waiting for transfers between devices  17.9 us (38%)
  starting transfers between devices  17.6 us (38%)
  Pallas kernels  10.2 us (22%)
  between operations  0.75 us (2%)
    ppermute x10, waiting for transfers between devices, swap(): return lax.ppermute(value, axis, [(j, j ^ k) for j in range(count)])  12.7 us
    pallas_call x10, Pallas kernels, call(): pl.pallas_call(kernel, out_shape=tuple((space(*out) for out in outs)) if...  10.2 us
    ppermute x10, starting transfers between devices, swap(): return lax.ppermute(value, axis, [(j, j ^ k) for j in range(count)])  9.09 us
    ppermute x8, starting transfers between devices, cross(): return lax.ppermute(value, ('dp', 'expert'), list(enumerate(there)))  8.52 us
    ppermute x8, waiting for transfers between devices, cross(): return lax.ppermute(value, ('dp', 'expert'), list(enumerate(there)))  5.14 us
  transfers between devices with their start and end apart: 18, of which 12 were waited for; matrix products, arithmetic and copies ran while one was open for 0% of the time, Pallas kernels for 10%

profile of v5, /device:TPU:0, one launch (start us, length us, event | category | flops | bytes accessed | tf_op | source)
XLA Modules:
  0.0 46.5 jit_solution(5231593431463446391)
XLA Ops:
  0.7 1.0 %shard_map.113 = (bf16[8,1088]{1,0:T(8,128)(2,1)S(1)}, bf16[2,960]{1,0:T(2,128)(2,1)S(1)}, bf16[4,960]{1,0:T(4,128)(2,1)S(1)}, bf16[2,960]{1,0:T(2,128)(2,1)S(1)}) custom-call(f32[1,8,32]{2,1,0:T(8,128)} %refs_0_.5, s32[1,8,8]{2,1,0:T(8,128)} %refs_1_.5, bf16[1,8,960]{2,1,0:T(8,128)(2,1)} %refs_2_.5, bf16[1,2,3840]{2,1,0:T(2,128)(2,1)} %refs_3_.5), custom_call_target="tpu_custom_call" | custom-call | flops 40000000000 | tf_op jit(solution)/shard_map/pallas_call | solution.py:31
  1.7 3.4 %collective-permute-start.2 = (bf16[8,1088]{1,0:T(8,128)(2,1)S(1)}, bf16[8,1088]{1,0:T(8,128)(2,1)S(1)}, u32[]{:S(2)}, u32[]{:S(2)}) collective-permute-start(bf16[8,1088]{1,0:T(8,128)(2,1)S(1)} %get-tuple-element.29.refs_0_), channel_id=1, source_target_pairs={{0,7},{1,6},{2,5},{3,4},{4,3},{5,2},{6,1},{7,0},{8,15},{9,14},{10,... | collective-permute-start | bytes 52232 | tf_op jit(solution)/shard_map/ppermute | solution.py:446
  5.2 0.8 %collective-permute-start.1 = (bf16[8,1088]{1,0:T(8,128)(2,1)S(1)}, bf16[8,1088]{1,0:T(8,128)(2,1)S(1)}, u32[]{:S(2)}, u32[]{:S(2)}) collective-permute-start(bf16[8,1088]{1,0:T(8,128)(2,1)S(1)} %get-tuple-element.29.refs_0_), channel_id=1, source_target_pairs={{0,5},{1,4},{2,7},{3,6},{4,1},{5,0},{6,3},{7,2},{8,13},{9,12},{10,... | collective-permute-start | bytes 52232 | tf_op jit(solution)/shard_map/ppermute | solution.py:446
  6.6 1.7 %collective-permute-done.1.refs_2_ = bf16[8,1088]{1,0:T(8,128)(2,1)S(1)} collective-permute-done((bf16[8,1088]{1,0:T(8,128)(2,1)S(1)}, bf16[8,1088]{1,0:T(8,128)(2,1)S(1)}, u32[]{:S(2)}, u32[]{:S(2)}) %collective-permute-start.1) | collective-permute-done | bytes 17440 | tf_op jit(solution)/shard_map/ppermute | solution.py:446
  8.4 0.9 %collective-permute-done.refs_1_ = bf16[8,1088]{1,0:T(8,128)(2,1)S(1)} collective-permute-done((bf16[8,1088]{1,0:T(8,128)(2,1)S(1)}, bf16[8,1088]{1,0:T(8,128)(2,1)S(1)}, u32[]{:S(2)}, u32[]{:S(2)}) %collective-permute-start) | collective-permute-done | bytes 17440 | tf_op jit(solution)/shard_map/ppermute | solution.py:446
  9.5 1.2 %collective-permute-done.3.refs_4_ = bf16[32,1088]{1,0:T(8,128)(2,1)S(1)} collective-permute-done((bf16[32,1088]{1,0:T(8,128)(2,1)S(1)}, bf16[32,1088]{1,0:T(8,128)(2,1)S(1)}, u32[]{:S(2)}, u32[]{:S(2)}) %collective-permute-start.3) | collective-permute-done | bytes 69664 | tf_op jit(solution)/shard_map/ppermute | solution.py:446
  10.6 1.7 %shard_map.115 = (bf16[24,1024]{1,0:T(8,128)(2,1)S(1)}, bf16[24,1024]{1,0:T(8,128)(2,1)S(1)}, bf16[24,1024]{1,0:T(8,128)(2,1)S(1)}, bf16[24,1024]{1,0:T(8,128)(2,1)S(1)}) custom-call(bf16[8,1088]{1,0:T(8,128)(2,1)S(1)} %get-tuple-element.29.refs_0_, bf16[8,1088]{1,0:T(8,128)(2,1)S(1)} %collective-permute-done.refs_1_, ...), custom_call_target="tpu_custom_call" | custom-call | tf_op jit(solution)/shard_map/pallas_call | solution.py:31
  12.5 1.5 %collective-permute-start.6 = (bf16[24,1024]{1,0:T(8,128)(2,1)S(1)}, bf16[24,1024]{1,0:T(8,128)(2,1)S(1)}, u32[]{:S(2)}, u32[]{:S(2)}) collective-permute-start(bf16[24,1024]{1,0:T(8,128)(2,1)S(1)} %get-tuple-element.34), channel_id=1, source_target_pairs={{0,9},{1,8},{2,11},{3,10},{4,13},{5,12},{6,15},{7,14},{8,1},{9,0},... | collective-permute-start | bytes 147464 | tf_op jit(solution)/shard_map/ppermute | solution.py:450
  14.0 2.3 %collective-permute-start.7 = (bf16[24,1024]{1,0:T(8,128)(2,1)S(1)}, bf16[24,1024]{1,0:T(8,128)(2,1)S(1)}, u32[]{:S(2)}, u32[]{:S(2)}) collective-permute-start(bf16[24,1024]{1,0:T(8,128)(2,1)S(1)} %get-tuple-element.35), channel_id=1, source_target_pairs={{0,17},{1,16},{2,19},{3,18},{4,21},{5,20},{6,23},{7,22},{8,25},{9,... | collective-permute-start | bytes 147464 | tf_op jit(solution)/shard_map/ppermute | solution.py:450
  16.6 3.2 %collective-permute-done.7 = bf16[24,1024]{1,0:T(8,128)(2,1)S(1)} collective-permute-done((bf16[24,1024]{1,0:T(8,128)(2,1)S(1)}, bf16[24,1024]{1,0:T(8,128)(2,1)S(1)}, u32[]{:S(2)}, u32[]{:S(2)}) %collective-permute-start.7) | collective-permute-done | bytes 49184 | tf_op jit(solution)/shard_map/ppermute | solution.py:450
  19.8 1.9 %collective-permute-done.8 = bf16[24,1024]{1,0:T(8,128)(2,1)S(1)} collective-permute-done((bf16[24,1024]{1,0:T(8,128)(2,1)S(1)}, bf16[24,1024]{1,0:T(8,128)(2,1)S(1)}, u32[]{:S(2)}, u32[]{:S(2)}) %collective-permute-start.8) | collective-permute-done | bytes 49184 | tf_op jit(solution)/shard_map/ppermute | solution.py:450
  21.7 1.7 %collective-permute-start.13 = (bf16[24,1024]{1,0:T(8,128)(2,1)S(1)}, bf16[24,1024]{1,0:T(8,128)(2,1)S(1)}, u32[]{:S(2)}, u32[]{:S(2)}) collective-permute-start(bf16[24,1024]{1,0:T(8,128)(2,1)S(1)} %add_convert_fusion), channel_id=1, source_target_pairs={{0,25},{1,24},{2,27},{3,26},{4,29},{5,28},{6,31},{7,30},{8,17},{9,... | collective-permute-start | bytes 147464 | tf_op jit(solution)/shard_map/ppermute | solution.py:450
  23.7 2.4 %collective-permute-start.9 = (bf16[24,1024]{1,0:T(8,128)(2,1)S(1)}, bf16[24,1024]{1,0:T(8,128)(2,1)S(1)}, u32[]{:S(2)}, u32[]{:S(2)}) collective-permute-start(bf16[24,1024]{1,0:T(8,128)(2,1)S(1)} %add_convert_fusion), channel_id=1, source_target_pairs={{0,9},{1,8},{2,11},{3,10},{4,13},{5,12},{6,15},{7,14},{8,1},{9,0},... | collective-permute-start | bytes 147464 | tf_op jit(solution)/shard_map/ppermute | solution.py:450
  26.3 3.7 %collective-permute-done.4.refs_6_ = bf16[4,960]{1,0:T(4,128)(2,1)S(1)} collective-permute-done((bf16[4,960]{1,0:T(4,128)(2,1)S(1)}, bf16[4,960]{1,0:T(4,128)(2,1)S(1)}, u32[]{:S(2)}, u32[]{:S(2)}) %collective-permute-start.4) | collective-permute-done | bytes 7712 | tf_op jit(solution)/shard_map/ppermute | solution.py:446
  30.5 0.7 %collective-permute-start.10 = (bf16[4,960]{1,0:T(4,128)(2,1)S(1)}, bf16[4,960]{1,0:T(4,128)(2,1)S(1)}, u32[]{:S(2)}, u32[]{:S(2)}) collective-permute-start(bf16[4,960]{1,0:T(4,128)(2,1)S(1)} %get-tuple-element.38), channel_id=1, source_target_pairs={{0,16},{8,24},{16,0},{24,8},{1,17},{9,25},{17,1},{25,9},{2,18},{10... | collective-permute-start | bytes 23048 | tf_op jit(solution)/shard_map/ppermute | solution.py:446
  31.2 1.2 %shard_map.118 = (f32[24,960]{1,0:T(8,128)S(1)}, f32[1,128]{1,0:T(1,128)S(1)}) custom-call(bf16[4,960,1024]{2,1,0:T(8,128)(2,1)S(1)} %copy-done, bf16[4,960,1024]{2,1,0:T(8,128)(2,1)S(1)} %copy-done.1, bf16[4,24,1024]{2,1,0:T(8,128)(2,1)S(1)} %copy-done.3, bf16[4,24,1024]{2,1,0:T(8,128)(2,1)S(1)} %copy-done.4, ...), custom_call_target="tpu_custom_call" | custom-call | tf_op jit(solution)/shard_map/pallas_call | solution.py:31
  32.5 1.2 %shard_map.117 = (f32[24,960]{1,0:T(8,128)S(1)}, f32[1,128]{1,0:T(1,128)S(1)}) custom-call(bf16[4,960,1024]{2,1,0:T(8,128)(2,1)S(1)} %copy-done, bf16[4,960,1024]{2,1,0:T(8,128)(2,1)S(1)} %copy-done.1, bf16[4,24,1024]{2,1,0:T(8,128)(2,1)S(1)} %copy-done.3, bf16[4,24,1024]{2,1,0:T(8,128)(2,1)S(1)} %copy-done.4, ...), custom_call_target="tpu_custom_call" | custom-call | tf_op jit(solution)/shard_map/pallas_call | solution.py:31
  33.7 1.2 %shard_map.116 = (f32[24,960]{1,0:T(8,128)S(1)}, f32[1,128]{1,0:T(1,128)S(1)}) custom-call(bf16[4,960,1024]{2,1,0:T(8,128)(2,1)S(1)} %copy-done, bf16[4,960,1024]{2,1,0:T(8,128)(2,1)S(1)} %copy-done.1, bf16[4,24,1024]{2,1,0:T(8,128)(2,1)S(1)} %copy-done.3, bf16[4,24,1024]{2,1,0:T(8,128)(2,1)S(1)} %copy-done.4, ...), custom_call_target="tpu_custom_call" | custom-call | tf_op jit(solution)/shard_map/pallas_call | solution.py:31
  35.1 1.5 %shard_map.119 = (f32[5,8,1024]{2,1,0:T(8,128)S(1)}, bf16[5,8,1024]{2,1,0:T(8,128)(2,1)S(1)}, f32[64,128]{1,0:T(8,128)S(1)}) custom-call(f32[64,96]{1,0:T(8,128)S(1)} %get-tuple-element.32.full_ref, bf16[4,960,1024]{2,1,0:T(8,128)(2,1)S(1)} %copy-done, bf16[4,960,1024]{2,1,0:T(8,128)(2,1)S(1)} %copy-done.1, bf16[4,24,1024]{2,1,0:T(8,128)(2,1)S(1)} %copy-done.3, ...), custom_call_target="tpu_custom_call" | custom-call | tf_op jit(solution)/shard_map/pallas_call | solution.py:31
  36.7 1.3 %collective-permute-done.14.far_ref = bf16[5,8,1024]{2,1,0:T(8,128)(2,1)S(1)} collective-permute-done((bf16[5,8,1024]{2,1,0:T(8,128)(2,1)S(1)}, bf16[5,8,1024]{2,1,0:T(8,128)(2,1)S(1)}, u32[]{:S(2)}, u32[]{:S(2)}) %collective-permute-start.14) | collective-permute-done | bytes 81952 | tf_op jit(solution)/shard_map/ppermute | solution.py:446
  38.6 1.7 %collective-permute-start.16 = (bf16[24,1024]{1,0:T(8,128)(2,1)S(1)}, bf16[24,1024]{1,0:T(8,128)(2,1)S(1)}, u32[]{:S(2)}, u32[]{:S(2)}) collective-permute-start(bf16[24,1024]{1,0:T(8,128)(2,1)S(1)} %get-tuple-element.49), channel_id=1, source_target_pairs={{0,4},{1,5},{2,6},{3,7},{4,0},{5,1},{6,2},{7,3},{8,12},{9,13},{10,... | collective-permute-start | bytes 147464 | tf_op jit(solution)/shard_map/ppermute | solution.py:446
  40.3 1.4 %collective-permute-start.17 = (bf16[24,1024]{1,0:T(8,128)(2,1)S(1)}, bf16[24,1024]{1,0:T(8,128)(2,1)S(1)}, u32[]{:S(2)}, u32[]{:S(2)}) collective-permute-start(bf16[24,1024]{1,0:T(8,128)(2,1)S(1)} %get-tuple-element.50), channel_id=1, source_target_pairs={{0,6},{1,7},{2,4},{3,5},{4,2},{5,3},{6,0},{7,1},{8,14},{9,15},{10,... | collective-permute-start | bytes 147464 | tf_op jit(solution)/shard_map/ppermute | solution.py:446
  42.7 2.6 %collective-permute-done.17.refs_3_ = bf16[24,1024]{1,0:T(8,128)(2,1)S(1)} collective-permute-done((bf16[24,1024]{1,0:T(8,128)(2,1)S(1)}, bf16[24,1024]{1,0:T(8,128)(2,1)S(1)}, u32[]{:S(2)}, u32[]{:S(2)}) %collective-permute-start.17) | collective-permute-done | bytes 49184 | tf_op jit(solution)/shard_map/ppermute | solution.py:446
  45.3 1.2 %shard_map.122 = (bf16[1,8,960]{2,1,0:T(8,128)(2,1)}, f32[4,960]{1,0:T(4,128)}) custom-call(bf16[24,1024]{1,0:T(8,128)(2,1)S(1)} %get-tuple-element.47.refs_0_, bf16[24,1024]{1,0:T(8,128)(2,1)S(1)} %collective-permute-done.15.refs_1_, bf16[24,1024]{1,0:T(8,128)(2,1)S(1)} %collective-permute-done.16.refs_2_, ...), custom_call_target="tpu_custom_call" | custom-call | tf_op jit(solution)/shard_map/pallas_call | solution.py:31
  (36 shorter events, 4.2 us)
Async XLA Ops:
  0.6 10.0 %copy-start.2 = (bf16[4,1024,960]{1,2,0:T(8,128)(2,1)S(1)}, bf16[4,1024,960]{1,2,0:T(8,128)(2,1)}, u32[]{:S(2)}) copy-start(bf16[4,1024,960]{1,2,0:T(8,128)(2,1)} %param.17) | copy-start | bytes 23592964
  0.6 30.6 %copy-start.1 = (bf16[4,960,1024]{2,1,0:T(8,128)(2,1)S(1)}, bf16[4,960,1024]{2,1,0:T(8,128)(2,1)}, u32[]{:S(2)}) copy-start(bf16[4,960,1024]{2,1,0:T(8,128)(2,1)} %refs_1_.9) | copy-start | bytes 23592964
  1.7 29.5 %copy-start = (bf16[4,960,1024]{2,1,0:T(8,128)(2,1)S(1)}, bf16[4,960,1024]{2,1,0:T(8,128)(2,1)}, u32[]{:S(2)}) copy-start(bf16[4,960,1024]{2,1,0:T(8,128)(2,1)} %refs_0_.9) | copy-start | bytes 23592964
  1.7 29.5 %copy-start.3 = (bf16[4,24,1024]{2,1,0:T(8,128)(2,1)S(1)}, bf16[4,24,1024]{2,1,0:T(8,128)(2,1)}, u32[]{:S(2)}) copy-start(bf16[4,24,1024]{2,1,0:T(8,128)(2,1)} %refs_2_.9) | copy-start | bytes 589828
  1.7 29.5 %copy-start.4 = (bf16[4,24,1024]{2,1,0:T(8,128)(2,1)S(1)}, bf16[4,24,1024]{2,1,0:T(8,128)(2,1)}, u32[]{:S(2)}) copy-start(bf16[4,24,1024]{2,1,0:T(8,128)(2,1)} %refs_3_.9) | copy-start | bytes 589828
  1.7 4.9 %collective-permute-start.2 = (bf16[8,1088]{1,0:T(8,128)(2,1)S(1)}, bf16[8,1088]{1,0:T(8,128)(2,1)S(1)}, u32[]{:S(2)}, u32[]{:S(2)}) collective-permute-start(bf16[8,1088]{1,0:T(8,128)(2,1)S(1)} %get-tuple-element.29.refs_0_), channel_id=1, source_target_pairs={{0,7},{1,6},{2,5},{3,4},{4,3},{5,2},{6,1},{7,0},{8,15},{9,14},{10,... | collective-permute-start | bytes 52232 | tf_op jit(solution)/shard_map/ppermute | solution.py:446
  5.2 3.2 %collective-permute-start.1 = (bf16[8,1088]{1,0:T(8,128)(2,1)S(1)}, bf16[8,1088]{1,0:T(8,128)(2,1)S(1)}, u32[]{:S(2)}, u32[]{:S(2)}) collective-permute-start(bf16[8,1088]{1,0:T(8,128)(2,1)S(1)} %get-tuple-element.29.refs_0_), channel_id=1, source_target_pairs={{0,5},{1,4},{2,7},{3,6},{4,1},{5,0},{6,3},{7,2},{8,13},{9,12},{10,... | collective-permute-start | bytes 52232 | tf_op jit(solution)/shard_map/ppermute | solution.py:446
  6.0 3.3 %collective-permute-start = (bf16[8,1088]{1,0:T(8,128)(2,1)S(1)}, bf16[8,1088]{1,0:T(8,128)(2,1)S(1)}, u32[]{:S(2)}, u32[]{:S(2)}) collective-permute-start(bf16[8,1088]{1,0:T(8,128)(2,1)S(1)} %get-tuple-element.29.refs_0_), channel_id=1, source_target_pairs={{0,3},{1,2},{2,1},{3,0},{4,7},{5,6},{6,5},{7,4},{8,11},{9,10},{10,... | collective-permute-start | bytes 52232 | tf_op jit(solution)/shard_map/ppermute | solution.py:446
  9.3 1.3 %collective-permute-start.3 = (bf16[32,1088]{1,0:T(8,128)(2,1)S(1)}, bf16[32,1088]{1,0:T(8,128)(2,1)S(1)}, u32[]{:S(2)}, u32[]{:S(2)}) collective-permute-start(bf16[32,1088]{1,0:T(8,128)(2,1)S(1)} %pad_maximum_fusion), channel_id=1, source_target_pairs={{0,1},{1,0},{2,3},{3,2},{4,5},{5,4},{6,7},{7,6},{8,9},{9,8},{10,11... | collective-permute-start | bytes 208904 | tf_op jit(solution)/shard_map/ppermute | solution.py:446
  12.3 4.2 %collective-permute-start.5 = (bf16[24,1024]{1,0:T(8,128)(2,1)S(1)}, bf16[24,1024]{1,0:T(8,128)(2,1)S(1)}, u32[]{:S(2)}, u32[]{:S(2)}) collective-permute-start(bf16[24,1024]{1,0:T(8,128)(2,1)S(1)} %get-tuple-element.33), channel_id=1, source_target_pairs={{0,1},{1,0},{2,3},{3,2},{4,5},{5,4},{6,7},{7,6},{8,9},{9,8},{10,11... | collective-permute-start | bytes 147464 | tf_op jit(solution)/shard_map/ppermute | solution.py:450
  12.5 4.1 %collective-permute-start.6 = (bf16[24,1024]{1,0:T(8,128)(2,1)S(1)}, bf16[24,1024]{1,0:T(8,128)(2,1)S(1)}, u32[]{:S(2)}, u32[]{:S(2)}) collective-permute-start(bf16[24,1024]{1,0:T(8,128)(2,1)S(1)} %get-tuple-element.34), channel_id=1, source_target_pairs={{0,9},{1,8},{2,11},{3,10},{4,13},{5,12},{6,15},{7,14},{8,1},{9,0},... | collective-permute-start | bytes 147464 | tf_op jit(solution)/shard_map/ppermute | solution.py:450
  14.0 5.8 %collective-permute-start.7 = (bf16[24,1024]{1,0:T(8,128)(2,1)S(1)}, bf16[24,1024]{1,0:T(8,128)(2,1)S(1)}, u32[]{:S(2)}, u32[]{:S(2)}) collective-permute-start(bf16[24,1024]{1,0:T(8,128)(2,1)S(1)} %get-tuple-element.35), channel_id=1, source_target_pairs={{0,17},{1,16},{2,19},{3,18},{4,21},{5,20},{6,23},{7,22},{8,25},{9,... | collective-permute-start | bytes 147464 | tf_op jit(solution)/shard_map/ppermute | solution.py:450
  16.4 5.3 %collective-permute-start.8 = (bf16[24,1024]{1,0:T(8,128)(2,1)S(1)}, bf16[24,1024]{1,0:T(8,128)(2,1)S(1)}, u32[]{:S(2)}, u32[]{:S(2)}) collective-permute-start(bf16[24,1024]{1,0:T(8,128)(2,1)S(1)} %get-tuple-element.36), channel_id=1, source_target_pairs={{0,25},{1,24},{2,27},{3,26},{4,29},{5,28},{6,31},{7,30},{8,17},{9,... | collective-permute-start | bytes 147464 | tf_op jit(solution)/shard_map/ppermute | solution.py:450
  21.7 9.5 %collective-permute-start.13 = (bf16[24,1024]{1,0:T(8,128)(2,1)S(1)}, bf16[24,1024]{1,0:T(8,128)(2,1)S(1)}, u32[]{:S(2)}, u32[]{:S(2)}) collective-permute-start(bf16[24,1024]{1,0:T(8,128)(2,1)S(1)} %add_convert_fusion), channel_id=1, source_target_pairs={{0,25},{1,24},{2,27},{3,26},{4,29},{5,28},{6,31},{7,30},{8,17},{9,... | collective-permute-start | bytes 147464 | tf_op jit(solution)/shard_map/ppermute | solution.py:450
  23.4 9.0 %collective-permute-start.12 = (bf16[24,1024]{1,0:T(8,128)(2,1)S(1)}, bf16[24,1024]{1,0:T(8,128)(2,1)S(1)}, u32[]{:S(2)}, u32[]{:S(2)}) collective-permute-start(bf16[24,1024]{1,0:T(8,128)(2,1)S(1)} %add_convert_fusion), channel_id=1, source_target_pairs={{0,17},{1,16},{2,19},{3,18},{4,21},{5,20},{6,23},{7,22},{8,25},{9,... | collective-permute-start | bytes 147464 | tf_op jit(solution)/shard_map/ppermute | solution.py:450
  23.4 10.3 %collective-permute-start.11 = (bf16[24,1024]{1,0:T(8,128)(2,1)S(1)}, bf16[24,1024]{1,0:T(8,128)(2,1)S(1)}, u32[]{:S(2)}, u32[]{:S(2)}) collective-permute-start(bf16[24,1024]{1,0:T(8,128)(2,1)S(1)} %add_convert_fusion), channel_id=1, source_target_pairs={{0,1},{1,0},{2,3},{3,2},{4,5},{5,4},{6,7},{7,6},{8,9},{9,8},{10,11... | collective-permute-start | bytes 147464 | tf_op jit(solution)/shard_map/ppermute | solution.py:450
  23.7 11.4 %collective-permute-start.9 = (bf16[24,1024]{1,0:T(8,128)(2,1)S(1)}, bf16[24,1024]{1,0:T(8,128)(2,1)S(1)}, u32[]{:S(2)}, u32[]{:S(2)}) collective-permute-start(bf16[24,1024]{1,0:T(8,128)(2,1)S(1)} %add_convert_fusion), channel_id=1, source_target_pairs={{0,9},{1,8},{2,11},{3,10},{4,13},{5,12},{6,15},{7,14},{8,1},{9,0},... | collective-permute-start | bytes 147464 | tf_op jit(solution)/shard_map/ppermute | solution.py:450
  26.0 4.0 %collective-permute-start.4 = (bf16[4,960]{1,0:T(4,128)(2,1)S(1)}, bf16[4,960]{1,0:T(4,128)(2,1)S(1)}, u32[]{:S(2)}, u32[]{:S(2)}) collective-permute-start(bf16[4,960]{1,0:T(4,128)(2,1)S(1)} %get-tuple-element.31), channel_id=1, source_target_pairs={{0,8},{8,0},{16,24},{24,16},{1,9},{9,1},{17,25},{25,17},{2,10},{10... | collective-permute-start | bytes 23048 | tf_op jit(solution)/shard_map/ppermute | solution.py:446
  30.5 4.6 %collective-permute-start.10 = (bf16[4,960]{1,0:T(4,128)(2,1)S(1)}, bf16[4,960]{1,0:T(4,128)(2,1)S(1)}, u32[]{:S(2)}, u32[]{:S(2)}) collective-permute-start(bf16[4,960]{1,0:T(4,128)(2,1)S(1)} %get-tuple-element.38), channel_id=1, source_target_pairs={{0,16},{8,24},{16,0},{24,8},{1,17},{9,25},{17,1},{25,9},{2,18},{10... | collective-permute-start | bytes 23048 | tf_op jit(solution)/shard_map/ppermute | solution.py:446
  35.1 10.2 %copy-start.5 = (bf16[32,960]{1,0:T(8,128)(2,1)S(1)}, bf16[32,960]{1,0:T(8,128)(2,1)}, u32[]{:S(2)}) copy-start(bf16[32,960]{1,0:T(8,128)(2,1)} %refs_8_.1) | copy-start | bytes 184324
  36.6 1.3 %collective-permute-start.14 = (bf16[5,8,1024]{2,1,0:T(8,128)(2,1)S(1)}, bf16[5,8,1024]{2,1,0:T(8,128)(2,1)S(1)}, u32[]{:S(2)}, u32[]{:S(2)}) collective-permute-start(bf16[5,8,1024]{2,1,0:T(8,128)(2,1)S(1)} %get-tuple-element.46), channel_id=1, source_target_pairs={{0,1},{1,0},{2,3},{3,2},{4,5},{5,4},{6,7},{7,6},{8,9},{9,8},{10,11... | collective-permute-start | bytes 245768 | tf_op jit(solution)/shard_map/ppermute | solution.py:446
  38.2 4.1 %collective-permute-start.15 = (bf16[24,1024]{1,0:T(8,128)(2,1)S(1)}, bf16[24,1024]{1,0:T(8,128)(2,1)S(1)}, u32[]{:S(2)}, u32[]{:S(2)}) collective-permute-start(bf16[24,1024]{1,0:T(8,128)(2,1)S(1)} %get-tuple-element.48), channel_id=1, source_target_pairs={{0,2},{1,3},{2,0},{3,1},{4,6},{5,7},{6,4},{7,5},{8,10},{9,11},{10,... | collective-permute-start | bytes 147464 | tf_op jit(solution)/shard_map/ppermute | solution.py:446
  38.6 4.1 %collective-permute-start.16 = (bf16[24,1024]{1,0:T(8,128)(2,1)S(1)}, bf16[24,1024]{1,0:T(8,128)(2,1)S(1)}, u32[]{:S(2)}, u32[]{:S(2)}) collective-permute-start(bf16[24,1024]{1,0:T(8,128)(2,1)S(1)} %get-tuple-element.49), channel_id=1, source_target_pairs={{0,4},{1,5},{2,6},{3,7},{4,0},{5,1},{6,2},{7,3},{8,12},{9,13},{10,... | collective-permute-start | bytes 147464 | tf_op jit(solution)/shard_map/ppermute | solution.py:446
  40.3 5.0 %collective-permute-start.17 = (bf16[24,1024]{1,0:T(8,128)(2,1)S(1)}, bf16[24,1024]{1,0:T(8,128)(2,1)S(1)}, u32[]{:S(2)}, u32[]{:S(2)}) collective-permute-start(bf16[24,1024]{1,0:T(8,128)(2,1)S(1)} %get-tuple-element.50), channel_id=1, source_target_pairs={{0,6},{1,7},{2,4},{3,5},{4,2},{5,3},{6,0},{7,1},{8,14},{9,15},{10,... | collective-permute-start | bytes 147464 | tf_op jit(solution)/shard_map/ppermute | solution.py:446

commit v6 on v5

--- a/solution.py
+++ b/solution.py
@@ -101,6 +101,10 @@
     else:
         out_ref[group:, :aux] = jnp.zeros((group, aux), jnp.bfloat16)
         out_ref[group:, aux:] = jnp.concatenate(lines, axis=0).astype(jnp.bfloat16)
+
+
+def keep_kernel(value_ref, out_ref):
+    out_ref[...] = value_ref[...]
 
 
 def routing(head, sizes, cubed):
@@ -373,19 +377,6 @@
     for got, _ in sources:
         sums = sums + got[:, share : share + 2 * count].astype(jnp.float32)
     mixture = sums[:, :count] + sums[:, count:]
-    wide = jnp.dot(
-        mixture, place_ref[:count], precision=HIGH, preferred_element_type=jnp.float32
-    )
-    row_mixture = jnp.sum(wide * place_ref[count:], axis=0, keepdims=True)
-    lines = slope_rows_ref[...] * (mine_ref[...] - row_mixture)
-    grads = jnp.dot(
-        lines.astype(jnp.bfloat16), inputs, preferred_element_type=jnp.float32
-    )
-    for e in range(local_experts):
-        place = place_of(e, dp_me, paired)
-        router_ref[pl.ds(place, 1)] = grads[e : e + 1]
-    last = pltpu.make_async_copy(router_ref, router_far, sems.at[1])
-    last.start()
     mixed = jnp.zeros((group, share), jnp.float32)
     given = jnp.zeros((group, expert_total), jnp.float32)
     part = (4 * local_experts, expert_total)
@@ -409,6 +400,19 @@
     input_ref[0] = (mixed + routed).astype(jnp.bfloat16)
     store = pltpu.make_async_copy(input_ref, input_far, sems.at[0])
     store.start()
+    wide = jnp.dot(
+        mixture, place_ref[:count], precision=HIGH, preferred_element_type=jnp.float32
+    )
+    row_mixture = jnp.sum(wide * place_ref[count:], axis=0, keepdims=True)
+    lines = slope_rows_ref[...] * (mine_ref[...] - row_mixture)
+    grads = jnp.dot(
+        lines.astype(jnp.bfloat16), inputs, preferred_element_type=jnp.float32
+    )
+    for e in range(local_experts):
+        place = place_of(e, dp_me, paired)
+        router_ref[pl.ds(place, 1)] = grads[e : e + 1]
+    last = pltpu.make_async_copy(router_ref, router_far, sems.at[1])
+    last.start()
     last.wait()
     store.wait()
 
@@ -471,9 +475,9 @@
             VMEM(router_input.shape, bf16),
             pltpu.SemaphoreType.DMA((4,)),
         ),
-        flops=4 * 10**10,
         far_args=True,
     )
+    packed = call(keep_kernel, (packed.shape, bf16), (packed,), flops=4 * 10**10)
     if cubed:
         pieces[1] = swap(pieces[1], "dp", 1)
     token_parts = gather(packed)
@@ -515,7 +519,7 @@
     weights = (gate_weight, up_weight, gate_saved, up_saved)
     lanes = -(-rows // LANES) * LANES
     done = []
-    turns = (0, 2, 3, 1) if cubed else tuple(range(local_experts))
+    turns = (0, 1, 2, 3) if cubed else tuple(range(local_experts))
     for k in turns[:-1]:
         done += call(
             functools.partial(input_kernel, k, paired),

time: 46.7 us -> 46.6 us (level)
    pallas_call x10 -> x11, Pallas kernels: 10.2 us -> 9.91 us  [call(): pl.pallas_call(kernel, out_shape=tuple((space(*out) for out in outs)) if...]
where the time goes in v6:
time: 46.6 us; the launch traced here: 46.3 us
  waiting for transfers between devices  18.3 us (39%)
  starting transfers between devices  17.2 us (37%)
  Pallas kernels  9.91 us (21%)
  between operations  0.81 us (2%)
    ppermute x10, waiting for transfers between devices, swap(): return lax.ppermute(value, axis, [(j, j ^ k) for j in range(count)])  13.2 us
    pallas_call x11, Pallas kernels, call(): pl.pallas_call(kernel, out_shape=tuple((space(*out) for out in outs)) if...  9.91 us
    ppermute x10, starting transfers between devices, swap(): return lax.ppermute(value, axis, [(j, j ^ k) for j in range(count)])  8.73 us
    ppermute x8, starting transfers between devices, cross(): return lax.ppermute(value, ('dp', 'expert'), list(enumerate(there)))  8.52 us
    ppermute x8, waiting for transfers between devices, cross(): return lax.ppermute(value, ('dp', 'expert'), list(enumerate(there)))  5.14 us
  transfers between devices with their start and end apart: 18, of which 12 were waited for; matrix products, arithmetic and copies ran while one was open for 0% of the time, Pallas kernels for 10%

profile of v6, /device:TPU:0, one launch (start us, length us, event | category | flops | bytes accessed | tf_op | source)
XLA Modules:
  0.0 46.3 jit_solution(1553765111942646771)
XLA Ops:
  0.6 0.9 %shard_map.113 = (bf16[8,1088]{1,0:T(8,128)(2,1)S(1)}, bf16[2,960]{1,0:T(2,128)(2,1)S(1)}, bf16[4,960]{1,0:T(4,128)(2,1)S(1)}, bf16[2,960]{1,0:T(2,128)(2,1)S(1)}) custom-call(f32[1,8,32]{2,1,0:T(8,128)} %refs_0_.5, s32[1,8,8]{2,1,0:T(8,128)} %refs_1_.5, bf16[1,8,960]{2,1,0:T(8,128)(2,1)} %refs_2_.5, bf16[1,2,3840]{2,1,0:T(2,128)(2,1)} %refs_3_.5), custom_call_target="tpu_custom_call" | custom-call | tf_op jit(solution)/shard_map/pallas_call | solution.py:31
  1.6 3.4 %collective-permute-start.2 = (bf16[8,1088]{1,0:T(8,128)(2,1)S(1)}, bf16[8,1088]{1,0:T(8,128)(2,1)S(1)}, u32[]{:S(2)}, u32[]{:S(2)}) collective-permute-start(bf16[8,1088]{1,0:T(8,128)(2,1)S(1)} %shard_map.114.refs_0_), channel_id=1, source_target_pairs={{0,7},{1,6},{2,5},{3,4},{4,3},{5,2},{6,1},{7,0},{8,15},{9,14},{10,... | collective-permute-start | bytes 52232 | tf_op jit(solution)/shard_map/ppermute | solution.py:450
  5.1 0.8 %collective-permute-start.1 = (bf16[8,1088]{1,0:T(8,128)(2,1)S(1)}, bf16[8,1088]{1,0:T(8,128)(2,1)S(1)}, u32[]{:S(2)}, u32[]{:S(2)}) collective-permute-start(bf16[8,1088]{1,0:T(8,128)(2,1)S(1)} %shard_map.114.refs_0_), channel_id=1, source_target_pairs={{0,5},{1,4},{2,7},{3,6},{4,1},{5,0},{6,3},{7,2},{8,13},{9,12},{10,... | collective-permute-start | bytes 52232 | tf_op jit(solution)/shard_map/ppermute | solution.py:450
  6.5 1.7 %collective-permute-done.1.refs_2_ = bf16[8,1088]{1,0:T(8,128)(2,1)S(1)} collective-permute-done((bf16[8,1088]{1,0:T(8,128)(2,1)S(1)}, bf16[8,1088]{1,0:T(8,128)(2,1)S(1)}, u32[]{:S(2)}, u32[]{:S(2)}) %collective-permute-start.1) | collective-permute-done | bytes 17440 | tf_op jit(solution)/shard_map/ppermute | solution.py:450
  8.2 0.9 %collective-permute-done.refs_1_ = bf16[8,1088]{1,0:T(8,128)(2,1)S(1)} collective-permute-done((bf16[8,1088]{1,0:T(8,128)(2,1)S(1)}, bf16[8,1088]{1,0:T(8,128)(2,1)S(1)}, u32[]{:S(2)}, u32[]{:S(2)}) %collective-permute-start) | collective-permute-done | bytes 17440 | tf_op jit(solution)/shard_map/ppermute | solution.py:450
  9.4 1.2 %collective-permute-done.3.refs_4_ = bf16[32,1088]{1,0:T(8,128)(2,1)S(1)} collective-permute-done((bf16[32,1088]{1,0:T(8,128)(2,1)S(1)}, bf16[32,1088]{1,0:T(8,128)(2,1)S(1)}, u32[]{:S(2)}, u32[]{:S(2)}) %collective-permute-start.3) | collective-permute-done | bytes 69664 | tf_op jit(solution)/shard_map/ppermute | solution.py:450
  10.5 1.7 %shard_map.116 = (bf16[24,1024]{1,0:T(8,128)(2,1)S(1)}, bf16[24,1024]{1,0:T(8,128)(2,1)S(1)}, bf16[24,1024]{1,0:T(8,128)(2,1)S(1)}, bf16[24,1024]{1,0:T(8,128)(2,1)S(1)}) custom-call(bf16[8,1088]{1,0:T(8,128)(2,1)S(1)} %shard_map.114.refs_0_, bf16[8,1088]{1,0:T(8,128)(2,1)S(1)} %collective-permute-done.refs_1_, ...), custom_call_target="tpu_custom_call" | custom-call | tf_op jit(solution)/shard_map/pallas_call | solution.py:31
  12.4 1.5 %collective-permute-start.6 = (bf16[24,1024]{1,0:T(8,128)(2,1)S(1)}, bf16[24,1024]{1,0:T(8,128)(2,1)S(1)}, u32[]{:S(2)}, u32[]{:S(2)}) collective-permute-start(bf16[24,1024]{1,0:T(8,128)(2,1)S(1)} %get-tuple-element.34), channel_id=1, source_target_pairs={{0,9},{1,8},{2,11},{3,10},{4,13},{5,12},{6,15},{7,14},{8,1},{9,0},... | collective-permute-start | bytes 147464 | tf_op jit(solution)/shard_map/ppermute | solution.py:454
  13.9 2.3 %collective-permute-start.7 = (bf16[24,1024]{1,0:T(8,128)(2,1)S(1)}, bf16[24,1024]{1,0:T(8,128)(2,1)S(1)}, u32[]{:S(2)}, u32[]{:S(2)}) collective-permute-start(bf16[24,1024]{1,0:T(8,128)(2,1)S(1)} %get-tuple-element.35), channel_id=1, source_target_pairs={{0,17},{1,16},{2,19},{3,18},{4,21},{5,20},{6,23},{7,22},{8,25},{9,... | collective-permute-start | bytes 147464 | tf_op jit(solution)/shard_map/ppermute | solution.py:454
  16.5 3.2 %collective-permute-done.7 = bf16[24,1024]{1,0:T(8,128)(2,1)S(1)} collective-permute-done((bf16[24,1024]{1,0:T(8,128)(2,1)S(1)}, bf16[24,1024]{1,0:T(8,128)(2,1)S(1)}, u32[]{:S(2)}, u32[]{:S(2)}) %collective-permute-start.7) | collective-permute-done | bytes 49184 | tf_op jit(solution)/shard_map/ppermute | solution.py:454
  19.7 1.9 %collective-permute-done.8 = bf16[24,1024]{1,0:T(8,128)(2,1)S(1)} collective-permute-done((bf16[24,1024]{1,0:T(8,128)(2,1)S(1)}, bf16[24,1024]{1,0:T(8,128)(2,1)S(1)}, u32[]{:S(2)}, u32[]{:S(2)}) %collective-permute-start.8) | collective-permute-done | bytes 49184 | tf_op jit(solution)/shard_map/ppermute | solution.py:454
  21.6 1.5 %collective-permute-start.13 = (bf16[24,1024]{1,0:T(8,128)(2,1)S(1)}, bf16[24,1024]{1,0:T(8,128)(2,1)S(1)}, u32[]{:S(2)}, u32[]{:S(2)}) collective-permute-start(bf16[24,1024]{1,0:T(8,128)(2,1)S(1)} %add_convert_fusion), channel_id=1, source_target_pairs={{0,17},{1,16},{2,19},{3,18},{4,21},{5,20},{6,23},{7,22},{8,25},{9,... | collective-permute-start | bytes 147464 | tf_op jit(solution)/shard_map/ppermute | solution.py:454
  24.0 1.9 %collective-permute-start.9 = (bf16[24,1024]{1,0:T(8,128)(2,1)S(1)}, bf16[24,1024]{1,0:T(8,128)(2,1)S(1)}, u32[]{:S(2)}, u32[]{:S(2)}) collective-permute-start(bf16[24,1024]{1,0:T(8,128)(2,1)S(1)} %add_convert_fusion), channel_id=1, source_target_pairs={{0,25},{1,24},{2,27},{3,26},{4,29},{5,28},{6,31},{7,30},{8,17},{9,... | collective-permute-start | bytes 147464 | tf_op jit(solution)/shard_map/ppermute | solution.py:454
  25.9 4.1 %collective-permute-done.4.refs_6_ = bf16[4,960]{1,0:T(4,128)(2,1)S(1)} collective-permute-done((bf16[4,960]{1,0:T(4,128)(2,1)S(1)}, bf16[4,960]{1,0:T(4,128)(2,1)S(1)}, u32[]{:S(2)}, u32[]{:S(2)}) %collective-permute-start.4) | collective-permute-done | bytes 7712 | tf_op jit(solution)/shard_map/ppermute | solution.py:450
  30.5 0.6 %collective-permute-start.10 = (bf16[4,960]{1,0:T(4,128)(2,1)S(1)}, bf16[4,960]{1,0:T(4,128)(2,1)S(1)}, u32[]{:S(2)}, u32[]{:S(2)}) collective-permute-start(bf16[4,960]{1,0:T(4,128)(2,1)S(1)} %get-tuple-element.38), channel_id=1, source_target_pairs={{0,16},{8,24},{16,0},{24,8},{1,17},{9,25},{17,1},{25,9},{2,18},{10... | collective-permute-start | bytes 23048 | tf_op jit(solution)/shard_map/ppermute | solution.py:450
  31.2 1.2 %shard_map.119 = (f32[24,960]{1,0:T(8,128)S(1)}, f32[1,128]{1,0:T(1,128)S(1)}) custom-call(bf16[4,960,1024]{2,1,0:T(8,128)(2,1)S(1)} %bitcast.2, bf16[4,960,1024]{2,1,0:T(8,128)(2,1)S(1)} %bitcast.4, bf16[4,24,1024]{2,1,0:T(8,128)(2,1)S(1)} %copy-done.1, bf16[4,24,1024]{2,1,0:T(8,128)(2,1)S(1)} %copy-done.2, bf16[24,1024]{1,0:T(8,128)(2,1)S(1)} %collective-permute-done.13.refs_4_), custom_call_target="tpu_custom_call" | custom-call | tf_op jit(solution)/shard_map/pallas_call | solution.py:31
  32.4 1.2 %shard_map.118 = (f32[24,960]{1,0:T(8,128)S(1)}, f32[1,128]{1,0:T(1,128)S(1)}) custom-call(bf16[4,960,1024]{2,1,0:T(8,128)(2,1)S(1)} %bitcast.2, bf16[4,960,1024]{2,1,0:T(8,128)(2,1)S(1)} %bitcast.4, bf16[4,24,1024]{2,1,0:T(8,128)(2,1)S(1)} %copy-done.1, bf16[4,24,1024]{2,1,0:T(8,128)(2,1)S(1)} %copy-done.2, bf16[24,1024]{1,0:T(8,128)(2,1)S(1)} %collective-permute-done.12.refs_4_), custom_call_target="tpu_custom_call" | custom-call | tf_op jit(solution)/shard_map/pallas_call | solution.py:31
  33.6 1.2 %shard_map.117 = (f32[24,960]{1,0:T(8,128)S(1)}, f32[1,128]{1,0:T(1,128)S(1)}) custom-call(bf16[4,960,1024]{2,1,0:T(8,128)(2,1)S(1)} %bitcast.2, bf16[4,960,1024]{2,1,0:T(8,128)(2,1)S(1)} %bitcast.4, bf16[4,24,1024]{2,1,0:T(8,128)(2,1)S(1)} %copy-done.1, bf16[4,24,1024]{2,1,0:T(8,128)(2,1)S(1)} %copy-done.2, bf16[24,1024]{1,0:T(8,128)(2,1)S(1)} %collective-permute-done.11.refs_4_), custom_call_target="tpu_custom_call" | custom-call | tf_op jit(solution)/shard_map/pallas_call | solution.py:31
  35.1 1.5 %shard_map.120 = (f32[5,8,1024]{2,1,0:T(8,128)S(1)}, bf16[5,8,1024]{2,1,0:T(8,128)(2,1)S(1)}, f32[64,128]{1,0:T(8,128)S(1)}) custom-call(f32[64,96]{1,0:T(8,128)S(1)} %get-tuple-element.32.full_ref, bf16[4,960,1024]{2,1,0:T(8,128)(2,1)S(1)} %bitcast.2, bf16[4,960,1024]{2,1,0:T(8,128)(2,1)S(1)} %bitcast.4, bf16[4,24,1024]{2,1,0:T(8,128)(2,1)S(1)} %copy-done.1, ...), custom_call_target="tpu_custom_call" | custom-call | tf_op jit(solution)/shard_map/pallas_call | solution.py:31
  36.7 1.3 %collective-permute-done.14.far_ref = bf16[5,8,1024]{2,1,0:T(8,128)(2,1)S(1)} collective-permute-done((bf16[5,8,1024]{2,1,0:T(8,128)(2,1)S(1)}, bf16[5,8,1024]{2,1,0:T(8,128)(2,1)S(1)}, u32[]{:S(2)}, u32[]{:S(2)}) %collective-permute-start.14) | collective-permute-done | bytes 81952 | tf_op jit(solution)/shard_map/ppermute | solution.py:450
  38.6 1.7 %collective-permute-start.16 = (bf16[24,1024]{1,0:T(8,128)(2,1)S(1)}, bf16[24,1024]{1,0:T(8,128)(2,1)S(1)}, u32[]{:S(2)}, u32[]{:S(2)}) collective-permute-start(bf16[24,1024]{1,0:T(8,128)(2,1)S(1)} %get-tuple-element.49), channel_id=1, source_target_pairs={{0,4},{1,5},{2,6},{3,7},{4,0},{5,1},{6,2},{7,3},{8,12},{9,13},{10,... | collective-permute-start | bytes 147464 | tf_op jit(solution)/shard_map/ppermute | solution.py:450
  40.3 1.4 %collective-permute-start.17 = (bf16[24,1024]{1,0:T(8,128)(2,1)S(1)}, bf16[24,1024]{1,0:T(8,128)(2,1)S(1)}, u32[]{:S(2)}, u32[]{:S(2)}) collective-permute-start(bf16[24,1024]{1,0:T(8,128)(2,1)S(1)} %get-tuple-element.50), channel_id=1, source_target_pairs={{0,6},{1,7},{2,4},{3,5},{4,2},{5,3},{6,0},{7,1},{8,14},{9,15},{10,... | collective-permute-start | bytes 147464 | tf_op jit(solution)/shard_map/ppermute | solution.py:450
  42.7 2.6 %collective-permute-done.17.refs_3_ = bf16[24,1024]{1,0:T(8,128)(2,1)S(1)} collective-permute-done((bf16[24,1024]{1,0:T(8,128)(2,1)S(1)}, bf16[24,1024]{1,0:T(8,128)(2,1)S(1)}, u32[]{:S(2)}, u32[]{:S(2)}) %collective-permute-start.17) | collective-permute-done | bytes 49184 | tf_op jit(solution)/shard_map/ppermute | solution.py:450
  45.3 1.1 %shard_map.123 = (bf16[1,8,960]{2,1,0:T(8,128)(2,1)}, f32[4,960]{1,0:T(4,128)}) custom-call(bf16[24,1024]{1,0:T(8,128)(2,1)S(1)} %get-tuple-element.47.refs_0_, bf16[24,1024]{1,0:T(8,128)(2,1)S(1)} %collective-permute-done.15.refs_1_, bf16[24,1024]{1,0:T(8,128)(2,1)S(1)} %collective-permute-done.16.refs_2_, ...), custom_call_target="tpu_custom_call" | custom-call | tf_op jit(solution)/shard_map/pallas_call | solution.py:31
  (43 shorter events, 4.7 us)
Async XLA Ops:
  1.5 29.6 %slice-start = ((s8[7864320]{0:T(1024)(128)(4,1)}), s8[4194304]{0:T(1024)(128)(4,1)S(1)}, s32[]{:S(2)}) async-start(s8[7864320]{0:T(1024)(128)(4,1)} %bitcast.1), calls=%async_computation | async-start | bytes 8388608
  1.5 29.6 %slice-start.2 = ((s8[7864320]{0:T(1024)(128)(4,1)}), s8[4194304]{0:T(1024)(128)(4,1)S(1)}, s32[]{:S(2)}) async-start(s8[7864320]{0:T(1024)(128)(4,1)} %bitcast.3), calls=%async_computation.2 | async-start | bytes 8388608
  1.6 29.5 %slice-start.1 = ((s8[7864320]{0:T(1024)(128)(4,1)}), s8[3670016]{0:T(1024)(128)(4,1)S(1)}, s32[]{:S(2)}) async-start(s8[7864320]{0:T(1024)(128)(4,1)} %bitcast.1), calls=%async_computation.1 | async-start | bytes 7340032
  1.6 29.5 %slice-start.3 = ((s8[7864320]{0:T(1024)(128)(4,1)}), s8[3670016]{0:T(1024)(128)(4,1)S(1)}, s32[]{:S(2)}) async-start(s8[7864320]{0:T(1024)(128)(4,1)} %bitcast.3), calls=%async_computation.3 | async-start | bytes 7340032
  1.6 29.5 %copy-start.1 = (bf16[4,24,1024]{2,1,0:T(8,128)(2,1)S(1)}, bf16[4,24,1024]{2,1,0:T(8,128)(2,1)}, u32[]{:S(2)}) copy-start(bf16[4,24,1024]{2,1,0:T(8,128)(2,1)} %refs_2_.9) | copy-start | bytes 589828
  1.6 29.5 %copy-start.2 = (bf16[4,24,1024]{2,1,0:T(8,128)(2,1)S(1)}, bf16[4,24,1024]{2,1,0:T(8,128)(2,1)}, u32[]{:S(2)}) copy-start(bf16[4,24,1024]{2,1,0:T(8,128)(2,1)} %refs_3_.9) | copy-start | bytes 589828
  1.6 4.9 %collective-permute-start.2 = (bf16[8,1088]{1,0:T(8,128)(2,1)S(1)}, bf16[8,1088]{1,0:T(8,128)(2,1)S(1)}, u32[]{:S(2)}, u32[]{:S(2)}) collective-permute-start(bf16[8,1088]{1,0:T(8,128)(2,1)S(1)} %shard_map.114.refs_0_), channel_id=1, source_target_pairs={{0,7},{1,6},{2,5},{3,4},{4,3},{5,2},{6,1},{7,0},{8,15},{9,14},{10,... | collective-permute-start | bytes 52232 | tf_op jit(solution)/shard_map/ppermute | solution.py:450
  5.1 3.2 %collective-permute-start.1 = (bf16[8,1088]{1,0:T(8,128)(2,1)S(1)}, bf16[8,1088]{1,0:T(8,128)(2,1)S(1)}, u32[]{:S(2)}, u32[]{:S(2)}) collective-permute-start(bf16[8,1088]{1,0:T(8,128)(2,1)S(1)} %shard_map.114.refs_0_), channel_id=1, source_target_pairs={{0,5},{1,4},{2,7},{3,6},{4,1},{5,0},{6,3},{7,2},{8,13},{9,12},{10,... | collective-permute-start | bytes 52232 | tf_op jit(solution)/shard_map/ppermute | solution.py:450
  5.8 3.3 %collective-permute-start = (bf16[8,1088]{1,0:T(8,128)(2,1)S(1)}, bf16[8,1088]{1,0:T(8,128)(2,1)S(1)}, u32[]{:S(2)}, u32[]{:S(2)}) collective-permute-start(bf16[8,1088]{1,0:T(8,128)(2,1)S(1)} %shard_map.114.refs_0_), channel_id=1, source_target_pairs={{0,3},{1,2},{2,1},{3,0},{4,7},{5,6},{6,5},{7,4},{8,11},{9,10},{10,... | collective-permute-start | bytes 52232 | tf_op jit(solution)/shard_map/ppermute | solution.py:450
  9.2 1.3 %collective-permute-start.3 = (bf16[32,1088]{1,0:T(8,128)(2,1)S(1)}, bf16[32,1088]{1,0:T(8,128)(2,1)S(1)}, u32[]{:S(2)}, u32[]{:S(2)}) collective-permute-start(bf16[32,1088]{1,0:T(8,128)(2,1)S(1)} %pad_maximum_fusion), channel_id=1, source_target_pairs={{0,1},{1,0},{2,3},{3,2},{4,5},{5,4},{6,7},{7,6},{8,9},{9,8},{10,11... | collective-permute-start | bytes 208904 | tf_op jit(solution)/shard_map/ppermute | solution.py:450
  12.2 4.2 %collective-permute-start.5 = (bf16[24,1024]{1,0:T(8,128)(2,1)S(1)}, bf16[24,1024]{1,0:T(8,128)(2,1)S(1)}, u32[]{:S(2)}, u32[]{:S(2)}) collective-permute-start(bf16[24,1024]{1,0:T(8,128)(2,1)S(1)} %get-tuple-element.33), channel_id=1, source_target_pairs={{0,1},{1,0},{2,3},{3,2},{4,5},{5,4},{6,7},{7,6},{8,9},{9,8},{10,11... | collective-permute-start | bytes 147464 | tf_op jit(solution)/shard_map/ppermute | solution.py:454
  12.4 4.1 %collective-permute-start.6 = (bf16[24,1024]{1,0:T(8,128)(2,1)S(1)}, bf16[24,1024]{1,0:T(8,128)(2,1)S(1)}, u32[]{:S(2)}, u32[]{:S(2)}) collective-permute-start(bf16[24,1024]{1,0:T(8,128)(2,1)S(1)} %get-tuple-element.34), channel_id=1, source_target_pairs={{0,9},{1,8},{2,11},{3,10},{4,13},{5,12},{6,15},{7,14},{8,1},{9,0},... | collective-permute-start | bytes 147464 | tf_op jit(solution)/shard_map/ppermute | solution.py:454
  13.9 5.8 %collective-permute-start.7 = (bf16[24,1024]{1,0:T(8,128)(2,1)S(1)}, bf16[24,1024]{1,0:T(8,128)(2,1)S(1)}, u32[]{:S(2)}, u32[]{:S(2)}) collective-permute-start(bf16[24,1024]{1,0:T(8,128)(2,1)S(1)} %get-tuple-element.35), channel_id=1, source_target_pairs={{0,17},{1,16},{2,19},{3,18},{4,21},{5,20},{6,23},{7,22},{8,25},{9,... | collective-permute-start | bytes 147464 | tf_op jit(solution)/shard_map/ppermute | solution.py:454
  16.3 5.3 %collective-permute-start.8 = (bf16[24,1024]{1,0:T(8,128)(2,1)S(1)}, bf16[24,1024]{1,0:T(8,128)(2,1)S(1)}, u32[]{:S(2)}, u32[]{:S(2)}) collective-permute-start(bf16[24,1024]{1,0:T(8,128)(2,1)S(1)} %get-tuple-element.36), channel_id=1, source_target_pairs={{0,25},{1,24},{2,27},{3,26},{4,29},{5,28},{6,31},{7,30},{8,17},{9,... | collective-permute-start | bytes 147464 | tf_op jit(solution)/shard_map/ppermute | solution.py:454
  21.6 9.5 %collective-permute-start.13 = (bf16[24,1024]{1,0:T(8,128)(2,1)S(1)}, bf16[24,1024]{1,0:T(8,128)(2,1)S(1)}, u32[]{:S(2)}, u32[]{:S(2)}) collective-permute-start(bf16[24,1024]{1,0:T(8,128)(2,1)S(1)} %add_convert_fusion), channel_id=1, source_target_pairs={{0,17},{1,16},{2,19},{3,18},{4,21},{5,20},{6,23},{7,22},{8,25},{9,... | collective-permute-start | bytes 147464 | tf_op jit(solution)/shard_map/ppermute | solution.py:454
  23.1 9.3 %collective-permute-start.12 = (bf16[24,1024]{1,0:T(8,128)(2,1)S(1)}, bf16[24,1024]{1,0:T(8,128)(2,1)S(1)}, u32[]{:S(2)}, u32[]{:S(2)}) collective-permute-start(bf16[24,1024]{1,0:T(8,128)(2,1)S(1)} %add_convert_fusion), channel_id=1, source_target_pairs={{0,9},{1,8},{2,11},{3,10},{4,13},{5,12},{6,15},{7,14},{8,1},{9,0},... | collective-permute-start | bytes 147464 | tf_op jit(solution)/shard_map/ppermute | solution.py:454
  23.5 10.1 %collective-permute-start.11 = (bf16[24,1024]{1,0:T(8,128)(2,1)S(1)}, bf16[24,1024]{1,0:T(8,128)(2,1)S(1)}, u32[]{:S(2)}, u32[]{:S(2)}) collective-permute-start(bf16[24,1024]{1,0:T(8,128)(2,1)S(1)} %add_convert_fusion), channel_id=1, source_target_pairs={{0,1},{1,0},{2,3},{3,2},{4,5},{5,4},{6,7},{7,6},{8,9},{9,8},{10,11... | collective-permute-start | bytes 147464 | tf_op jit(solution)/shard_map/ppermute | solution.py:454
  24.0 11.1 %collective-permute-start.9 = (bf16[24,1024]{1,0:T(8,128)(2,1)S(1)}, bf16[24,1024]{1,0:T(8,128)(2,1)S(1)}, u32[]{:S(2)}, u32[]{:S(2)}) collective-permute-start(bf16[24,1024]{1,0:T(8,128)(2,1)S(1)} %add_convert_fusion), channel_id=1, source_target_pairs={{0,25},{1,24},{2,27},{3,26},{4,29},{5,28},{6,31},{7,30},{8,17},{9,... | collective-permute-start | bytes 147464 | tf_op jit(solution)/shard_map/ppermute | solution.py:454
  25.9 4.1 %collective-permute-start.4 = (bf16[4,960]{1,0:T(4,128)(2,1)S(1)}, bf16[4,960]{1,0:T(4,128)(2,1)S(1)}, u32[]{:S(2)}, u32[]{:S(2)}) collective-permute-start(bf16[4,960]{1,0:T(4,128)(2,1)S(1)} %get-tuple-element.31), channel_id=1, source_target_pairs={{0,8},{8,0},{16,24},{24,16},{1,9},{9,1},{17,25},{25,17},{2,10},{10... | collective-permute-start | bytes 23048 | tf_op jit(solution)/shard_map/ppermute | solution.py:450
  30.5 4.6 %collective-permute-start.10 = (bf16[4,960]{1,0:T(4,128)(2,1)S(1)}, bf16[4,960]{1,0:T(4,128)(2,1)S(1)}, u32[]{:S(2)}, u32[]{:S(2)}) collective-permute-start(bf16[4,960]{1,0:T(4,128)(2,1)S(1)} %get-tuple-element.38), channel_id=1, source_target_pairs={{0,16},{8,24},{16,0},{24,8},{1,17},{9,25},{17,1},{25,9},{2,18},{10... | collective-permute-start | bytes 23048 | tf_op jit(solution)/shard_map/ppermute | solution.py:450
  36.6 1.3 %collective-permute-start.14 = (bf16[5,8,1024]{2,1,0:T(8,128)(2,1)S(1)}, bf16[5,8,1024]{2,1,0:T(8,128)(2,1)S(1)}, u32[]{:S(2)}, u32[]{:S(2)}) collective-permute-start(bf16[5,8,1024]{2,1,0:T(8,128)(2,1)S(1)} %get-tuple-element.46), channel_id=1, source_target_pairs={{0,1},{1,0},{2,3},{3,2},{4,5},{5,4},{6,7},{7,6},{8,9},{9,8},{10,11... | collective-permute-start | bytes 245768 | tf_op jit(solution)/shard_map/ppermute | solution.py:450
  38.2 4.1 %collective-permute-start.15 = (bf16[24,1024]{1,0:T(8,128)(2,1)S(1)}, bf16[24,1024]{1,0:T(8,128)(2,1)S(1)}, u32[]{:S(2)}, u32[]{:S(2)}) collective-permute-start(bf16[24,1024]{1,0:T(8,128)(2,1)S(1)} %get-tuple-element.48), channel_id=1, source_target_pairs={{0,2},{1,3},{2,0},{3,1},{4,6},{5,7},{6,4},{7,5},{8,10},{9,11},{10,... | collective-permute-start | bytes 147464 | tf_op jit(solution)/shard_map/ppermute | solution.py:450
  38.6 4.1 %collective-permute-start.16 = (bf16[24,1024]{1,0:T(8,128)(2,1)S(1)}, bf16[24,1024]{1,0:T(8,128)(2,1)S(1)}, u32[]{:S(2)}, u32[]{:S(2)}) collective-permute-start(bf16[24,1024]{1,0:T(8,128)(2,1)S(1)} %get-tuple-element.49), channel_id=1, source_target_pairs={{0,4},{1,5},{2,6},{3,7},{4,0},{5,1},{6,2},{7,3},{8,12},{9,13},{10,... | collective-permute-start | bytes 147464 | tf_op jit(solution)/shard_map/ppermute | solution.py:450
  40.3 5.0 %collective-permute-start.17 = (bf16[24,1024]{1,0:T(8,128)(2,1)S(1)}, bf16[24,1024]{1,0:T(8,128)(2,1)S(1)}, u32[]{:S(2)}, u32[]{:S(2)}) collective-permute-start(bf16[24,1024]{1,0:T(8,128)(2,1)S(1)} %get-tuple-element.50), channel_id=1, source_target_pairs={{0,6},{1,7},{2,4},{3,5},{4,2},{5,3},{6,0},{7,1},{8,14},{9,15},{10,... | collective-permute-start | bytes 147464 | tf_op jit(solution)/shard_map/ppermute | solution.py:450
  (2 other events, 19.1 us)
